TPU v7x, 32 devices: a whole 2x2x4 slice. The times are simulated.
32 devices in a mesh: dp: 2 (over x), row: 4 (over y, core), col: 4 (over z).
Axes of the slice: x: 2, y: 2, z: 4, core: 2. Of those that a mesh axis runs over, the one named last changes fastest.
Arguments:
- inputs: bfloat16 [4096, 2048], P(('dp', 'row'), 'col'), may hold values from -6 to 6
- cotangent: bfloat16 [4096, 2048], P(('dp', 'row'), 'col'), may hold values from -6 to 6
- segments: int32 [4096], P('dp'), may hold values from 1999 to 4095, as said below
- positions: int32 [4096], P('dp'), may hold values from 0 to 1999, as said below
- w_qkv: bfloat16 [2048, 3, 2048], P('col', None, 'row'), may hold values from -1 to 1
- w_out: bfloat16 [2048, 2048], P('row', 'col'), may hold values from -0.5 to 0.5
- w_up: bfloat16 [2048, 8192], P('col', 'row'), may hold values from -1 to 1
- w_down: bfloat16 [8192, 2048], P('row', 'col'), may hold values from -0.0625 to 0.0625
- vectors: float32 [11, 2048], replicated, may hold values from -1.5 to 3
- tile_moment: float32 [4, 4, 24, 512, 256], P('row', 'col', 'dp'), may hold values from -40 to 40
- vector_moment: float32 [11, 2048], replicated, may hold values from -3 to 3
Outputs:
- result: float32 [4096, 2048], P(('dp', 'row'), 'col')
- grad_input: float32 [4096, 2048], P(('dp', 'row'), 'col')
- tile_grads: float32 [4, 4, 24, 512, 256], P('row', 'col', 'dp')
- new_tiles: float32 [4, 4, 24, 512, 256], P('row', 'col', 'dp')
- new_tile_moment: float32 [4, 4, 24, 512, 256], P('row', 'col', 'dp')
- vector_grads: float32 [11, 2048], replicated
- new_vectors: float32 [11, 2048], replicated
- new_vector_moment: float32 [11, 2048], replicated
Inputs may be any that keep to these rules, and one draw needn't show every extreme that they name: `segments`: each token's document label, the index in the whole array of its document's last token (the last document's label is 4095); labels never fall; every document but the last has 200 to 2000 tokens, documents run on across sequence ends, and the first has exactly 2000. `positions`: each token's place in its document, counted from 0 and running on across sequence ends.
All inputs are finite; a program needn't handle non-finite values.
Results may differ from a plain program's by a relative error of at most 0.015.
The roundings to bfloat16 on the way count: a program that leaves them out, or rounds other values in their place, can miss the bound.
Values may be sent and summed in bfloat16 or wider, within the bound.
A program may use at most 256 MiB of HBM per device.

v0:
```python
import math

import jax
import jax.numpy as jnp
from jax import lax
from jax.sharding import PartitionSpec as P

HEAD_DIM = 64
ROTARY = 32
SEQ_LEN = 512


MOMENTUM_RATE = 0.95
MUON_RATE = 0.05
VECTOR_RATE = 0.12
NEWTON_A = 3.4445
NEWTON_B = -4.775
NEWTON_C = 2.0315
GELU_SCALE = 0.7978845608028654
GELU_CUBIC = 0.044715
NORM_EPS = 1e-05
STAT_EPS = 1e-06
MASKED_SCORE = -1e30


def to_low(tensor_in):
    return lax.optimization_barrier(tensor_in.astype(jnp.bfloat16))


def gelu_value(pre_act):
    inner_arg = GELU_SCALE * (pre_act + GELU_CUBIC * pre_act * pre_act * pre_act)
    return 0.5 * pre_act * (1.0 + jnp.tanh(inner_arg))


def gelu_slope(pre_act):
    tanh_val = jnp.tanh(GELU_SCALE * (pre_act + GELU_CUBIC * pre_act * pre_act * pre_act))
    return 0.5 * (1.0 + tanh_val) + 0.5 * pre_act * (1.0 - tanh_val * tanh_val) * GELU_SCALE * (
        1.0 + 3.0 * GELU_CUBIC * pre_act * pre_act
    )


def rotary_tables(positions):
    half_dims = ROTARY // 2
    frequency = jnp.exp(
        jnp.arange(half_dims, dtype=jnp.float32) * (-2.0 * math.log(10000.0) / ROTARY)
    )
    angles = positions.astype(jnp.float32)[:, None] * frequency[None, :]
    return (jnp.cos(angles), jnp.sin(angles))


def rotate(tensor_in, cosine, sine_tab, direction_sign):
    half_dims = ROTARY // 2
    first_half = tensor_in[..., :half_dims]
    second_half = tensor_in[..., half_dims:ROTARY]
    cos_wide = cosine[:, None, :]
    sin_wide = sine_tab[:, None, :] * direction_sign
    return jnp.concatenate(
        [
            first_half * cos_wide - second_half * sin_wide,
            second_half * cos_wide + first_half * sin_wide,
            tensor_in[..., ROTARY:],
        ],
        axis=-1,
    )


def causal_allowed(segment):
    token_order = jnp.arange(segment.shape[0])
    return (segment[:, None] == segment[None, :]) & (token_order[:, None] >= token_order[None, :])


def masked_scores(queries, key_vecs, segment, score_scale):
    scores = (
        jnp.einsum("lhe,mhe->hlm", queries, key_vecs, preferred_element_type=jnp.float32)
        * score_scale
    )
    return jnp.where(causal_allowed(segment)[None], scores, MASKED_SCORE)


def attend_forward(queries, key_vecs, values, segment, score_scale):
    scores = masked_scores(queries, key_vecs, segment, score_scale)
    row_max = jnp.max(scores, axis=-1, keepdims=True)
    exp_scores = jnp.exp(scores - row_max)
    row_total = jnp.sum(exp_scores, axis=-1, keepdims=True)
    probs_low = to_low(exp_scores / row_total)
    attended = jnp.einsum("hlm,mhe->lhe", probs_low, values, preferred_element_type=jnp.float32)
    return (attended, (row_max + jnp.log(row_total))[..., 0])


def attend_backward(queries, key_vecs, values, output_low, grad_low, logsum, segment, score_scale):
    scores = masked_scores(queries, key_vecs, segment, score_scale)
    probs = jnp.exp(scores - logsum[..., None])
    grad_values = jnp.einsum(
        "hlm,lhe->mhe", to_low(probs), grad_low, preferred_element_type=jnp.float32
    )
    grad_probs = jnp.einsum("lhe,mhe->hlm", grad_low, values, preferred_element_type=jnp.float32)
    row_delta = jnp.sum(grad_low.astype(jnp.float32) * output_low.astype(jnp.float32), axis=-1)
    grad_scores = to_low(probs * (grad_probs - row_delta.T[:, :, None]) * score_scale)
    grad_queries = jnp.einsum(
        "hlm,mhe->lhe", grad_scores, key_vecs, preferred_element_type=jnp.float32
    )
    grad_keys = jnp.einsum("hlm,lhe->mhe", grad_scores, queries, preferred_element_type=jnp.float32)
    return (grad_queries, grad_keys, grad_values)


def newton_schulz(moment):
    iterate = to_low(moment * lax.rsqrt(jnp.sum(moment * moment) + STAT_EPS))
    for newton_step in range(5):
        gram = to_low(jnp.dot(iterate.T, iterate, preferred_element_type=jnp.float32))
        square = jnp.dot(gram, gram, preferred_element_type=jnp.float32)
        poly = to_low(NEWTON_B * gram.astype(jnp.float32) + NEWTON_C * square)
        iterate = to_low(
            NEWTON_A * iterate.astype(jnp.float32)
            + jnp.dot(iterate, poly, preferred_element_type=jnp.float32)
        )
    return iterate


def tile_blocks(qkv_block, out_block, up_block, down_block):
    tile_rows = qkv_block.shape[0]
    tile_cols = qkv_block.shape[2] // 2

    def split_cols(block_in):
        return block_in.reshape(
            block_in.shape[0], block_in.shape[1] // tile_cols, tile_cols
        ).transpose(1, 0, 2)

    down_part = down_block.reshape(
        down_block.shape[0] // tile_rows, tile_rows, down_block.shape[1] // tile_cols, tile_cols
    )
    down_part = down_part.transpose(0, 2, 1, 3).reshape(-1, tile_rows, tile_cols)
    return jnp.concatenate(
        [
            split_cols(qkv_block[:, 0]),
            split_cols(qkv_block[:, 1]),
            split_cols(qkv_block[:, 2]),
            split_cols(out_block),
            split_cols(up_block),
            down_part,
        ],
        axis=0,
    )


def body(
    inputs,
    cotangent,
    segments,
    positions,
    w_qkv,
    w_out,
    w_up,
    w_down,
    vectors,
    tile_moment,
    vector_moment,
):
    row_index = lax.axis_index("row")
    col_index = lax.axis_index("col")
    col_count = lax.axis_size("col")
    row_count_axis = lax.axis_size("row")
    local_rows, col_width = inputs.shape
    model_width = vectors.shape[1]
    row_width = w_qkv.shape[2]
    head_feats = row_width // col_count
    unit_width = w_up.shape[1] // col_count
    up_total = w_up.shape[1] * row_count_axis
    score_scale = HEAD_DIM ** (-0.5)
    feat_start = (row_index * col_count + col_index) * head_feats
    unit_start = (row_index * col_count + col_index) * unit_width
    col_start = col_index * col_width
    norm_gain = lax.dynamic_slice_in_dim(vectors[5], col_start, col_width)
    norm_shift = lax.dynamic_slice_in_dim(vectors[6], col_start, col_width)
    out_bias = lax.dynamic_slice_in_dim(vectors[3] + vectors[4], col_start, col_width)
    qkv_bias = lax.dynamic_slice_in_dim(vectors[0:3], feat_start, head_feats, axis=1)
    up_bias = lax.dynamic_slice_in_dim(vectors[7:].reshape(-1), unit_start, unit_width)
    x_val = inputs.astype(jnp.float32)
    row_stats = lax.psum((jnp.sum(x_val, axis=1), jnp.sum(x_val * x_val, axis=1)), "col")
    mean_x = (row_stats[0] / model_width)[:, None]
    var_x = (row_stats[1] / model_width)[:, None] - mean_x * mean_x
    inv_std = lax.rsqrt(var_x + NORM_EPS)
    x_hat = (x_val - mean_x) * inv_std
    normed = (x_hat * norm_gain + norm_shift).astype(jnp.bfloat16)
    gathered, cot_rows = (
        lax.all_gather(normed, "row", axis=0, tiled=True),
        lax.all_gather(cotangent, "row", axis=0, tiled=True),
    )
    seq_rows = gathered.shape[0]
    qkv_perm = (
        w_qkv.reshape(col_width, 3, col_count, head_feats)
        .transpose(0, 2, 1, 3)
        .reshape(col_width, col_count, 3 * head_feats)
    )
    w_in = jnp.concatenate([qkv_perm, w_up.reshape(col_width, col_count, unit_width)], axis=2)
    group_width = w_in.shape[2]
    w_in_flat = w_in.reshape(col_width, col_count * group_width)
    mixed_out = lax.psum_scatter(
        jnp.dot(gathered, w_in_flat, preferred_element_type=jnp.float32),
        "col",
        scatter_dimension=1,
        tiled=True,
    )
    qkv_part = mixed_out[:, : 3 * head_feats].reshape(seq_rows, 3, head_feats) + qkv_bias[None]
    up_pre = mixed_out[:, 3 * head_feats :] + up_bias
    heads_here = head_feats // HEAD_DIM
    seq_count = seq_rows // SEQ_LEN

    def by_seq(tensor_in):
        return tensor_in.reshape((seq_count, SEQ_LEN) + tensor_in.shape[1:])

    cosine, sine_tab = rotary_tables(positions)
    queries = rotate(
        qkv_part[:, 0].reshape(seq_rows, heads_here, HEAD_DIM), cosine, sine_tab, 1.0
    ).astype(jnp.bfloat16)
    key_vecs = rotate(
        qkv_part[:, 1].reshape(seq_rows, heads_here, HEAD_DIM), cosine, sine_tab, 1.0
    ).astype(jnp.bfloat16)
    values = qkv_part[:, 2].reshape(seq_rows, heads_here, HEAD_DIM).astype(jnp.bfloat16)
    attended, logsum = jax.vmap(attend_forward, in_axes=(0, 0, 0, 0, None))(
        by_seq(queries), by_seq(key_vecs), by_seq(values), by_seq(segments), score_scale
    )
    attn_low = attended.reshape(seq_rows, head_feats).astype(jnp.bfloat16)
    act_low = gelu_value(up_pre).astype(jnp.bfloat16)
    attn_rows, act_rows = (
        lax.all_gather(attn_low, "col", axis=1, tiled=True),
        lax.all_gather(act_low, "col", axis=1, tiled=True),
    )
    branch = lax.psum_scatter(
        jnp.dot(attn_rows, w_out, preferred_element_type=jnp.float32)
        + jnp.dot(act_rows, w_down, preferred_element_type=jnp.float32),
        "row",
        scatter_dimension=0,
        tiled=True,
    )
    result = x_val + branch + out_bias
    cot_val = cotangent.astype(jnp.float32)
    grad_w_out = jnp.einsum("ti,tj->ij", attn_rows, cot_rows, preferred_element_type=jnp.float32)
    grad_w_down = jnp.einsum("ti,tj->ij", act_rows, cot_rows, preferred_element_type=jnp.float32)
    back_attn = jnp.einsum("tj,ij->ti", cot_rows, w_out, preferred_element_type=jnp.float32)
    back_act = jnp.einsum("tj,ij->ti", cot_rows, w_down, preferred_element_type=jnp.float32)
    grad_attn, grad_act = (
        lax.psum_scatter(back_attn, "col", scatter_dimension=1, tiled=True),
        lax.psum_scatter(back_act, "col", scatter_dimension=1, tiled=True),
    )
    grad_attn_low = grad_attn.astype(jnp.bfloat16)
    grad_up = grad_act * gelu_slope(up_pre)
    g_queries, g_keys, g_values = jax.vmap(attend_backward, in_axes=(0, 0, 0, 0, 0, 0, 0, None))(
        by_seq(queries),
        by_seq(key_vecs),
        by_seq(values),
        by_seq(attn_low.reshape(seq_rows, heads_here, HEAD_DIM)),
        by_seq(grad_attn_low.reshape(seq_rows, heads_here, HEAD_DIM)),
        logsum,
        by_seq(segments),
        score_scale,
    )
    g_queries = rotate(
        g_queries.reshape(seq_rows, heads_here, HEAD_DIM), cosine, sine_tab, -1.0
    ).reshape(seq_rows, head_feats)
    g_keys = rotate(g_keys.reshape(seq_rows, heads_here, HEAD_DIM), cosine, sine_tab, -1.0).reshape(
        seq_rows, head_feats
    )
    g_values = g_values.reshape(seq_rows, head_feats)
    grad_mixed = jnp.concatenate([g_queries, g_keys, g_values, grad_up], axis=1)
    grad_cols = lax.all_gather(grad_mixed.astype(jnp.bfloat16), "col", axis=1, tiled=True)
    grad_w_in = jnp.einsum("ti,tj->ij", gathered, grad_cols, preferred_element_type=jnp.float32)
    grad_norm = lax.psum_scatter(
        jnp.einsum("tj,ij->ti", grad_cols, w_in_flat, preferred_element_type=jnp.float32),
        "row",
        scatter_dimension=0,
        tiled=True,
    )
    grad_hat = grad_norm * norm_gain
    back_stats = lax.psum((jnp.sum(grad_hat, axis=1), jnp.sum(grad_hat * x_hat, axis=1)), "col")
    grad_x = inv_std * (
        grad_hat
        - (back_stats[0] / model_width)[:, None]
        - x_hat * (back_stats[1] / model_width)[:, None]
    )
    grad_input = cot_val + grad_x
    qkv_sums = jnp.sum(grad_mixed[:, : 3 * head_feats].reshape(seq_rows, 3, head_feats), axis=0)
    out_sums = jnp.sum(cot_val, axis=0)
    norm_sums = jnp.stack(
        [out_sums, out_sums, jnp.sum(grad_norm * x_hat, axis=0), jnp.sum(grad_norm, axis=0)]
    )
    qkv_rows = lax.dynamic_update_slice_in_dim(
        jnp.zeros((3, model_width), jnp.float32), qkv_sums, feat_start, axis=1
    )
    norm_rows = lax.dynamic_update_slice_in_dim(
        jnp.zeros((4, model_width), jnp.float32), norm_sums, col_start, axis=1
    )
    up_rows = lax.dynamic_update_slice_in_dim(
        jnp.zeros((up_total,), jnp.float32), jnp.sum(grad_up, axis=0), unit_start, axis=0
    ).reshape(-1, model_width)
    local_vec = jnp.concatenate([qkv_rows, norm_rows, up_rows], axis=0)
    vec_grad = lax.psum(local_vec, ("dp", "row", "col"))
    scaled = vec_grad * lax.rsqrt(jnp.mean(vec_grad * vec_grad, axis=1, keepdims=True) + STAT_EPS)
    vec_moment_new = MOMENTUM_RATE * vector_moment + scaled
    vectors_new = vectors - VECTOR_RATE * vec_moment_new
    grad_perm = grad_w_in.reshape(col_width, col_count, group_width)
    grad_qkv = (
        grad_perm[:, :, : 3 * head_feats]
        .reshape(col_width, col_count, 3, head_feats)
        .transpose(0, 2, 1, 3)
        .reshape(col_width, 3, row_width)
    )
    grad_up_w = grad_perm[:, :, 3 * head_feats :].reshape(col_width, col_count * unit_width)
    grad_tiles = tile_blocks(grad_qkv, grad_w_out, grad_up_w, grad_w_down)
    owned_grads = lax.psum_scatter(grad_tiles[None, None], "dp", scatter_dimension=2, tiled=True)
    owned_count = owned_grads.shape[2]
    weight_tiles = lax.dynamic_slice_in_dim(
        tile_blocks(w_qkv, w_out, w_up, w_down), lax.axis_index("dp") * owned_count, owned_count, 0
    ).astype(jnp.float32)
    moment_new = MOMENTUM_RATE * tile_moment[0, 0] + owned_grads[0, 0]
    ortho_tiles = jax.vmap(newton_schulz)(moment_new)
    tile_ratio = math.sqrt(max(1.0, moment_new.shape[1] / moment_new.shape[2]))
    tiles_new = weight_tiles - MUON_RATE * tile_ratio * ortho_tiles.astype(jnp.float32)
    return (
        result,
        grad_input,
        owned_grads,
        tiles_new[None, None],
        moment_new[None, None],
        vec_grad,
        vectors_new,
        vec_moment_new,
    )


def solution(mesh):
    placed = (
        P(("dp", "row"), "col"),
        P(("dp", "row"), "col"),
        P("dp"),
        P("dp"),
        P("col", None, "row"),
        P("row", "col"),
        P("col", "row"),
        P("row", "col"),
        P(),
        P("row", "col", "dp", None, None),
        P(),
    )
    return jax.shard_map(
        body,
        mesh=mesh,
        in_specs=placed,
        out_specs=(
            P(("dp", "row"), "col"),
            P(("dp", "row"), "col"),
            P("row", "col", "dp", None, None),
            P("row", "col", "dp", None, None),
            P("row", "col", "dp", None, None),
            P(),
            P(),
            P(),
        ),
        check_vma=False,
    )
```

profile of v0, /device:TPU:0, one launch (start us, length us, event | category | flops | bytes accessed | tf_op | source)
XLA Modules:
  0.0 1773.4 jit_solution(18095130869114446671)
XLA Ops:
  9.2 13.5 all-reduce.1
  24.4 2.1 fusion.18
  26.5 8.3 all-gather.12.cloned.1.call-done
  34.9 5.0 fusion.35
  41.4 2.7 reshape.239
  47.6 3.0 copy.86
  50.6 3.2 pad_maximum_fusion
  53.9 2.4 copy.158
  56.3 3.3 all-gather.6.cloned.1.call-done
  59.6 16.2 fusion.33
  77.4 9.7 fusion.36
  91.7 47.6 %reduce-scatter.11.cloned.1.call-done = f32[2048,128]{1,0:T(8,128)} async-done(((f32[2048,512]{1,0:T(8,128)}), f32[2048,128]{1,0:T(8,128)}) %reduce-scatter.11.cloned.1.call-update) | async-done | bytes 1048592 | tf_op jit(solution)/shard_map/reduce_scatter | solution.py:242
  142.8 480.9 %reduce-scatter.7.cloned.1.call-done = f32[2048,896]{1,0:T(8,128)} async-done(((f32[2048,3584]{1,0:T(8,128)}), f32[2048,896]{1,0:T(8,128)}) %reduce-scatter.7.cloned.1.call-update) | async-done | bytes 7340048 | tf_op jit(solution)/shard_map/reduce_scatter | solution.py:197
  623.7 3.8 slice.129
  627.5 2.4 copy.87
  636.7 4.5 fusion.1
  645.8 4.0 multiply_reduce_fusion
  649.8 6.1 multiply_convert_fusion
  663.4 245.1 %reduce-scatter.13.cloned.1.call-done = f32[2048,512]{1,0:T(8,128)} async-done(((f32[2048,2048]{1,0:T(8,128)}), f32[2048,512]{1,0:T(8,128)}) %reduce-scatter.13.cloned.1.call-update) | async-done | bytes 4194320 | tf_op jit(solution)/shard_map/reduce_scatter | solution.py:243
  908.5 6.5 fusion.27
  915.1 2.1 pad_maximum_fusion.1
  920.4 250.0 %all-gather.14.cloned.1.call-done = bf16[2048,3584]{1,0:T(8,128)(2,1)} async-done(((bf16[2048,896]{1,0:T(8,128)(2,1)}), bf16[2048,3584]{1,0:T(8,128)(2,1)}) %all-gather.14.cloned.1.call-update) | async-done | bytes 14680080 | tf_op jit(solution)/shard_map/all_gather | solution.py:265
  1170.4 13.4 fusion.37
  1183.9 136.5 %all-gather.10.cloned.1.call-done = bf16[2048,2048]{1,0:T(8,128)(2,1)} async-done(((bf16[2048,512]{1,0:T(8,128)(2,1)}), bf16[2048,2048]{1,0:T(8,128)(2,1)}) %all-gather.10.cloned.1.call-update) | async-done | bytes 8388624 | tf_op jit(solution)/shard_map/all_gather | solution.py:226
  1320.3 10.5 fusion.34
  1330.9 35.5 %all-gather.8.cloned.1.call-done = bf16[2048,512]{0,1:T(8,128)(2,1)} async-done(((bf16[2048,128]{0,1:T(8,128)(2,1)}), bf16[2048,512]{0,1:T(8,128)(2,1)}) %all-gather.8.cloned.1.call-update) | async-done | bytes 2097168 | tf_op jit(solution)/shard_map/all_gather | solution.py:225
  1366.4 6.3 convolution_add_fusion
  1373.5 4.7 fusion.39
  1379.9 9.7 fusion.40
  1389.6 5.9 reshape.252
  1395.5 4.8 copy.120
  1400.2 11.4 fusion.38
  1412.0 2.5 slice.150
  1418.3 2.5 copy.116
  1420.9 5.7 copy.119
  1430.8 2.5 bitcast_dynamic-update-slice_fusion
  1435.2 9.7 all-reduce
  1444.9 15.5 reduce-scatter.9.cloned.1.call-done
  1460.5 3.3 convert_reduce_fusion.1
  1464.6 4.5 constant_dynamic-update-slice_fusion
  1471.2 4.0 copy.129
  1475.2 4.0 reshape.256
  1481.7 2.1 copy.124
  1486.0 2.6 copy.130
  1498.9 92.2 %all-reduce.4.cloned.1.call-done = f32[11,2048]{1,0:T(8,128)} async-done(((f32[11,2048]{1,0:T(8,128)}), f32[11,2048]{1,0:T(8,128)}) %all-reduce.4.cloned.1.call-update) | async-done | bytes 90128 | tf_op jit(solution)/shard_map/psum | solution.py:296
  1593.9 143.6 %reduce-scatter.17.cloned.1.call-done = f32[1,1,12,512,256]{4,3,2,1,0:T(8,128)} async-done(((f32[1,1,24,512,256]{4,3,2,1,0:T(8,128)}), f32[1,1,12,512,256]{4,3,2,1,0:T(8,128)}) %reduce-scatter.17.cloned.1.call-update) | async-done | bytes 6291472 | tf_op jit(solution)/shard_map/reduce_scatter | solution.py:309
  1737.4 5.7 fusion.2
  1759.9 5.5 subtract_bitcast_fusion
  (213 shorter events, 91.0 us)
Async XLA Ops:
  7.2 27.7 %all-gather.12.cloned.1.call-start = ((), (), s32[]{:S(2)}) async-start(), calls=%async_computation.11 | async-start | bytes 2621440 | tf_op jit(solution)/shard_map/all_gather | solution.py:186
  7.9 51.7 %all-gather.6.cloned.1.call-start = ((), (), s32[]{:S(2)}) async-start(), calls=%async_computation.6 | async-start | bytes 2621440 | tf_op jit(solution)/shard_map/all_gather | solution.py:185
  26.5 112.8 %reduce-scatter.11.cloned.1.call-start = ((), (), s32[]{:S(2)}) async-start(), calls=%async_computation.12 | async-start | bytes 5242880 | tf_op jit(solution)/shard_map/reduce_scatter | solution.py:242
  39.8 1.6 copy-start.6
  39.9 583.9 %reduce-scatter.7.cloned.1.call-start = ((), (), s32[]{:S(2)}) async-start(), calls=%async_computation.7 | async-start | bytes 36700160 | tf_op jit(solution)/shard_map/reduce_scatter | solution.py:197
  46.1 7.7 copy-start.3
  75.8 1.6 copy-start.10
  75.8 832.7 %reduce-scatter.13.cloned.1.call-start = ((), (), s32[]{:S(2)}) async-start(), calls=%async_computation.13 | async-start | bytes 20971520 | tf_op jit(solution)/shard_map/reduce_scatter | solution.py:243
  87.1 0.9 copy-start.36
  87.1 1.0 copy-start.37
  87.1 1.6 slice-start
  87.1 1083.3 %all-gather.14.cloned.1.call-start = ((), (), s32[]{:S(2)}) async-start(), calls=%async_computation.14 | async-start | bytes 18350080 | tf_op jit(solution)/shard_map/all_gather | solution.py:265
  630.2 1.2 copy-start.5
  630.7 2.6 copy-start.23
  631.4 1.9 copy-start.21
  633.3 3.4 copy-start
  636.7 4.5 copy-start.13
  645.8 4.1 copy-start.19
  649.8 6.1 copy-start.24
  655.9 1.5 copy-start.22
  657.5 1.8 copy-start.25
  660.1 248.4 %copy-start.35 = (f32[512]{0:T(512)S(1)}, f32[512]{0:T(512)}, u32[]{:S(2)}) copy-start(f32[512]{0:T(512)} %dynamic_slice.23) | copy-start | bytes 6148
  908.5 6.5 copy-start.15
  908.5 6.5 copy-start.16
  908.5 6.5 copy-start.17
  917.1 403.2 %all-gather.10.cloned.1.call-start = ((), (), s32[]{:S(2)}) async-start(), calls=%async_computation.9 | async-start | bytes 10485760 | tf_op jit(solution)/shard_map/all_gather | solution.py:226
  917.9 448.5 %all-gather.8.cloned.1.call-start = ((), (), s32[]{:S(2)}) async-start(), calls=%async_computation.8 | async-start | bytes 2621440 | tf_op jit(solution)/shard_map/all_gather | solution.py:225
  920.3 513.0 %reduce-scatter.15.cloned.1.call-start = ((), (), s32[]{:S(2)}) async-start(), calls=%async_computation.15 | async-start | bytes 5242880 | tf_op jit(solution)/shard_map/reduce_scatter | solution.py:267
  1183.8 276.6 %reduce-scatter.9.cloned.1.call-start = ((), (), s32[]{:S(2)}) async-start(), calls=%async_computation.10 | async-start | bytes 5242880 | tf_op jit(solution)/shard_map/reduce_scatter | solution.py:228
  1372.7 218.4 %all-reduce.4.cloned.1.call-start = ((), (), s32[]{:S(2)}) async-start(), calls=%async_computation.17 | async-start | bytes 262144 | tf_op jit(solution)/shard_map/psum | solution.py:296
  1373.5 6.4 copy-start.11
  1395.5 4.8 copy-start.38
  1426.5 2.1 copy-start.14
  1427.6 3.1 copy-start.2
  1430.8 2.5 copy-start.9
  1430.8 2.5 copy-start.30
  1430.8 2.5 copy-start.32
  1430.8 2.5 copy-start.34
  1430.8 29.7 %copy-start.18 = (bf16[512,512]{1,0:T(8,128)(2,1)S(1)}, bf16[512,512]{1,0:T(8,128)(2,1)}, u32[]{:S(2)}) copy-start(bf16[512,512]{1,0:T(8,128)(2,1)} %param.12) | copy-start | bytes 1572868
  1464.5 272.9 %reduce-scatter.17.cloned.1.call-start = ((), (), s32[]{:S(2)}) async-start(), calls=%async_computation.16 | async-start | bytes 18874368 | tf_op jit(solution)/shard_map/reduce_scatter | solution.py:309
  1469.1 1.0 copy-start.12
  1471.2 8.0 copy-start.4
  1480.3 5.7 copy-start.8
  1490.5 5.5 copy-start.7
  1496.0 96.2 %copy-start.27 = (f32[11,2048]{1,0:T(8,128)S(1)}, f32[11,2048]{1,0:T(8,128)}, u32[]{:S(2)}) copy-start(f32[11,2048]{1,0:T(8,128)} %param.19) | copy-start | bytes 270340
  1496.0 96.2 %copy-start.28 = (f32[11,2048]{1,0:T(8,128)S(1)}, f32[11,2048]{1,0:T(8,128)}, u32[]{:S(2)}) copy-start(f32[11,2048]{1,0:T(8,128)} %param.21) | copy-start | bytes 270340
  1743.1 2.7 copy-start.1
  1759.9 5.6 copy-start.20
  (4 other events, 2.6 us)
Sparse Core Ops, SparseCore 0:
  9.5 25.2 all-gather.11
  37.0 22.5 all-gather.5
  62.5 76.7 reduce-scatter.10
  141.5 482.1 reduce-scatter.6
  625.9 282.5 reduce-scatter.12
  917.3 253.0 all-gather.13
  1172.5 147.7 all-gather.9
  1322.5 43.8 all-gather.7
  1369.5 43.3 reduce-scatter.14
  1415.8 44.5 reduce-scatter.8
  1466.6 124.5 all-reduce.3
  1593.8 143.5 reduce-scatter.16
where the time goes:
time: 1780 us; the launch traced here: 1770 us
  waiting for transfers between devices  1460 us (82%)
  matrix products  116 us (7%)
  local copies, waits for them, and re-layouts  108 us (6%)
  other arithmetic  49.4 us (3%)
  blocking collectives  23.1 us (1%)
    reduce_scatter x1, waiting for transfers between devices, body(): lax.psum_scatter(jnp.dot(gathered, w_in_flat, preferred_element_type=jnp....  481 us
    all_gather x1, waiting for transfers between devices, body(): lax.all_gather(grad_mixed.astype(jnp.bfloat16), 'col', axis=1, tiled=True)  250 us
    reduce_scatter x1, waiting for transfers between devices, body(): lax.psum_scatter(back_act, 'col', scatter_dimension=1, tiled=True)  245 us
    reduce_scatter x1, waiting for transfers between devices, body(): lax.psum_scatter(grad_tiles[None, None], 'dp', scatter_dimension=2, tiled...  144 us
    all_gather x1, waiting for transfers between devices, body(): lax.all_gather(act_low, 'col', axis=1, tiled=True)  136 us
    psum x1, waiting for transfers between devices, body(): vec_grad = lax.psum(local_vec, ('dp', 'row', 'col'))  92.2 us
    reduce_scatter x1, waiting for transfers between devices, body(): lax.psum_scatter(back_attn, 'col', scatter_dimension=1, tiled=True)  47.6 us
  transfers between devices with their start and end apart: 12, of which 11 were waited for; matrix products, arithmetic and copies ran while one was open for 13% of the time, Pallas kernels for 0%

commit v1 on v0

v1 whole, which is shorter than its diff:
```python
import functools
import math

import jax
import jax.numpy as jnp
from jax import lax
from jax.experimental import pallas as pl
from jax.experimental.pallas import tpu as pltpu
from jax.sharding import PartitionSpec as P

HEAD_DIM = 64
ROTARY = 32
SEQ_LEN = 512

MOMENTUM_RATE = 0.95
MUON_RATE = 0.05
VECTOR_RATE = 0.12
NEWTON_A = 3.4445
NEWTON_B = -4.775
NEWTON_C = 2.0315
GELU_SCALE = 0.7978845608028654
GELU_CUBIC = 0.044715
NORM_EPS = 1e-05
STAT_EPS = 1e-06
MASKED_SCORE = -1e30

MESH = pl.DeviceIdType.MESH
ANY = pl.BlockSpec(memory_space=pl.ANY)
F32 = jnp.float32
BF16 = jnp.bfloat16


def to_low(tensor_in):
    return lax.optimization_barrier(tensor_in.astype(BF16))


def gelu_value(pre_act):
    inner_arg = GELU_SCALE * (pre_act + GELU_CUBIC * pre_act * pre_act * pre_act)
    return 0.5 * pre_act * (1.0 + jnp.tanh(inner_arg))


def gelu_slope(pre_act):
    tanh_val = jnp.tanh(GELU_SCALE * (pre_act + GELU_CUBIC * pre_act * pre_act * pre_act))
    return 0.5 * (1.0 + tanh_val) + 0.5 * pre_act * (1.0 - tanh_val * tanh_val) * GELU_SCALE * (
        1.0 + 3.0 * GELU_CUBIC * pre_act * pre_act
    )


def rotary_tables(positions):
    half_dims = ROTARY // 2
    frequency = jnp.exp(jnp.arange(half_dims, dtype=F32) * (-2.0 * math.log(10000.0) / ROTARY))
    angles = positions.astype(F32)[:, None] * frequency[None, :]
    return (jnp.cos(angles), jnp.sin(angles))


def rotate(tensor_in, cosine, sine_tab, direction_sign):
    half_dims = ROTARY // 2
    first_half = tensor_in[..., :half_dims]
    second_half = tensor_in[..., half_dims:ROTARY]
    cos_wide = cosine[:, None, :]
    sin_wide = sine_tab[:, None, :] * direction_sign
    return jnp.concatenate(
        [
            first_half * cos_wide - second_half * sin_wide,
            second_half * cos_wide + first_half * sin_wide,
            tensor_in[..., ROTARY:],
        ],
        axis=-1,
    )


def causal_allowed(segment):
    token_order = jnp.arange(segment.shape[0])
    return (segment[:, None] == segment[None, :]) & (token_order[:, None] >= token_order[None, :])


def masked_scores(queries, key_vecs, segment, score_scale):
    scores = (
        jnp.einsum("lhe,mhe->hlm", queries, key_vecs, preferred_element_type=F32) * score_scale
    )
    return jnp.where(causal_allowed(segment)[None], scores, MASKED_SCORE)


def attend_forward(queries, key_vecs, values, segment, score_scale):
    scores = masked_scores(queries, key_vecs, segment, score_scale)
    row_max = jnp.max(scores, axis=-1, keepdims=True)
    exp_scores = jnp.exp(scores - row_max)
    row_total = jnp.sum(exp_scores, axis=-1, keepdims=True)
    probs_low = to_low(exp_scores / row_total)
    attended = jnp.einsum("hlm,mhe->lhe", probs_low, values, preferred_element_type=F32)
    return (attended, (row_max + jnp.log(row_total))[..., 0])


def attend_backward(queries, key_vecs, values, output_low, grad_low, logsum, segment, score_scale):
    scores = masked_scores(queries, key_vecs, segment, score_scale)
    probs = jnp.exp(scores - logsum[..., None])
    grad_values = jnp.einsum("hlm,lhe->mhe", to_low(probs), grad_low, preferred_element_type=F32)
    grad_probs = jnp.einsum("lhe,mhe->hlm", grad_low, values, preferred_element_type=F32)
    row_delta = jnp.sum(grad_low.astype(F32) * output_low.astype(F32), axis=-1)
    grad_scores = to_low(probs * (grad_probs - row_delta.T[:, :, None]) * score_scale)
    grad_queries = jnp.einsum("hlm,mhe->lhe", grad_scores, key_vecs, preferred_element_type=F32)
    grad_keys = jnp.einsum("hlm,lhe->mhe", grad_scores, queries, preferred_element_type=F32)
    return (grad_queries, grad_keys, grad_values)


def newton_schulz(moment):
    iterate = to_low(moment * lax.rsqrt(jnp.sum(moment * moment) + STAT_EPS))
    for newton_step in range(5):
        gram = to_low(jnp.dot(iterate.T, iterate, preferred_element_type=F32))
        square = jnp.dot(gram, gram, preferred_element_type=F32)
        poly = to_low(NEWTON_B * gram.astype(F32) + NEWTON_C * square)
        iterate = to_low(
            NEWTON_A * iterate.astype(F32) + jnp.dot(iterate, poly, preferred_element_type=F32)
        )
    return iterate


def tile_blocks(qkv_block, out_block, up_block, down_block):
    tile_rows = qkv_block.shape[0]
    tile_cols = qkv_block.shape[2] // 2

    def split_cols(block_in):
        return block_in.reshape(
            block_in.shape[0], block_in.shape[1] // tile_cols, tile_cols
        ).transpose(1, 0, 2)

    down_part = down_block.reshape(
        down_block.shape[0] // tile_rows, tile_rows, down_block.shape[1] // tile_cols, tile_cols
    )
    down_part = down_part.transpose(0, 2, 1, 3).reshape(-1, tile_rows, tile_cols)
    return jnp.concatenate(
        [
            split_cols(qkv_block[:, 0]),
            split_cols(qkv_block[:, 1]),
            split_cols(qkv_block[:, 2]),
            split_cols(out_block),
            split_cols(up_block),
            down_part,
        ],
        axis=0,
    )


def gather_kernel(n_dp, n_row, n_col, dims, x_ref, g_ref, wq_ref, wu_ref, wo_ref, wd_ref,
                  xf, gf, wi, wf, stage_x, stage_q, stage_u, stage_o, stage_d,
                  zs, zr, ys, yr, cs, cr, ws, wr, ds, dr, ls, lo):
    T, C, HF, UT = dims
    d, r, c = lax.axis_index("dp"), lax.axis_index("row"), lax.axis_index("col")
    chunks = 2
    tc = T // chunks
    qw = 3 * HF
    acts = ((x_ref, xf), (g_ref, gf))

    def blk(a, rr, cc, t):
        return acts[a][1].at[pl.ds(rr * T + t * tc, tc), pl.ds(cc * C, C)]

    barrier = pltpu.get_barrier_semaphore()
    peers = [{"row": r ^ 1}, {"row": r ^ 2}]
    peers += [{"col": lax.rem(c + k, n_col)} for k in range(1, n_col)]
    peers += [{"dp": lax.rem(d + k, n_dp)} for k in range(1, n_dp)]
    for peer in peers:
        pl.semaphore_signal(barrier, inc=1, device_id=peer, device_id_type=MESH)
    pl.semaphore_wait(barrier, len(peers))

    def own(a, t):
        return acts[a][0].at[pl.ds(t * tc, tc), :]

    def copy(src, dst, s, rcv, peer):
        return pltpu.make_async_remote_copy(
            src_ref=src, dst_ref=dst, send_sem=s, recv_sem=rcv, device_id=peer, device_id_type=MESH
        )

    def z_copy(a, t, cc, src, right):
        peer = {"col": c + 1} if right else {"col": c - 1}
        return copy(src, blk(a, r, cc, t), zs.at[a, t, int(right), cc], zr.at[a, t, cc], peer)

    def y_copy(a, t, cc, src):
        return copy(src, blk(a, r, cc, t), ys.at[a, t, cc], yr.at[a, t, cc], {"row": r ^ 2})

    def c_copy(a, t, cc, src, rr, which):
        return copy(
            src, blk(a, rr, cc, t), cs.at[a, t, which, cc], cr.at[a, t, which, cc], {"row": r ^ 1}
        )

    order = [(a, t) for a in range(2) for t in range(chunks)]

    for a, t in order:
        @pl.when(c < n_col - 1)
        def _(a=a, t=t):
            z_copy(a, t, c, own(a, t), True).start()

        @pl.when(c > 0)
        def _(a=a, t=t):
            z_copy(a, t, c, own(a, t), False).start()

        y_copy(a, t, c, own(a, t)).start()
        c_copy(a, t, c, own(a, t), r, 0).start()

    loads = [
        pltpu.make_async_copy(x_ref, stage_x.at[0], ls.at[0]),
        pltpu.make_async_copy(g_ref, stage_x.at[1], ls.at[1]),
        pltpu.make_async_copy(wq_ref.at[c], stage_q, ls.at[2]),
        pltpu.make_async_copy(wu_ref.at[:, pl.ds(c * UT, UT)], stage_u.at[0], ls.at[3]),
        pltpu.make_async_copy(
            wu_ref.at[:, pl.ds((n_col + c) * UT, UT)], stage_u.at[1], ls.at[4]
        ),
        pltpu.make_async_copy(wo_ref.at[pl.ds(c * HF, HF), :], stage_o, ls.at[5]),
        pltpu.make_async_copy(wd_ref.at[pl.ds(c * UT, UT), :], stage_d.at[0], ls.at[6]),
        pltpu.make_async_copy(wd_ref.at[pl.ds((n_col + c) * UT, UT), :], stage_d.at[1], ls.at[7]),
    ]
    for item in loads:
        item.start()
    stores = [
        pltpu.make_async_copy(stage_x.at[0], xf.at[pl.ds(r * T, T), pl.ds(c * C, C)], lo.at[0]),
        pltpu.make_async_copy(stage_x.at[1], gf.at[pl.ds(r * T, T), pl.ds(c * C, C)], lo.at[1]),
        pltpu.make_async_copy(stage_q, wi.at[pl.ds(c * C, C), pl.ds(0, qw)], lo.at[2]),
        pltpu.make_async_copy(stage_u.at[0], wi.at[pl.ds(c * C, C), pl.ds(qw, UT)], lo.at[3]),
        pltpu.make_async_copy(stage_u.at[1], wi.at[pl.ds(c * C, C), pl.ds(qw + UT, UT)], lo.at[4]),
        pltpu.make_async_copy(stage_o, wf.at[pl.ds(0, HF), pl.ds(c * C, C)], lo.at[5]),
        pltpu.make_async_copy(stage_d.at[0], wf.at[pl.ds(HF, UT), pl.ds(c * C, C)], lo.at[6]),
        pltpu.make_async_copy(stage_d.at[1], wf.at[pl.ds(HF + UT, UT), pl.ds(c * C, C)], lo.at[7]),
    ]
    for load, store in zip(loads, stores):
        load.wait()
        store.start()

    ck, hk, uk = C // n_dp, HF // n_dp, UT // n_dp

    def w_dst(part, dd, cc):
        if part == 0:
            return wi.at[pl.ds(cc * C + dd * ck, ck), pl.ds(0, qw)]
        if part == 1:
            return wi.at[pl.ds(cc * C + dd * ck, ck), pl.ds(qw, UT)]
        if part == 2:
            return wi.at[pl.ds(cc * C + dd * ck, ck), pl.ds(qw + UT, UT)]
        if part == 3:
            return wf.at[pl.ds(dd * hk, hk), pl.ds(cc * C, C)]
        if part == 4:
            return wf.at[pl.ds(HF + dd * uk, uk), pl.ds(cc * C, C)]
        return wf.at[pl.ds(HF + UT + dd * uk, uk), pl.ds(cc * C, C)]

    def w_src(part, cc):
        if part == 0:
            return wq_ref.at[cc, pl.ds(d * ck, ck), :]
        if part == 1:
            return wu_ref.at[pl.ds(d * ck, ck), pl.ds(cc * UT, UT)]
        if part == 2:
            return wu_ref.at[pl.ds(d * ck, ck), pl.ds((n_col + cc) * UT, UT)]
        if part == 3:
            return wo_ref.at[pl.ds(cc * HF + d * hk, hk), :]
        if part == 4:
            return wd_ref.at[pl.ds(cc * UT + d * uk, uk), :]
        return wd_ref.at[pl.ds((n_col + cc) * UT + d * uk, uk), :]

    def w_copy(part, k):
        dest = lax.rem(c + k, n_col)
        return copy(
            w_src(part, dest), w_dst(part, d, c), ws.at[part, k], wr.at[part, k], {"col": dest}
        )

    def w_got(part, k):
        return w_dst(part, d, lax.rem(c + n_col - k, n_col))

    def x_copy(part, k, j):
        return copy(
            w_got(part, k), w_got(part, k), ds.at[part, k, j], dr.at[part, k, j],
            {"dp": lax.rem(d + j, n_dp)},
        )

    parts = range(6)

    for s in range(1, n_col):
        for a, t in order:
            @pl.when(c - s >= 0)
            def _(a=a, t=t, s=s):
                cc = c - s
                z_copy(a, t, cc, blk(a, r, cc, t), True).wait_recv()

                @pl.when(c < n_col - 1)
                def _():
                    z_copy(a, t, cc, blk(a, r, cc, t), True).start()

                y_copy(a, t, cc, blk(a, r, cc, t)).start()
                c_copy(a, t, cc, blk(a, r, cc, t), r, 0).start()

            @pl.when(c + s < n_col)
            def _(a=a, t=t, s=s):
                cc = c + s
                z_copy(a, t, cc, blk(a, r, cc, t), False).wait_recv()

                @pl.when(c > 0)
                def _():
                    z_copy(a, t, cc, blk(a, r, cc, t), False).start()

                y_copy(a, t, cc, blk(a, r, cc, t)).start()
                c_copy(a, t, cc, blk(a, r, cc, t), r, 0).start()

        for part in parts:
            w_copy(part, s).start()

    for s in range(n_col):
        for a, t in order:
            for cc in ((c,) if s == 0 else (c - s, c + s)):
                @pl.when((cc >= 0) & (cc < n_col))
                def _(a=a, t=t, cc=cc):
                    y_copy(a, t, cc, blk(a, r, cc, t)).wait_recv()
                    c_copy(a, t, cc, blk(a, r ^ 2, cc, t), r ^ 2, 1).start()

    for k in range(1, n_col):
        for part in parts:
            w_copy(part, k).wait_recv()
            for j in range(1, n_dp):
                x_copy(part, k, j).start()

    for a, t in order:
        for cc in range(n_col):
            c_copy(a, t, cc, blk(a, r, cc, t), r, 0).wait_recv()
            c_copy(a, t, cc, blk(a, r, cc, t), r, 1).wait_recv()
    for k in range(1, n_col):
        for part in parts:
            for j in range(1, n_dp):
                x_copy(part, k, j).wait_recv()
    for a, t in order:
        for cc in range(n_col):
            @pl.when((cc <= c) & (c < n_col - 1))
            def _(a=a, t=t, cc=cc):
                z_copy(a, t, cc, blk(a, r, cc, t), True).wait_send()

            @pl.when((cc >= c) & (c > 0))
            def _(a=a, t=t, cc=cc):
                z_copy(a, t, cc, blk(a, r, cc, t), False).wait_send()

            y_copy(a, t, cc, blk(a, r, cc, t)).wait_send()
            c_copy(a, t, cc, blk(a, r, cc, t), r, 0).wait_send()
            c_copy(a, t, cc, blk(a, r, cc, t), r, 1).wait_send()
    for k in range(1, n_col):
        for part in parts:
            w_copy(part, k).wait_send()
            for j in range(1, n_dp):
                x_copy(part, k, j).wait_send()
    for store in stores:
        store.wait()


def gather_all(x, g, w_q, w_up, w_out, w_down, n_dp, n_row, n_col):
    T, C = x.shape
    HF = w_q.shape[2] // 3
    UT = w_up.shape[1] // (2 * n_col)
    n_in, n_out = 3 * HF + 2 * UT, HF + 2 * UT
    dma = pltpu.SemaphoreType.DMA
    return pl.pallas_call(
        functools.partial(gather_kernel, n_dp, n_row, n_col, (T, C, HF, UT)),
        name="gather_all",
        out_shape=(
            jax.ShapeDtypeStruct((n_row * T, n_col * C), BF16),
            jax.ShapeDtypeStruct((n_row * T, n_col * C), BF16),
            jax.ShapeDtypeStruct((n_col * C, n_in), BF16),
            jax.ShapeDtypeStruct((n_out, n_col * C), BF16),
        ),
        in_specs=[ANY] * 6,
        out_specs=(ANY,) * 4,
        scratch_shapes=[
            pltpu.VMEM((2, T, C), BF16),
            pltpu.VMEM((C, 3 * HF), BF16),
            pltpu.VMEM((2, C, UT), BF16),
            pltpu.VMEM((HF, C), BF16),
            pltpu.VMEM((2, UT, C), BF16),
            dma((2, 2, 2, n_col)),
            dma((2, 2, n_col)),
            dma((2, 2, n_col)),
            dma((2, 2, n_col)),
            dma((2, 2, 2, n_col)),
            dma((2, 2, 2, n_col)),
            dma((6, n_col)),
            dma((6, n_col)),
            dma((6, n_col, n_dp)),
            dma((6, n_col, n_dp)),
            dma((8,)),
            dma((8,)),
        ],
        compiler_params=pltpu.CompilerParams(collective_id=0, has_side_effects=True),
    )(x, g, w_q, w_up, w_out, w_down)


def body(
    inputs,
    cotangent,
    segments,
    positions,
    w_qkv,
    w_out,
    w_up,
    w_down,
    vectors,
    tile_moment,
    vector_moment,
):
    d_index = lax.axis_index("dp")
    row_index = lax.axis_index("row")
    col_index = lax.axis_index("col")
    n_dp, n_row, n_col = lax.axis_size("dp"), lax.axis_size("row"), lax.axis_size("col")
    T, C = inputs.shape
    D = vectors.shape[1]
    row_width = w_qkv.shape[2]
    HF = row_width // n_col
    UT = w_up.shape[1] // (2 * n_col)
    score_scale = HEAD_DIM ** (-0.5)
    feat_start = (row_index * n_col + col_index) * HF
    unit_a = (row_index * 2 * n_col + col_index) * UT
    unit_b = unit_a + n_col * UT
    col_start = col_index * C
    gain, shift = vectors[5], vectors[6]
    norm_gain = lax.dynamic_slice_in_dim(gain, col_start, C)
    out_bias = lax.dynamic_slice_in_dim(vectors[3] + vectors[4], col_start, C)
    qkv_bias = lax.dynamic_slice_in_dim(vectors[0:3], feat_start, HF, axis=1)
    up_flat = vectors[7:].reshape(-1)
    up_bias = jnp.concatenate(
        [
            lax.dynamic_slice_in_dim(up_flat, unit_a, UT),
            lax.dynamic_slice_in_dim(up_flat, unit_b, UT),
        ]
    )
    w_q = (
        w_qkv.reshape(C, 3, n_col, HF).transpose(2, 0, 1, 3).reshape(n_col, C, 3 * HF)
    )
    x_full, cot_rows, w_in, w_fin = gather_all(
        inputs, cotangent, w_q, w_up, w_out, w_down, n_dp, n_row, n_col
    )
    seq_rows = x_full.shape[0]

    x_wide = x_full.astype(F32)
    mean_all = jnp.mean(x_wide, axis=1, keepdims=True)
    var_all = jnp.mean(x_wide * x_wide, axis=1, keepdims=True) - mean_all * mean_all
    rstd_all = lax.rsqrt(var_all + NORM_EPS)
    normed = ((x_wide - mean_all) * rstd_all * gain + shift).astype(BF16)

    mixed_out = jnp.dot(normed, w_in, preferred_element_type=F32)
    qkv_part = mixed_out[:, : 3 * HF].reshape(seq_rows, 3, HF) + qkv_bias[None]
    up_pre = mixed_out[:, 3 * HF :] + up_bias
    heads_here = HF // HEAD_DIM
    seq_count = seq_rows // SEQ_LEN

    def by_seq(tensor_in):
        return tensor_in.reshape((seq_count, SEQ_LEN) + tensor_in.shape[1:])

    cosine, sine_tab = rotary_tables(positions)
    queries = rotate(
        qkv_part[:, 0].reshape(seq_rows, heads_here, HEAD_DIM), cosine, sine_tab, 1.0
    ).astype(BF16)
    key_vecs = rotate(
        qkv_part[:, 1].reshape(seq_rows, heads_here, HEAD_DIM), cosine, sine_tab, 1.0
    ).astype(BF16)
    values = qkv_part[:, 2].reshape(seq_rows, heads_here, HEAD_DIM).astype(BF16)
    attended, logsum = jax.vmap(attend_forward, in_axes=(0, 0, 0, 0, None))(
        by_seq(queries), by_seq(key_vecs), by_seq(values), by_seq(segments), score_scale
    )
    attn_low = attended.reshape(seq_rows, HF).astype(BF16)
    act_low = gelu_value(up_pre).astype(BF16)
    hidden = jnp.concatenate([attn_low, act_low], axis=1)

    partial_out = jnp.dot(hidden, w_fin, preferred_element_type=F32).astype(BF16)
    branch = lax.psum_scatter(partial_out, "row", scatter_dimension=0, tiled=True)
    branch = lax.psum_scatter(branch, "col", scatter_dimension=1, tiled=True).astype(F32)
    x_val = inputs.astype(F32)
    result = x_val + branch + out_bias

    cot_val = cotangent.astype(F32)
    grad_w_fin = jnp.einsum("ti,tj->ij", hidden, cot_rows, preferred_element_type=F32).astype(BF16)
    back = jnp.einsum("tj,ij->ti", cot_rows, w_fin, preferred_element_type=F32)
    grad_attn_low = back[:, :HF].astype(BF16)
    grad_up = back[:, HF:] * gelu_slope(up_pre)
    g_queries, g_keys, g_values = jax.vmap(attend_backward, in_axes=(0, 0, 0, 0, 0, 0, 0, None))(
        by_seq(queries),
        by_seq(key_vecs),
        by_seq(values),
        by_seq(attn_low.reshape(seq_rows, heads_here, HEAD_DIM)),
        by_seq(grad_attn_low.reshape(seq_rows, heads_here, HEAD_DIM)),
        logsum,
        by_seq(segments),
        score_scale,
    )
    g_queries = rotate(
        g_queries.reshape(seq_rows, heads_here, HEAD_DIM), cosine, sine_tab, -1.0
    ).reshape(seq_rows, HF)
    g_keys = rotate(g_keys.reshape(seq_rows, heads_here, HEAD_DIM), cosine, sine_tab, -1.0).reshape(
        seq_rows, HF
    )
    g_values = g_values.reshape(seq_rows, HF)
    grad_mixed = jnp.concatenate([g_queries, g_keys, g_values, grad_up], axis=1)
    grad_mixed_low = grad_mixed.astype(BF16)
    grad_w_in = jnp.einsum(
        "ti,tj->ij", normed, grad_mixed_low, preferred_element_type=F32
    ).astype(BF16)
    partial_norm = jnp.einsum(
        "tj,ij->ti", grad_mixed_low, w_in, preferred_element_type=F32
    ).astype(BF16)
    grad_norm = lax.psum_scatter(partial_norm, "row", scatter_dimension=0, tiled=True)
    grad_norm = lax.psum_scatter(grad_norm, "col", scatter_dimension=1, tiled=True).astype(F32)

    mean_x = lax.dynamic_slice_in_dim(mean_all, row_index * T, T)
    inv_std = lax.dynamic_slice_in_dim(rstd_all, row_index * T, T)
    x_hat = (x_val - mean_x) * inv_std
    grad_hat = grad_norm * norm_gain
    back_stats = lax.psum((jnp.sum(grad_hat, axis=1), jnp.sum(grad_hat * x_hat, axis=1)), "col")
    grad_x = inv_std * (
        grad_hat - (back_stats[0] / D)[:, None] - x_hat * (back_stats[1] / D)[:, None]
    )
    grad_input = cot_val + grad_x

    sums = jnp.sum(grad_mixed, axis=0)
    qkv_sums = sums[: 3 * HF].reshape(3, HF)
    out_sums = jnp.sum(cot_val, axis=0)
    norm_sums = jnp.stack(
        [out_sums, out_sums, jnp.sum(grad_norm * x_hat, axis=0), jnp.sum(grad_norm, axis=0)]
    )
    qkv_rows = lax.dynamic_update_slice_in_dim(
        jnp.zeros((3, D), F32), qkv_sums, feat_start, axis=1
    )
    norm_rows = lax.dynamic_update_slice_in_dim(
        jnp.zeros((4, D), F32), norm_sums, col_start, axis=1
    )
    up_rows = jnp.zeros((up_flat.shape[0],), F32)
    up_rows = lax.dynamic_update_slice_in_dim(up_rows, sums[3 * HF : 3 * HF + UT], unit_a, axis=0)
    up_rows = lax.dynamic_update_slice_in_dim(up_rows, sums[3 * HF + UT :], unit_b, axis=0)
    local_vec = jnp.concatenate([qkv_rows, norm_rows, up_rows.reshape(-1, D)], axis=0)
    vec_grad = lax.psum(local_vec, ("dp", "row", "col"))
    scaled = vec_grad * lax.rsqrt(jnp.mean(vec_grad * vec_grad, axis=1, keepdims=True) + STAT_EPS)
    vec_moment_new = MOMENTUM_RATE * vector_moment + scaled
    vectors_new = vectors - VECTOR_RATE * vec_moment_new

    wi4 = lax.all_to_all(grad_w_in.reshape(n_col, C, -1), "col", 0, 0)
    wf4 = lax.all_to_all(
        grad_w_fin.reshape(-1, n_col, C).transpose(1, 0, 2), "col", 0, 0
    )
    grad_qkv = (
        wi4[:, :, : 3 * HF].reshape(n_col, C, 3, HF).transpose(1, 2, 0, 3).reshape(C, 3, row_width)
    )
    grad_up_w = (
        wi4[:, :, 3 * HF :].reshape(n_col, C, 2, UT).transpose(1, 2, 0, 3).reshape(C, -1)
    )
    grad_w_out = wf4[:, :HF].reshape(-1, C)
    grad_w_down = wf4[:, HF:].reshape(n_col, 2, UT, C).transpose(1, 0, 2, 3).reshape(-1, C)
    grad_tiles = tile_blocks(grad_qkv, grad_w_out, grad_up_w, grad_w_down)
    owned_grads = lax.psum_scatter(grad_tiles, "dp", scatter_dimension=0, tiled=True).astype(F32)
    owned_count = owned_grads.shape[0]
    weight_tiles = lax.dynamic_slice_in_dim(
        tile_blocks(w_qkv, w_out, w_up, w_down), d_index * owned_count, owned_count, 0
    ).astype(F32)
    moment_new = MOMENTUM_RATE * tile_moment[0, 0] + owned_grads
    ortho_tiles = jax.vmap(newton_schulz)(moment_new)
    tile_ratio = math.sqrt(max(1.0, moment_new.shape[1] / moment_new.shape[2]))
    tiles_new = weight_tiles - MUON_RATE * tile_ratio * ortho_tiles.astype(F32)
    return (
        result,
        grad_input,
        owned_grads[None, None],
        tiles_new[None, None],
        moment_new[None, None],
        vec_grad,
        vectors_new,
        vec_moment_new,
    )


def solution(mesh):
    placed = (
        P(("dp", "row"), "col"),
        P(("dp", "row"), "col"),
        P("dp"),
        P("dp"),
        P("col", None, "row"),
        P("row", "col"),
        P("col", "row"),
        P("row", "col"),
        P(),
        P("row", "col", "dp", None, None),
        P(),
    )
    return jax.shard_map(
        body,
        mesh=mesh,
        in_specs=placed,
        out_specs=(
            P(("dp", "row"), "col"),
            P(("dp", "row"), "col"),
            P("row", "col", "dp", None, None),
            P("row", "col", "dp", None, None),
            P("row", "col", "dp", None, None),
            P(),
            P(),
            P(),
        ),
        check_vma=False,
    )
```

time: 1780 us -> 770 us (0.43)
  waiting for transfers between devices: 1460 us -> 322 us
  Pallas kernels: 0 us -> 169 us
  matrix products: 116 us -> 86.6 us
    reduce_scatter x6 -> x5, waiting for transfers between devices: 933 us -> 90 us  [the longest x1 42.1 us: body(): lax.psum_scatter(grad_tiles, 'dp', scatter_dimension=0, tiled=True)]
    all_gather x5 -> x0, waiting for transfers between devices: 434 us -> none  [the longest x1 250 us: body(): lax.all_gather(grad_mixed.astype(jnp.bfloat16), 'col', axis=1, tiled=True)]
    pallas_call x0 -> x1, Pallas kernels: none -> 169 us  [gather_all(): pl.pallas_call(functools.partial(gather_kernel, n_dp, n_row, n_col, (T, C...]
    all_to_all x0 -> x2, waiting for transfers between devices: none -> 109 us  [the longest x1 72.2 us: body(): wi4 = lax.all_to_all(grad_w_in.reshape(n_col, C, -1), 'col', 0, 0)]
    psum x1, waiting for transfers between devices: 92.2 us -> 122 us  [body(): vec_grad = lax.psum(local_vec, ('dp', 'row', 'col'))]
    dot_general x27 -> x25, matrix products: 103 us -> 84.4 us  [the longest x1 14.9 us: body(): jnp.einsum('ti,tj->ij', normed, grad_mixed_low, preferred_element_type=F32)]
    unnamed x101 -> x91, local copies, waits for them, and re-layouts: 34.4 us -> 36.4 us
  transfers between devices with their start and end apart: 12 -> 8, of which waited for: 11 -> 6; matrix products, arithmetic and copies ran while one was open for 13% -> 18% of each run, Pallas kernels for 0% -> 0%
where the time goes in v1:
time: 770 us; the launch traced here: 764 us
  waiting for transfers between devices  322 us (42%)
  Pallas kernels  169 us (22%)
  local copies, waits for them, and re-layouts  94.6 us (12%)
  matrix products  86.6 us (11%)
  other arithmetic  56.9 us (7%)
  between operations  15.2 us (2%)
  blocking collectives  10.3 us (1%)
  starting transfers between devices  8.71 us (1%)
    pallas_call x1, Pallas kernels, gather_all(): pl.pallas_call(functools.partial(gather_kernel, n_dp, n_row, n_col, (T, C...  169 us
    psum x1, waiting for transfers between devices, body(): vec_grad = lax.psum(local_vec, ('dp', 'row', 'col'))  122 us
    all_to_all x1, waiting for transfers between devices, body(): wi4 = lax.all_to_all(grad_w_in.reshape(n_col, C, -1), 'col', 0, 0)  72.2 us
    reduce_scatter x1, waiting for transfers between devices, body(): lax.psum_scatter(grad_tiles, 'dp', scatter_dimension=0, tiled=True)  42.1 us
    all_to_all x1, waiting for transfers between devices, body(): lax.all_to_all(grad_w_fin.reshape(-1, n_col, C).transpose(1, 0, 2), 'col'...  36.9 us
    unnamed x91, local copies, waits for them, and re-layouts  36.4 us
    reduce_scatter x1, waiting for transfers between devices, body(): lax.psum_scatter(branch, 'col', scatter_dimension=1, tiled=True).astype(F32)  33 us
  transfers between devices with their start and end apart: 8, of which 6 were waited for; matrix products, arithmetic and copies ran while one was open for 18% of the time, Pallas kernels for 0%

profile of v1, /device:TPU:0, one launch (start us, length us, event | category | flops | bytes accessed | tf_op | source)
XLA Modules:
  0.0 763.6 jit_solution(18256211764555426689)
XLA Ops:
  14.4 169.4 %gather_all.1 = (bf16[2048,2048]{1,0:T(8,128)(2,1)}, bf16[2048,2048]{1,0:T(8,128)(2,1)}, bf16[2048,896]{1,0:T(8,128)(2,1)}, bf16[640,2048]{1,0:T(8,128)(2,1)}) custom-call(bf16[512,512]{1,0:T(8,128)(2,1)} %x_ref.1, bf16[512,512]{1,0:T(8,128)(2,1)} %g_ref.1, bf16[4,512,384]{2,1,0:T(8,128)(2,1)} %copy.82.wq_ref, bf16[512,2048]{1,0:T(8,128)(2,1)} %wu_ref.1, ...), custom_call_target="tpu_custom_call" | custom-call | tf_op jit(solution)/shard_map/gather_all/pallas_call | solution.py:351
  183.9 5.9 convert_reduce_fusion
  189.8 3.9 fusion.3
  193.8 8.2 %fusion.41 = f32[2048,896]{0,1:T(8,128)S(1)} fusion(bf16[2048,2048]{1,0:T(8,128)(2,1)S(1)} %fusion.3, bf16[2048,896]{1,0:T(8,128)(2,1)S(1)} %copy-done.30), kind=kOutput, calls=%fused_computation.149 | convolution fusion | flops 7516192768 | bytes 19398656 | tf_op jit(solution)/shard_map/dot_general | solution.py:437
  202.0 2.9 copy-done.11
  206.7 9.3 %fusion.42 = f32[2048,640]{0,1:T(8,128)S(1)} fusion(bf16[2048,2048]{1,0:T(8,128)(2,1)} %get-tuple-element.15, bf16[640,2048]{1,0:T(8,128)(2,1)} %get-tuple-element.14), kind=kOutput, calls=%fused_computation.150 | convolution fusion | flops 5368709120 | bytes 16252928 | tf_op jit(solution)/shard_map/tj,ij->ti/dot_general | solution.py:469
  216.0 2.3 copy-done.12
  221.9 1.9 broadcast_multiply_fusion
  224.9 1.9 fusion.7
  226.8 2.0 fusion.5
  228.8 4.4 fusion.6
  234.0 3.4 multiply_convert_fusion
  239.8 6.7 fusion.15
  252.2 11.2 %convolution_convert_fusion = bf16[2048,2048]{1,0:T(8,128)(2,1)} fusion(bf16[2048,896]{1,0:T(8,128)(2,1)S(1)} %copy-done.31, f32[2048,512]{0,1:T(8,128)S(1)} %get-tuple-element.30, f32[2048,128]{0,1:T(8,128)S(1)} %bitcast.196, f32[2048,128]{0,1:T(8,128)S(1)} %bitcast.202, f32[2048,128]{0,1:T(8,128)S(1)} %bitcast.199), kind=kOutput, calls=%fused_computation.15 | convolution fusion | flops 7535067136 | bytes 19398656 | tf_op jit(solution)/shard_map/tj,ij->ti/dot_general | solution.py:494
  264.9 11.5 %convolution_convert_fusion.1 = bf16[2048,2048]{1,0:T(8,128)(2,1)} fusion(bf16[640,2048]{1,0:T(8,128)(2,1)} %get-tuple-element.14, bf16[2048,512]{0,1:T(8,128)(2,1)S(1)} %copy-done.19, bf16[2048,128]{0,1:T(8,128)(2,1)S(1)} %bitcast.232), kind=kOutput, calls=%fused_computation.16 | convolution fusion | flops 5378146304 | bytes 13631488 | tf_op jit(solution)/shard_map/dot_general | solution.py:461
  276.4 8.0 %convolution_convert_fusion.3 = bf16[640,2048]{1,0:T(8,128)(2,1)S(1)} fusion(bf16[2048,2048]{1,0:T(8,128)(2,1)} %get-tuple-element.15, bf16[2048,512]{0,1:T(8,128)(2,1)S(1)} %copy-done.19, bf16[2048,128]{0,1:T(8,128)(2,1)S(1)} %bitcast.233), kind=kOutput, calls=%fused_computation.43 | convolution fusion | flops 5375262720 | bytes 13631488 | tf_op jit(solution)/shard_map/ti,tj->ij/dot_general | solution.py:468
  286.1 3.7 all-to-all-start.1
  289.7 14.9 %convolution_convert_fusion.2 = bf16[2048,896]{1,0:T(8,128)(2,1)} fusion(bf16[2048,2048]{1,0:T(8,128)(2,1)} %copy-done.7, f32[2048,512]{0,1:T(8,128)} %copy-done.3, f32[2048,128]{0,1:T(8,128)} %bitcast.197, f32[2048,128]{0,1:T(8,128)} %bitcast.203, f32[2048,128]{0,1:T(8,128)} %bitcast.200), kind=kOutput, calls=%fused_computation.42 | convolution fusion | flops 7532707840 | bytes 19398656 | tf_op jit(solution)/shard_map/ti,tj->ij/dot_general | solution.py:491
  304.6 5.9 copy.103
  310.6 36.9 %all-to-all-done.1 = bf16[4,640,512]{2,1,0:T(8,128)(2,1)S(1)} async-done(((bf16[4,640,512]{2,1,0:T(8,128)(2,1)}), bf16[4,640,512]{2,1,0:T(8,128)(2,1)S(1)}, u32[]{:S(2)}, u32[]{:S(2)}) %all-to-all-start.1) | async-done | bytes 2621472 | tf_op jit(solution)/shard_map/all_to_all | solution.py:532
  347.4 4.8 all-to-all-start
  354.0 4.1 reshape_reshape.16
  358.1 3.2 copy.112
  361.5 72.2 %all-to-all-done = bf16[4,512,896]{1,2,0:T(8,128)(2,1)} async-done(((bf16[4,512,896]{1,2,0:T(8,128)(2,1)}), bf16[4,512,896]{1,2,0:T(8,128)(2,1)}, u32[]{:S(2)}, u32[]{:S(2)}) %all-to-all-start) | async-done | bytes 3670048 | tf_op jit(solution)/shard_map/all_to_all | solution.py:531
  433.8 3.0 slice.191
  436.8 2.8 copy.110
  443.7 2.1 copy.106
  445.7 2.0 copy.105
  447.8 2.0 bitcast_dynamic-update-slice_fusion.8
  449.8 1.9 bitcast_dynamic-update-slice_fusion.7
  457.5 4.1 copy.121
  461.6 4.1 reshape.296
  469.1 2.2 copy.118
  473.4 2.4 copy.122
  475.7 2.0 copy.123
  478.5 1.8 fusion.8
  486.8 2.7 copy-done.17
  489.6 42.1 %reduce-scatter.14.cloned.1.call-done = bf16[12,512,256]{2,1,0:T(8,128)(2,1)} async-done(((bf16[24,512,256]{2,1,0:T(8,128)(2,1)}), bf16[12,512,256]{2,1,0:T(8,128)(2,1)}) %reduce-scatter.14.cloned.1.call-update) | async-done | bytes 3145744 | tf_op jit(solution)/shard_map/reduce_scatter | solution.py:544
  531.7 5.0 multiply_reduce_fusion
  536.7 6.8 fusion.16
  559.0 3.6 subtract_bitcast_fusion
  562.6 14.9 %reduce-scatter.12.cloned.1.call-done = bf16[512,512]{1,0:T(8,128)(2,1)} async-done(((bf16[512,2048]{1,0:T(8,128)(2,1)}), bf16[512,512]{1,0:T(8,128)(2,1)}) %reduce-scatter.12.cloned.1.call-update) | async-done | bytes 524304 | tf_op jit(solution)/shard_map/reduce_scatter | solution.py:498
  577.5 1.8 fusion.27
  579.3 10.3 %all-reduce = (f32[512]{0:T(512)S(1)}, f32[512]{0:T(512)S(1)}) all-reduce(f32[512]{0:T(512)S(1)} %get-tuple-element.19, f32[512]{0:T(512)S(1)} %get-tuple-element.20), channel_id=1, replica_groups=mesh['dp'=2,'row'=4,'col'=4] {'col'}, use_global_device_ids=true, to_apply=%region_12.13 | all-reduce | flops 1024 | bytes 8192 | tf_op jit(solution)/shard_map/psum | solution.py:504
  589.5 33.0 %reduce-scatter.8.cloned.1.call-done = bf16[512,512]{1,0:T(8,128)(2,1)} async-done(((bf16[512,2048]{1,0:T(8,128)(2,1)}), bf16[512,512]{1,0:T(8,128)(2,1)}) %reduce-scatter.8.cloned.1.call-update) | async-done | bytes 524304 | tf_op jit(solution)/shard_map/reduce_scatter | solution.py:463
  622.5 3.4 convert_reduce_fusion.2
  626.7 3.3 convert_bitcast_fusion
  630.0 122.2 %all-reduce.3.cloned.1.call-done = f32[11,2048]{1,0:T(8,128)} async-done(((f32[11,2048]{1,0:T(8,128)}), f32[11,2048]{1,0:T(8,128)}) %all-reduce.3.cloned.1.call-update) | async-done | bytes 90128 | tf_op jit(solution)/shard_map/psum | solution.py:526
  (187 shorter events, 70.4 us)
Async XLA Ops:
  7.2 449.2 %reduce-scatter.10.cloned.1.call-start = ((), (), s32[]{:S(2)}) async-start(), calls=%async_computation.9 | async-start | bytes 10485760 | tf_op jit(solution)/shard_map/reduce_scatter | solution.py:497
  10.9 178.9 %copy-start.27 = (f32[1,2048]{1,0:T(1,128)}, f32[1,2048]{1,0:T(1,128)S(1)}, u32[]{:S(2)}) copy-start(f32[1,2048]{1,0:T(1,128)S(1)} %get-tuple-element.57) | copy-start | bytes 24580
  12.7 171.1 %copy-start.5 = (bf16[512,3,512]{0,2,1:T(8,128)(2,1)}, bf16[512,3,512]{0,2,1:T(8,128)(2,1)S(1)}, u32[]{:S(2)}) copy-start(bf16[512,3,512]{0,2,1:T(8,128)(2,1)S(1)} %copy.80) | copy-start | bytes 4718596
  183.8 6.0 copy-start
  189.8 4.0 copy-start.25
  189.8 4.0 copy-start.26
  189.8 4.0 copy-start.30
  193.7 8.3 %copy-start.7 = (bf16[2048,2048]{1,0:T(8,128)(2,1)}, bf16[2048,2048]{1,0:T(8,128)(2,1)S(1)}, u32[]{:S(2)}) copy-start(bf16[2048,2048]{1,0:T(8,128)(2,1)S(1)} %fusion.3) | copy-start | bytes 25165828
  202.0 3.0 copy-start.11
  205.0 0.7 slice-start.2
  206.0 0.7 copy-start.28
  206.0 0.7 copy-start.29
  216.0 2.4 copy-start.12
  228.8 4.4 copy-start.20
  238.8 0.9 copy-start.23
  239.8 6.7 copy-start.2
  246.5 3.4 copy-start.3
  248.6 0.9 copy-start.21
  249.0 1.0 copy-start.13
  249.2 3.0 copy-start.31
  249.7 1.0 copy-start.15
  249.8 1.2 copy-start.16
  263.3 1.6 copy-start.19
  263.3 226.2 %reduce-scatter.6.cloned.1.call-start = ((), (), s32[]{:S(2)}) async-start(), calls=%async_computation.7 | async-start | bytes 10485760 | tf_op jit(solution)/shard_map/reduce_scatter | solution.py:462
  286.1 61.4 %all-to-all-start.1 = ((bf16[4,640,512]{2,1,0:T(8,128)(2,1)}), bf16[4,640,512]{2,1,0:T(8,128)(2,1)S(1)}, u32[]{:S(2)}, u32[]{:S(2)}) async-start(bf16[4,640,512]{2,1,0:T(8,128)(2,1)} %bitcast.185), calls=%async_computation.5 | async-start | bytes 5242880 | tf_op jit(solution)/shard_map/all_to_all | solution.py:532
  347.4 86.3 %all-to-all-start = ((bf16[4,512,896]{1,2,0:T(8,128)(2,1)}), bf16[4,512,896]{1,2,0:T(8,128)(2,1)}, u32[]{:S(2)}, u32[]{:S(2)}) async-start(bf16[4,512,896]{1,2,0:T(8,128)(2,1)} %copy.103), calls=%async_computation.4 | async-start | bytes 7340032 | tf_op jit(solution)/shard_map/all_to_all | solution.py:531
  352.3 179.4 %reduce-scatter.14.cloned.1.call-start = ((), (), s32[]{:S(2)}) async-start(), calls=%async_computation.11 | async-start | bytes 9437184 | tf_op jit(solution)/shard_map/reduce_scatter | solution.py:544
  447.8 7.0 copy-start.8
  456.3 1.0 copy-start.18
  456.3 121.2 %reduce-scatter.12.cloned.1.call-start = ((), (), s32[]{:S(2)}) async-start(), calls=%async_computation.10 | async-start | bytes 2621440 | tf_op jit(solution)/shard_map/reduce_scatter | solution.py:498
  456.9 165.6 %reduce-scatter.8.cloned.1.call-start = ((), (), s32[]{:S(2)}) async-start(), calls=%async_computation.8 | async-start | bytes 2621440 | tf_op jit(solution)/shard_map/reduce_scatter | solution.py:463
  457.5 10.7 %copy-start.6 = (bf16[512,3,512]{0,2,1:T(8,128)(2,1)S(1)}, bf16[512,3,512]{0,2,1:T(8,128)(2,1)}, u32[]{:S(2)}) copy-start(bf16[512,3,512]{0,2,1:T(8,128)(2,1)} %copy-done.5) | copy-start | bytes 4718596
  469.1 4.2 copy-start.10
  473.3 4.4 copy-start.14
  475.7 2.8 copy-start.4
  480.5 5.9 copy-start.9
  486.8 2.7 copy-start.17
  489.5 262.7 %all-reduce.3.cloned.1.call-start = ((), (), s32[]{:S(2)}) async-start(), calls=%async_computation.12 | async-start | bytes 262144 | tf_op jit(solution)/shard_map/psum | solution.py:526
  531.7 5.1 copy-start.1
  555.9 2.2 slice-start
  556.5 2.4 slice-start.1
  626.7 126.6 %copy-start.22 = (f32[11,2048]{1,0:T(8,128)S(1)}, f32[11,2048]{1,0:T(8,128)}, u32[]{:S(2)}) copy-start(f32[11,2048]{1,0:T(8,128)} %param.19) | copy-start | bytes 270340
  626.7 126.6 %copy-start.24 = (f32[11,2048]{1,0:T(8,128)S(1)}, f32[11,2048]{1,0:T(8,128)}, u32[]{:S(2)}) copy-start(f32[11,2048]{1,0:T(8,128)} %param.21) | copy-start | bytes 270340
Sparse Core Ops, SparseCore 0:
  263.4 68.4 reduce-scatter.9
  334.5 71.3 reduce-scatter.5
  456.4 75.1 reduce-scatter.13
  533.8 43.6 reduce-scatter.11
  579.6 42.8 reduce-scatter.7
  628.5 123.6 all-reduce.2

commit v2 on v1

--- a/solution.py
+++ b/solution.py
@@ -146,6 +146,8 @@
                   zs, zr, ys, yr, cs, cr, ws, wr, ds, dr, ls, lo):
     T, C, HF, UT = dims
     d, r, c = lax.axis_index("dp"), lax.axis_index("row"), lax.axis_index("col")
+    r1 = r + 1 - 2 * lax.rem(r, 2)
+    r2 = lax.rem(r + 2, n_row)
     chunks = 2
     tc = T // chunks
     qw = 3 * HF
@@ -155,7 +157,7 @@
         return acts[a][1].at[pl.ds(rr * T + t * tc, tc), pl.ds(cc * C, C)]
 
     barrier = pltpu.get_barrier_semaphore()
-    peers = [{"row": r ^ 1}, {"row": r ^ 2}]
+    peers = [{"row": r1}, {"row": r2}]
     peers += [{"col": lax.rem(c + k, n_col)} for k in range(1, n_col)]
     peers += [{"dp": lax.rem(d + k, n_dp)} for k in range(1, n_dp)]
     for peer in peers:
@@ -175,11 +177,11 @@
         return copy(src, blk(a, r, cc, t), zs.at[a, t, int(right), cc], zr.at[a, t, cc], peer)
 
     def y_copy(a, t, cc, src):
-        return copy(src, blk(a, r, cc, t), ys.at[a, t, cc], yr.at[a, t, cc], {"row": r ^ 2})
+        return copy(src, blk(a, r, cc, t), ys.at[a, t, cc], yr.at[a, t, cc], {"row": r2})
 
     def c_copy(a, t, cc, src, rr, which):
         return copy(
-            src, blk(a, rr, cc, t), cs.at[a, t, which, cc], cr.at[a, t, which, cc], {"row": r ^ 1}
+            src, blk(a, rr, cc, t), cs.at[a, t, which, cc], cr.at[a, t, which, cc], {"row": r1}
         )
 
     order = [(a, t) for a in range(2) for t in range(chunks)]
@@ -304,7 +306,7 @@
                 @pl.when((cc >= 0) & (cc < n_col))
                 def _(a=a, t=t, cc=cc):
                     y_copy(a, t, cc, blk(a, r, cc, t)).wait_recv()
-                    c_copy(a, t, cc, blk(a, r ^ 2, cc, t), r ^ 2, 1).start()
+                    c_copy(a, t, cc, blk(a, r2, cc, t), r2, 1).start()
 
     for k in range(1, n_col):
         for part in parts:
@@ -382,6 +384,514 @@
     )(x, g, w_q, w_up, w_out, w_down)
 
 
+def pick(index, table):
+    out = jnp.int32(table[0])
+    for k in range(1, len(table)):
+        out = jnp.where(index == k, jnp.int32(table[k]), out)
+    return out
+
+
+def reduce_kernel(n_row, n_col, dims, p_ref, q_ref, dwi_ref, dwf_ref,
+                  res_ref, gn_ref, tiles_ref,
+                  abuf, obuf, sbuf, bbuf, zsb, zin, gi, gf, oi, of,
+                  a_s, a_r, o_l, y_s, y_r, z_s, z_r, x_s, x_r, g_l, t_s, t_r):
+    T, C, HF, UT, chunks = dims
+    tc = T // chunks
+    step_rows = 64
+    d, r, c = lax.axis_index("dp"), lax.axis_index("row"), lax.axis_index("col")
+    r1 = r + 1 - 2 * lax.rem(r, 2)
+    r2 = lax.rem(r + 2, n_row)
+    r12 = lax.rem(r1 + 2, n_row)
+    srcs = (p_ref, q_ref)
+    outs = (res_ref, gn_ref)
+    far = [
+        sorted(range(n_col), key=lambda f: (-abs(f - cc), f < cc if cc < n_col // 2 else f > cc))
+        for cc in range(n_col)
+    ]
+    forder = [pick(c, [far[cc][i] for cc in range(n_col)]) for i in range(n_col)]
+
+    barrier = pltpu.get_barrier_semaphore()
+    peers = [{"row": r1}, {"row": r2}, {"dp": 1 - d}]
+    peers += [{"col": lax.rem(c + k, n_col)} for k in range(1, n_col)]
+    for peer in peers:
+        pl.semaphore_signal(barrier, inc=1, device_id=peer, device_id_type=MESH)
+    pl.semaphore_wait(barrier, len(peers))
+
+    def copy(src, dst, s, rcv, peer):
+        return pltpu.make_async_remote_copy(
+            src_ref=src, dst_ref=dst, send_sem=s, recv_sem=rcv, device_id=peer, device_id_type=MESH
+        )
+
+    def unit(v, rr, f, t):
+        return srcs[v].at[pl.ds(rr * T + t * tc, tc), pl.ds(f * C, C)]
+
+    def a_copy(v, h, f, t):
+        return copy(
+            unit(v, r12 if h else r1, f, t), abuf.at[v, h, f, t],
+            a_s.at[v, h, f, t], a_r.at[v, h, f, t], {"row": r1},
+        )
+
+    def o_copy(v, h, f, t):
+        return pltpu.make_async_copy(
+            unit(v, r2 if h else r, f, t), obuf.at[v, h, f, t], o_l.at[v, h, f, t]
+        )
+
+    def y_copy(v, f, t):
+        return copy(sbuf.at[v, f, t], bbuf.at[v, f, t], y_s.at[v, f, t], y_r.at[v, f, t],
+                    {"row": r2})
+
+    def z_copy(v, f, t, slot, step):
+        return copy(zsb.at[v, f, t], zin.at[v, slot, t], z_s.at[v, f, t], z_r.at[v, slot, t],
+                    {"col": c + step})
+
+    for v in range(2):
+        for i in range(n_col):
+            for t in range(chunks):
+                for h in (1, 0):
+                    a_copy(v, h, forder[i], t).start()
+                    o_copy(v, h, forder[i], t).start()
+
+    qw, n_in, n_out = 3 * HF, 3 * HF + 2 * UT, HF + 2 * UT
+    wide = (qw + UT, UT)
+    lane0 = (0, qw + UT)
+    tall = (HF, 2 * UT)
+    row0 = (0, HF)
+
+    def gi_src(own, cc):
+        return dwi_ref.at[pl.ds(cc * C, C), pl.ds(lane0[own], wide[own])]
+
+    def gf_src(own, cc):
+        return dwf_ref.at[pl.ds(row0[own], tall[own]), pl.ds(cc * C, C)]
+
+    def xi_copy(own, cc):
+        return copy(gi_src(own, cc), gi.at[cc, :, pl.ds(0, wide[own])], x_s.at[0, cc],
+                    x_r.at[0, cc], {"dp": 1 - d})
+
+    def xf_copy(own, cc):
+        return copy(gf_src(own, cc), gf.at[cc, pl.ds(0, tall[own]), :], x_s.at[1, cc],
+                    x_r.at[1, cc], {"dp": 1 - d})
+
+    def li_copy(own, cc):
+        return pltpu.make_async_copy(gi_src(own, cc), oi.at[cc, :, pl.ds(0, wide[own])],
+                                     g_l.at[0, cc])
+
+    def lf_copy(own, cc):
+        return pltpu.make_async_copy(gf_src(own, cc), of.at[cc, pl.ds(0, tall[own]), :],
+                                     g_l.at[1, cc])
+
+    def tile_parts(own, cc, source):
+        half, odd = source // 2, lax.rem(source, 2)
+        lw = 2 * HF
+        if own == 0:
+            parts = [
+                (oi.at[cc, :, pl.ds(j * HF, HF)], tiles_ref.at[2 * j + half, :, pl.ds(odd * HF, HF)])
+                for j in range(3)
+            ]
+            parts += [(oi.at[cc, :, pl.ds(qw, UT)], tiles_ref.at[8 + source])]
+            parts += [
+                (of.at[cc, pl.ds(0, HF), pl.ds(j * lw, lw)],
+                 tiles_ref.at[6 + j, pl.ds(source * HF, HF), :])
+                for j in range(2)
+            ]
+            return parts
+        parts = [(oi.at[cc, :, pl.ds(0, UT)], tiles_ref.at[source])]
+        for m in range(2):
+            for j in range(2):
+                parts.append(
+                    (of.at[cc, pl.ds(m * UT, UT), pl.ds(j * lw, lw)],
+                     tiles_ref.at[4 + 2 * (2 * m + half) + j, pl.ds(odd * UT, UT), :])
+                )
+        return parts
+
+    def t_copies(own, cc):
+        return [
+            copy(src, dst, t_s.at[n, cc], t_r.at[n, c], {"col": cc})
+            for n, (src, dst) in enumerate(tile_parts(own, cc, c))
+        ]
+
+    def t_waits(own, source):
+        return [
+            copy(src, dst, t_s.at[n, source], t_r.at[n, source], {"col": source})
+            for n, (src, dst) in enumerate(tile_parts(own, source, source))
+        ]
+
+    def t_local(own):
+        return [
+            pltpu.make_async_copy(src, dst, t_s.at[n, c])
+            for n, (src, dst) in enumerate(tile_parts(own, c, c))
+        ]
+
+    for i in range(n_col):
+        for own in range(2):
+            @pl.when(d == own)
+            def _(own=own, i=i):
+                xi_copy(1 - own, forder[i]).start()
+                xf_copy(1 - own, forder[i]).start()
+                li_copy(own, forder[i]).start()
+                lf_copy(own, forder[i]).start()
+
+    def looped(rows, fn):
+        def one(k, carry):
+            fn(pl.ds(pl.multiple_of(k * step_rows, step_rows), step_rows))
+            return carry
+        lax.fori_loop(0, rows // step_rows, one, 0)
+
+    def first_sum(v, i):
+        f = forder[i]
+        for t in range(chunks):
+            a_copy(v, 1, f, t).wait_recv()
+            o_copy(v, 1, f, t).wait()
+
+            def add(rows, t=t):
+                sbuf[v, f, t, rows, :] = (
+                    obuf[v, 1, f, t, rows, :].astype(F32) + abuf[v, 1, f, t, rows, :].astype(F32)
+                ).astype(BF16)
+
+            looped(tc, add)
+            y_copy(v, f, t).start()
+
+    def second_sum(v, i):
+        f = forder[i]
+        for t in range(chunks):
+            a_copy(v, 0, f, t).wait_recv()
+            o_copy(v, 0, f, t).wait()
+            y_copy(v, f, t).wait_recv()
+
+            def base(rows, t=t):
+                return (
+                    obuf[v, 0, f, t, rows, :].astype(F32)
+                    + abuf[v, 0, f, t, rows, :].astype(F32)
+                    + bbuf[v, f, t, rows, :].astype(F32)
+                )
+
+            if i < n_col - 1:
+                right = f > c
+                step = jnp.where(right, jnp.int32(1), jnp.int32(-1))
+                landed = jnp.where(f == c + step, jnp.where(right, f, jnp.int32(n_col)), f)
+                inner = jnp.where(right, c, n_col - 1 - c) > 0
+
+                @pl.when(inner)
+                def _(t=t):
+                    z_copy(v, f, t, f, 0).wait_recv()
+
+                    def add(rows):
+                        zsb[v, f, t, rows, :] = (
+                            base(rows) + zin[v, f, t, rows, :].astype(F32)
+                        ).astype(BF16)
+
+                    looped(tc, add)
+
+                @pl.when(jnp.logical_not(inner))
+                def _(t=t):
+                    def add(rows):
+                        zsb[v, f, t, rows, :] = base(rows).astype(BF16)
+
+                    looped(tc, add)
+
+                z_copy(v, f, t, landed, step).start()
+            else:
+                out = outs[v]
+
+                def put(rows, value, t=t):
+                    out[pl.ds(pl.multiple_of(rows.start + t * tc, step_rows), step_rows), :] = value
+
+                @pl.when(c > 0)
+                def _(t=t):
+                    z_copy(v, f, t, f, 0).wait_recv()
+
+                @pl.when(c < n_col - 1)
+                def _(t=t):
+                    z_copy(v, f, t, n_col, 0).wait_recv()
+
+                @pl.when(c == 0)
+                def _(t=t):
+                    looped(tc, lambda rows: put(
+                        rows, base(rows) + zin[v, n_col, t, rows, :].astype(F32)))
+
+                @pl.when(c == n_col - 1)
+                def _(t=t):
+                    looped(tc, lambda rows: put(
+                        rows, base(rows) + zin[v, f, t, rows, :].astype(F32)))
+
+                @pl.when((c > 0) & (c < n_col - 1))
+                def _(t=t):
+                    looped(tc, lambda rows: put(
+                        rows, base(rows) + zin[v, f, t, rows, :].astype(F32)
+                        + zin[v, n_col, t, rows, :].astype(F32)))
+
+    def grad_piece(i):
+        cc = forder[i]
+        for own in range(2):
+            @pl.when(d == own)
+            def _(own=own):
+                xi_copy(own, cc).wait_recv()
+                xf_copy(own, cc).wait_recv()
+                li_copy(own, cc).wait()
+                lf_copy(own, cc).wait()
+
+                def add_i(rows):
+                    at = (cc, rows, pl.ds(0, wide[own]))
+                    oi[at] = (oi[at].astype(F32) + gi[at].astype(F32)).astype(BF16)
+
+                def add_f(rows):
+                    at = (cc, rows, slice(None))
+                    of[at] = (of[at].astype(F32) + gf[at].astype(F32)).astype(BF16)
+
+                looped(C, add_i)
+                looped(tall[own], add_f)
+                for item in t_local(own) if i == n_col - 1 else t_copies(own, cc):
+                    item.start()
+
+    for i in range(n_col):
+        first_sum(0, i)
+    for i in range(n_col):
+        second_sum(0, i)
+        first_sum(1, i)
+        grad_piece(i)
+    for i in range(n_col):
+        second_sum(1, i)
+
+    for own in range(2):
+        @pl.when(d == own)
+        def _(own=own):
+            for k in range(1, n_col):
+                for item in t_waits(own, lax.rem(c + k, n_col)):
+                    item.wait_recv()
+            for i in range(n_col - 1):
+                for item in t_copies(own, forder[i]):
+                    item.wait_send()
+            for item in t_local(own):
+                item.wait()
+            for cc in range(n_col):
+                xi_copy(1 - own, cc).wait_send()
+                xf_copy(1 - own, cc).wait_send()
+    for v in range(2):
+        for t in range(chunks):
+            for f in range(n_col):
+                a_copy(v, 0, f, t).wait_send()
+                a_copy(v, 1, f, t).wait_send()
+                y_copy(v, f, t).wait_send()
+            for i in range(n_col - 1):
+                z_copy(v, forder[i], t, forder[i], 0).wait_send()
+
+
+def reduce_all(p, q, dwi, dwf, T, C, HF, UT, n_row, n_col):
+    dma = pltpu.SemaphoreType.DMA
+    chunks = 2
+    tc = T // chunks
+    unit = (chunks, tc, C)
+    vm = pl.BlockSpec(memory_space=pltpu.VMEM)
+    return pl.pallas_call(
+        functools.partial(reduce_kernel, n_row, n_col, (T, C, HF, UT, chunks)),
+        name="reduce_all",
+        out_shape=(
+            jax.ShapeDtypeStruct((T, C), F32),
+            jax.ShapeDtypeStruct((T, C), F32),
+            jax.ShapeDtypeStruct((12, C, UT), BF16),
+        ),
+        in_specs=[ANY] * 4,
+        out_specs=(vm, vm, ANY),
+        scratch_shapes=[
+            pltpu.VMEM((2, 2, n_col) + unit, BF16),
+            pltpu.VMEM((2, 2, n_col) + unit, BF16),
+            pltpu.VMEM((2, n_col) + unit, BF16),
+            pltpu.VMEM((2, n_col) + unit, BF16),
+            pltpu.VMEM((2, n_col) + unit, BF16),
+            pltpu.VMEM((2, n_col + 1) + unit, BF16),
+            pltpu.VMEM((n_col, C, 3 * HF + UT), BF16),
+            pltpu.VMEM((n_col, 2 * UT, C), BF16),
+            pltpu.VMEM((n_col, C, 3 * HF + UT), BF16),
+            pltpu.VMEM((n_col, 2 * UT, C), BF16),
+            dma((2, 2, n_col, chunks)),
+            dma((2, 2, n_col, chunks)),
+            dma((2, 2, n_col, chunks)),
+            dma((2, n_col, chunks)),
+            dma((2, n_col, chunks)),
+            dma((2, n_col, chunks)),
+            dma((2, n_col + 1, chunks)),
+            dma((2, n_col)),
+            dma((2, n_col)),
+            dma((2, n_col)),
+            dma((6, n_col)),
+            dma((6, n_col)),
+        ],
+        compiler_params=pltpu.CompilerParams(
+            collective_id=1, has_side_effects=True, vmem_limit_bytes=62 * 1024 * 1024
+        ),
+    )(p, q, dwi, dwf)
+
+
+def finish_kernel(n_dp, n_row, n_col, width, gn_ref, x_ref, g_ref, mean_ref, rstd_ref, gain_ref, part_ref,
+                  gx_ref, va_ref, vb_ref,
+                  st, da, db, ra, rb,
+                  st_s, st_r, d_s, d_r, r_s, r_r, c_s, c_r):
+    d, r, c = lax.axis_index("dp"), lax.axis_index("row"), lax.axis_index("col")
+    T, C = gn_ref.shape
+
+    barrier = pltpu.get_barrier_semaphore()
+    dps = [lax.rem(d + k, n_dp) for k in range(1, n_dp)]
+    rows = [lax.rem(r + k, n_row) for k in range(1, n_row)]
+    cols = [lax.rem(c + k, n_col) for k in range(1, n_col)]
+    peers = [{"dp": k} for k in dps] + [{"row": k} for k in rows] + [{"col": k} for k in cols]
+    for peer in peers:
+        pl.semaphore_signal(barrier, inc=1, device_id=peer, device_id_type=MESH)
+    pl.semaphore_wait(barrier, len(peers))
+
+    def copy(src, dst, s, rcv, peer):
+        return pltpu.make_async_remote_copy(
+            src_ref=src, dst_ref=dst, send_sem=s, recv_sem=rcv, device_id=peer, device_id_type=MESH
+        )
+
+    gain = gain_ref[...]
+
+    def fold(value):
+        total = value[:, 0:128]
+        for k in range(1, C // 128):
+            total = total + value[:, k * 128 : (k + 1) * 128]
+        return jnp.sum(jnp.transpose(total), axis=0, keepdims=True)
+
+    gn = gn_ref[...]
+    x_hat = (x_ref[...].astype(F32) - mean_ref[...]) * rstd_ref[...]
+    gh = gn * gain
+    st[c, 0:1, :] = fold(gh)
+    st[c, 1:2, :] = fold(gh * x_hat)
+
+    def st_copy(k):
+        return copy(st.at[c], st.at[c], st_s.at[k], st_r.at[c], {"col": k})
+
+    def st_wait(k):
+        return copy(st.at[k], st.at[k], st_s.at[k], st_r.at[k], {"col": k})
+
+    for k in cols:
+        st_copy(k).start()
+
+    da[d] = part_ref[...]
+    db[d, 0:1, :] = jnp.sum(gn * x_hat, axis=0, keepdims=True)
+    db[d, 1:2, :] = jnp.sum(gn, axis=0, keepdims=True)
+    db[d, 2:3, :] = jnp.sum(g_ref[...].astype(F32), axis=0, keepdims=True)
+
+    def pair(a_src, b_src, a_dst, b_dst, s, rcv, peer):
+        return [copy(a_src, a_dst, s.at[0], rcv.at[0], peer),
+                copy(b_src, b_dst, s.at[1], rcv.at[1], peer)]
+
+    def d_pair(slot, peer):
+        return pair(da.at[slot], db.at[slot], da.at[slot], db.at[slot],
+                    d_s.at[peer], d_r.at[slot], {"dp": peer})
+
+    def r_pair(slot, peer):
+        return pair(ra.at[slot], rb.at[slot], ra.at[slot], rb.at[slot],
+                    r_s.at[peer], r_r.at[slot], {"row": peer})
+
+    def c_pair(slot, peer):
+        return pair(va_ref.at[slot], vb_ref.at[slot], va_ref.at[slot], vb_ref.at[slot],
+                    c_s.at[peer], c_r.at[slot], {"col": peer})
+
+    for k in dps:
+        for item in d_pair(d, k):
+            item.start()
+    for k in dps:
+        for item in d_pair(k, k):
+            item.wait_recv()
+    a_sum, b_sum = da[0], db[0]
+    for k in range(1, n_dp):
+        a_sum = a_sum + da[k]
+        b_sum = b_sum + db[k]
+    ra[r] = a_sum
+    rb[r] = b_sum
+    for k in rows:
+        for item in r_pair(r, k):
+            item.start()
+
+    for k in cols:
+        st_wait(k).wait_recv()
+    stats = st[0]
+    for k in range(1, n_col):
+        stats = stats + st[k]
+    stats = stats / width
+    m1 = jnp.transpose(jnp.broadcast_to(stats[0:1, :], (128, T)))[:, 0:1]
+    m2 = jnp.transpose(jnp.broadcast_to(stats[1:2, :], (128, T)))[:, 0:1]
+    gx_ref[...] = g_ref[...].astype(F32) + rstd_ref[...] * (gh - m1 - x_hat * m2)
+
+    for k in rows:
+        for item in r_pair(k, k):
+            item.wait_recv()
+    b_sum = rb[0]
+    for k in range(1, n_row):
+        b_sum = b_sum + rb[k]
+    for k in range(n_row):
+        va_ref[c, k] = ra[k]
+    vb_ref[c] = b_sum
+    for k in cols:
+        for item in c_pair(c, k):
+            item.start()
+    for k in cols:
+        for item in c_pair(k, k):
+            item.wait_recv()
+    for k in cols:
+        st_copy(k).wait_send()
+        for item in c_pair(c, k):
+            item.wait_send()
+    for k in dps:
+        for item in d_pair(d, k):
+            item.wait_send()
+    for k in rows:
+        for item in r_pair(r, k):
+            item.wait_send()
+
+
+def finish_all(gn, x, g, mean, rstd, gain, part, width, n_dp, n_row, n_col):
+    T, C = gn.shape
+    dma = pltpu.SemaphoreType.DMA
+    vm = pl.BlockSpec(memory_space=pltpu.VMEM)
+    return pl.pallas_call(
+        functools.partial(finish_kernel, n_dp, n_row, n_col, width),
+        name="finish_all",
+        out_shape=(
+            jax.ShapeDtypeStruct((T, C), F32),
+            jax.ShapeDtypeStruct((n_col, n_row, 8, 128), F32),
+            jax.ShapeDtypeStruct((n_col, 8, C), F32),
+        ),
+        in_specs=[vm] * 7,
+        out_specs=(vm,) * 3,
+        scratch_shapes=[
+            pltpu.VMEM((n_col, 8, T), F32),
+            pltpu.VMEM((n_dp, 8, 128), F32),
+            pltpu.VMEM((n_dp, 8, C), F32),
+            pltpu.VMEM((n_row, 8, 128), F32),
+            pltpu.VMEM((n_row, 8, C), F32),
+            dma((n_col,)),
+            dma((n_col,)),
+            dma((n_dp, 2)),
+            dma((n_dp, 2)),
+            dma((n_row, 2)),
+            dma((n_row, 2)),
+            dma((n_col, 2)),
+            dma((n_col, 2)),
+        ],
+        compiler_params=pltpu.CompilerParams(
+            collective_id=2, has_side_effects=True, vmem_limit_bytes=48 * 1024 * 1024
+        ),
+    )(gn, x, g, mean, rstd, gain, part)
+
+
+def reduce_plain(p, q, dwi, dwf, C, HF, UT, n_col, row_width):
+    def block(part):
+        part = lax.psum_scatter(part, "row", scatter_dimension=0, tiled=True)
+        return lax.psum_scatter(part, "col", scatter_dimension=1, tiled=True).astype(F32)
+
+    wi4 = lax.all_to_all(dwi.reshape(n_col, C, -1), "col", 0, 0)
+    wf4 = lax.all_to_all(dwf.reshape(-1, n_col, C).transpose(1, 0, 2), "col", 0, 0)
+    grad_qkv = (
+        wi4[:, :, : 3 * HF].reshape(n_col, C, 3, HF).transpose(1, 2, 0, 3).reshape(C, 3, row_width)
+    )
+    grad_up_w = wi4[:, :, 3 * HF :].reshape(n_col, C, 2, UT).transpose(1, 2, 0, 3).reshape(C, -1)
+    grad_w_out = wf4[:, :HF].reshape(-1, C)
+    grad_w_down = wf4[:, HF:].reshape(n_col, 2, UT, C).transpose(1, 0, 2, 3).reshape(-1, C)
+    grad_tiles = tile_blocks(grad_qkv, grad_w_out, grad_up_w, grad_w_down)
+    owned = lax.psum_scatter(grad_tiles, "dp", scatter_dimension=0, tiled=True)
+    return block(p), block(q), owned
+
+
 def body(
     inputs,
     cotangent,
@@ -459,12 +969,8 @@
     hidden = jnp.concatenate([attn_low, act_low], axis=1)
 
     partial_out = jnp.dot(hidden, w_fin, preferred_element_type=F32).astype(BF16)
-    branch = lax.psum_scatter(partial_out, "row", scatter_dimension=0, tiled=True)
-    branch = lax.psum_scatter(branch, "col", scatter_dimension=1, tiled=True).astype(F32)
     x_val = inputs.astype(F32)
-    result = x_val + branch + out_bias
-
-    cot_val = cotangent.astype(F32)
+
     grad_w_fin = jnp.einsum("ti,tj->ij", hidden, cot_rows, preferred_element_type=F32).astype(BF16)
     back = jnp.einsum("tj,ij->ti", cot_rows, w_fin, preferred_element_type=F32)
     grad_attn_low = back[:, :HF].astype(BF16)
@@ -494,54 +1000,44 @@
     partial_norm = jnp.einsum(
         "tj,ij->ti", grad_mixed_low, w_in, preferred_element_type=F32
     ).astype(BF16)
-    grad_norm = lax.psum_scatter(partial_norm, "row", scatter_dimension=0, tiled=True)
-    grad_norm = lax.psum_scatter(grad_norm, "col", scatter_dimension=1, tiled=True).astype(F32)
-
-    mean_x = lax.dynamic_slice_in_dim(mean_all, row_index * T, T)
-    inv_std = lax.dynamic_slice_in_dim(rstd_all, row_index * T, T)
-    x_hat = (x_val - mean_x) * inv_std
-    grad_hat = grad_norm * norm_gain
-    back_stats = lax.psum((jnp.sum(grad_hat, axis=1), jnp.sum(grad_hat * x_hat, axis=1)), "col")
-    grad_x = inv_std * (
-        grad_hat - (back_stats[0] / D)[:, None] - x_hat * (back_stats[1] / D)[:, None]
-    )
-    grad_input = cot_val + grad_x
+
+    if n_dp == 2:
+        branch, grad_norm, owned_low = reduce_all(
+            partial_out, partial_norm, grad_w_in, grad_w_fin, T, C, HF, UT, n_row, n_col
+        )
+    else:
+        branch, grad_norm, owned_low = reduce_plain(
+            partial_out, partial_norm, grad_w_in, grad_w_fin, C, HF, UT, n_col, row_width
+        )
+    result = x_val + branch + out_bias
+    owned_grads = owned_low.astype(F32)
 
     sums = jnp.sum(grad_mixed, axis=0)
-    qkv_sums = sums[: 3 * HF].reshape(3, HF)
-    out_sums = jnp.sum(cot_val, axis=0)
-    norm_sums = jnp.stack(
-        [out_sums, out_sums, jnp.sum(grad_norm * x_hat, axis=0), jnp.sum(grad_norm, axis=0)]
-    )
-    qkv_rows = lax.dynamic_update_slice_in_dim(
-        jnp.zeros((3, D), F32), qkv_sums, feat_start, axis=1
-    )
-    norm_rows = lax.dynamic_update_slice_in_dim(
-        jnp.zeros((4, D), F32), norm_sums, col_start, axis=1
-    )
-    up_rows = jnp.zeros((up_flat.shape[0],), F32)
-    up_rows = lax.dynamic_update_slice_in_dim(up_rows, sums[3 * HF : 3 * HF + UT], unit_a, axis=0)
-    up_rows = lax.dynamic_update_slice_in_dim(up_rows, sums[3 * HF + UT :], unit_b, axis=0)
-    local_vec = jnp.concatenate([qkv_rows, norm_rows, up_rows.reshape(-1, D)], axis=0)
-    vec_grad = lax.psum(local_vec, ("dp", "row", "col"))
+    part = jnp.pad(sums.reshape(-1, 128), ((0, 1), (0, 0)))
+    grad_input, vec_a, vec_b = finish_all(
+        grad_norm,
+        inputs,
+        cotangent,
+        lax.dynamic_slice_in_dim(mean_all, row_index * T, T),
+        lax.dynamic_slice_in_dim(rstd_all, row_index * T, T),
+        norm_gain[None],
+        part,
+        D,
+        n_dp,
+        n_row,
+        n_col,
+    )
+    vec_a = vec_a.transpose(2, 1, 0, 3)
+    qkv_rows = vec_a[:3].reshape(3, D)
+    up_rows = vec_a[3:7].reshape(2, UT // 128, n_row, n_col, 128).transpose(2, 0, 3, 1, 4)
+    norm_rows = vec_b.transpose(1, 0, 2).reshape(8, D)
+    vec_grad = jnp.concatenate(
+        [qkv_rows, norm_rows[2:3], norm_rows[2:3], norm_rows[:2], up_rows.reshape(-1, D)], axis=0
+    )
     scaled = vec_grad * lax.rsqrt(jnp.mean(vec_grad * vec_grad, axis=1, keepdims=True) + STAT_EPS)
     vec_moment_new = MOMENTUM_RATE * vector_moment + scaled
     vectors_new = vectors - VECTOR_RATE * vec_moment_new
 
-    wi4 = lax.all_to_all(grad_w_in.reshape(n_col, C, -1), "col", 0, 0)
-    wf4 = lax.all_to_all(
-        grad_w_fin.reshape(-1, n_col, C).transpose(1, 0, 2), "col", 0, 0
-    )
-    grad_qkv = (
-        wi4[:, :, : 3 * HF].reshape(n_col, C, 3, HF).transpose(1, 2, 0, 3).reshape(C, 3, row_width)
-    )
-    grad_up_w = (
-        wi4[:, :, 3 * HF :].reshape(n_col, C, 2, UT).transpose(1, 2, 0, 3).reshape(C, -1)
-    )
-    grad_w_out = wf4[:, :HF].reshape(-1, C)
-    grad_w_down = wf4[:, HF:].reshape(n_col, 2, UT, C).transpose(1, 0, 2, 3).reshape(-1, C)
-    grad_tiles = tile_blocks(grad_qkv, grad_w_out, grad_up_w, grad_w_down)
-    owned_grads = lax.psum_scatter(grad_tiles, "dp", scatter_dimension=0, tiled=True).astype(F32)
     owned_count = owned_grads.shape[0]
     weight_tiles = lax.dynamic_slice_in_dim(
         tile_blocks(w_qkv, w_out, w_up, w_down), d_index * owned_count, owned_count, 0

time: 770 us -> 517 us (0.67)
  waiting for transfers between devices: 322 us -> 0 us
  Pallas kernels: 169 us -> 318 us
  local copies, waits for them, and re-layouts: 94.6 us -> 47.2 us
  between operations: 15.2 us -> 2.02 us
  blocking collectives: 10.3 us -> 0 us
  starting transfers between devices: 8.71 us -> 0 us
  matrix products: 86.6 us -> 94.9 us
    pallas_call x0 -> x2, Pallas kernels: none -> 149 us  [the longest x1 136 us: reduce_all(): pl.pallas_call(functools.partial(reduce_kernel, n_row, n_col, (T, C, HF,...]
    psum x1 -> x0, waiting for transfers between devices: 122 us -> none  [body(): vec_grad = lax.psum(local_vec, ('dp', 'row', 'col'))]
    all_to_all x2 -> x0, waiting for transfers between devices: 109 us -> none  [the longest x1 72.2 us: body(): wi4 = lax.all_to_all(grad_w_in.reshape(n_col, C, -1), 'col', 0, 0)]
    reduce_scatter x5 -> x0, waiting for transfers between devices: 90 us -> none  [the longest x1 42.1 us: body(): lax.psum_scatter(grad_tiles, 'dp', scatter_dimension=0, tiled=True)]
    unnamed x91 -> x96, local copies, waits for them, and re-layouts: 36.4 us -> 22.1 us
    reshape x3 -> x1, local copies, waits for them, and re-layouts: 10.4 us -> 0.03 us  [body(): qkv_rows = vec_a[:3].reshape(3, D)]
    psum x1 -> x0, blocking collectives: 10.3 us -> none  [body(): lax.psum((jnp.sum(grad_hat, axis=1), jnp.sum(grad_hat * x_hat, axis=1)),...]
    all_to_all x2 -> x0, starting transfers between devices: 8.47 us -> none  [the longest x1 4.82 us: body(): wi4 = lax.all_to_all(grad_w_in.reshape(n_col, C, -1), 'col', 0, 0)]
  transfers between devices with their start and end apart: 8 -> 0, of which waited for: 6 -> 0; matrix products, arithmetic and copies ran while one was open for 18% -> 0% of each run, Pallas kernels for 0% -> 0%
where the time goes in v2:
time: 517 us; the launch traced here: 513 us
  Pallas kernels  318 us (62%)
  matrix products  94.9 us (18%)
  other arithmetic  50.6 us (10%)
  local copies, waits for them, and re-layouts  47.2 us (9%)
    pallas_call x1, Pallas kernels, gather_all(): pl.pallas_call(functools.partial(gather_kernel, n_dp, n_row, n_col, (T, C...  169 us
    pallas_call x1, Pallas kernels, reduce_all(): pl.pallas_call(functools.partial(reduce_kernel, n_row, n_col, (T, C, HF,...  136 us
    unnamed x96, local copies, waits for them, and re-layouts  22.1 us
    dot_general x1, matrix products, body(): jnp.einsum('tj,ij->ti', grad_mixed_low, w_in, preferred_element_type=F32)  13.6 us
    pallas_call x1, Pallas kernels, finish_all(): pl.pallas_call(functools.partial(finish_kernel, n_dp, n_row, n_col, width...  12.8 us
    dot_general x1, matrix products, body(): jnp.einsum('ti,tj->ij', normed, grad_mixed_low, preferred_element_type=F32)  12.2 us
    dot_general x1, matrix products, body(): back = jnp.einsum('tj,ij->ti', cot_rows, w_fin, preferred_element_type=F32)  11.4 us
    dot_general x1, matrix products, body(): jnp.einsum('ti,tj->ij', hidden, cot_rows, preferred_element_type=F32)  10.4 us

profile of v2, /device:TPU:0, one launch (start us, length us, event | category | flops | bytes accessed | tf_op | source)
XLA Modules:
  0.0 513.2 jit_solution(114991146274937270)
XLA Ops:
  0.6 1.7 copy.75
  2.5 1.6 copy.77.wq_ref
  4.1 169.4 %gather_all.1 = (bf16[2048,2048]{1,0:T(8,128)(2,1)}, bf16[2048,2048]{1,0:T(8,128)(2,1)}, bf16[2048,896]{1,0:T(8,128)(2,1)}, bf16[640,2048]{1,0:T(8,128)(2,1)}) custom-call(bf16[512,512]{1,0:T(8,128)(2,1)} %x_ref.3, bf16[512,512]{1,0:T(8,128)(2,1)} %g_ref.3, bf16[4,512,384]{2,1,0:T(8,128)(2,1)} %copy.77.wq_ref, bf16[512,2048]{1,0:T(8,128)(2,1)} %wu_ref.1, ...), custom_call_target="tpu_custom_call" | custom-call | tf_op jit(solution)/shard_map/gather_all/pallas_call | solution.py:353
  173.6 11.4 %fusion.31 = f32[2048,640]{0,1:T(8,128)} fusion(bf16[2048,2048]{1,0:T(8,128)(2,1)} %get-tuple-element.21, bf16[640,2048]{1,0:T(8,128)(2,1)} %get-tuple-element.20), kind=kOutput, calls=%fused_computation.119 | convolution fusion | flops 5368709120 | bytes 16252928 | tf_op jit(solution)/shard_map/tj,ij->ti/dot_general | solution.py:975
  185.1 2.4 convert_reduce_fusion
  187.5 3.7 fusion.3
  191.2 10.2 %fusion.30 = f32[2048,896]{0,1:T(8,128)} fusion(bf16[2048,2048]{1,0:T(8,128)(2,1)S(1)} %fusion.3, bf16[2048,896]{1,0:T(8,128)(2,1)S(1)} %copy-done.29), kind=kOutput, calls=%fused_computation.118 | convolution fusion | flops 7516192768 | bytes 19398656 | tf_op jit(solution)/shard_map/dot_general | solution.py:947
  201.5 7.3 %fusion.15 = (f32[2048,512]{0,1:T(8,128)}, bf16[2048,512]{0,1:T(8,128)(2,1)}) fusion(f32[2048,640]{0,1:T(8,128)} %fusion.31, f32[2048,896]{0,1:T(8,128)} %fusion.30, f32[512]{0:T(512)S(1)} %pad_maximum_fusion.6), kind=kLoop, calls=%fused_computation.38 | loop fusion | flops 22020096 | bytes 14682112 | tf_op jit(solution)/shard_map/mul | solution.py:977
  208.8 1.3 slice.200
  210.1 1.2 reshape_reshape.4
  211.4 1.7 compare_and_fusion
  215.2 1.9 fusion.7
  217.1 2.0 fusion.5
  219.2 1.2 copy-done.3
  220.4 5.1 fusion.6
  226.0 3.2 multiply_reduce_fusion.1
  229.8 9.4 %convolution_convert_fusion.1.p_ref = bf16[2048,2048]{1,0:T(8,128)(2,1)} fusion(bf16[640,2048]{1,0:T(8,128)(2,1)S(1)} %copy-done.30, bf16[2048,512]{0,1:T(8,128)(2,1)S(1)} %copy-done.15, bf16[2048,128]{0,1:T(8,128)(2,1)S(1)} %bitcast.197), kind=kOutput, calls=%fused_computation.16 | convolution fusion | flops 5378146304 | bytes 13631488 | tf_op jit(solution)/shard_map/dot_general | solution.py:971
  239.2 1.4 convolution_bitcast_fusion
  241.7 3.4 multiply_convert_fusion
  245.1 1.4 convolution_bitcast_fusion.1
  250.5 13.6 %convolution_convert_fusion.q_ref = bf16[2048,2048]{1,0:T(8,128)(2,1)} fusion(bf16[2048,896]{1,0:T(8,128)(2,1)} %get-tuple-element.19, f32[2048,512]{0,1:T(8,128)S(1)} %copy-done.6, f32[2048,128]{0,1:T(8,128)S(1)} %bitcast.168, f32[2048,128]{0,1:T(8,128)} %bitcast.171, f32[2048,128]{0,1:T(8,128)} %bitcast.174), kind=kOutput, calls=%fused_computation.15 | convolution fusion | flops 7535067136 | bytes 19398656 | tf_op jit(solution)/shard_map/tj,ij->ti/dot_general | solution.py:1000
  264.2 12.2 %convolution_convert_fusion.2.dwi_ref = bf16[2048,896]{1,0:T(8,128)(2,1)} fusion(bf16[2048,2048]{1,0:T(8,128)(2,1)S(1)} %bitcast.164, f32[2048,512]{0,1:T(8,128)S(1)} %copy-done.6, f32[2048,128]{0,1:T(8,128)S(1)} %bitcast.169, f32[2048,128]{0,1:T(8,128)} %bitcast.172, f32[2048,128]{0,1:T(8,128)} %bitcast.175), kind=kOutput, calls=%fused_computation.42 | convolution fusion | flops 7532707840 | bytes 19398656 | tf_op jit(solution)/shard_map/ti,tj->ij/dot_general | solution.py:997
  276.4 10.4 %convolution_convert_fusion.3.dwf_ref = bf16[640,2048]{1,0:T(8,128)(2,1)} fusion(bf16[2048,2048]{1,0:T(8,128)(2,1)} %get-tuple-element.21, bf16[2048,512]{0,1:T(8,128)(2,1)S(1)} %copy-done.16, bf16[2048,128]{0,1:T(8,128)(2,1)S(1)} %bitcast.198), kind=kOutput, calls=%fused_computation.43 | convolution fusion | flops 5375262720 | bytes 13631488 | tf_op jit(solution)/shard_map/ti,tj->ij/dot_general | solution.py:974
  286.8 136.3 %reduce_all.1 = (f32[512,512]{1,0:T(8,128)}, f32[512,512]{1,0:T(8,128)}, bf16[12,512,256]{2,1,0:T(8,128)(2,1)}) custom-call(bf16[2048,2048]{1,0:T(8,128)(2,1)} %convolution_convert_fusion.1.p_ref, bf16[2048,2048]{1,0:T(8,128)(2,1)} %convolution_convert_fusion.q_ref, bf16[2048,896]{1,0:T(8,128)(2,1)} %convolution_convert_fusion.2.dwi_ref, ...), custom_call_target="tpu_custom_call" | custom-call | tf_op jit(solution)/shard_map/reduce_all/pallas_call | solution.py:684
  423.1 2.4 add_add_fusion
  426.0 3.7 fusion.8
  429.7 1.2 copy-done.2
  430.9 12.8 %finish_all.1 = (f32[512,512]{1,0:T(8,128)S(1)}, f32[4,4,8,128]{3,2,1,0:T(8,128)S(1)}, f32[4,8,512]{2,1,0:T(8,128)S(1)}) custom-call(f32[512,512]{1,0:T(8,128)S(1)} %copy-done.2, bf16[512,512]{1,0:T(8,128)(2,1)S(1)} %copy-done, bf16[512,512]{1,0:T(8,128)(2,1)S(1)} %copy-done.1, f32[512,1]{1,0:T(8,128)S(1)} %copy.98.mean_ref, f32[512,1]{1,0:T(8,128)S(1)} %copy.99.rstd_ref, ...), custom_call_target="tpu_custom_call" | custom-call | tf_op jit(solution)/shard_map/finish_all/pallas_call | solution.py:846
  443.7 3.5 convert_bitcast_fusion
  447.2 4.1 multiply_reduce_fusion
  451.3 4.0 fusion.16
  462.5 1.3 add_convert_fusion.2
  468.3 2.7 add_convert_fusion
  473.0 2.1 bitcast_dynamic-update-slice_fusion.4
  475.1 2.0 copy.103
  477.1 1.9 bitcast_dynamic-update-slice_fusion.3
  479.0 2.0 copy.105
  481.0 1.9 bitcast_dynamic-update-slice_fusion.2
  482.9 2.0 copy.106
  484.9 2.0 copy.107
  487.0 1.9 bitcast_dynamic-update-slice_fusion.1
  488.9 2.5 copy.108
  491.3 4.1 copy.109
  495.4 3.1 bitcast_dynamic-update-slice_fusion
  498.5 2.0 reshape.269
  500.5 1.9 copy.110
  502.4 1.5 constant_dynamic-update-slice_fusion
  503.9 6.5 %subtract_bitcast_fusion = f32[1,1,12,512,256]{4,3,2,1,0:T(8,128)} fusion(bf16[12,512,256]{2,1,0:T(8,128)(2,1)} %add_convert_fusion, bf16[24,512,256]{2,1,0:T(8,128)(2,1)} %constant_dynamic-update-slice_fusion, s32[]{:T(128)S(6)} %select_n.31), kind=kLoop, calls=%fused_computation.20 | loop fusion | flops 6291456 | bytes 12582916 | tf_op jit(solution)/shard_map/broadcast_in_dim | solution.py:1053
  (157 shorter events, 24.8 us)
Async XLA Ops:
  2.4 171.2 %copy-start.7 = (bf16[512,3,512]{0,2,1:T(8,128)(2,1)}, bf16[512,3,512]{0,2,1:T(8,128)(2,1)S(1)}, u32[]{:S(2)}) copy-start(bf16[512,3,512]{0,2,1:T(8,128)(2,1)S(1)} %copy.75) | copy-start | bytes 4718596
  173.5 11.5 %slice-start.2 = ((s8[8388608]{0:T(1024)(128)(4,1)}), s8[4194304]{0:T(1024)(128)(4,1)S(1)}, s32[]{:S(2)}) async-start(s8[8388608]{0:T(1024)(128)(4,1)} %bitcast.157), calls=%async_computation.2 | async-start | bytes 8388608
  173.5 11.5 %copy-start.24 = (f32[11,2048]{1,0:T(8,128)S(1)}, f32[11,2048]{1,0:T(8,128)}, u32[]{:S(2)}) copy-start(f32[11,2048]{1,0:T(8,128)} %param.19) | copy-start | bytes 270340
  173.6 11.5 %slice-start.3 = ((s8[8388608]{0:T(1024)(128)(4,1)}), s8[4194304]{0:T(1024)(128)(4,1)S(1)}, s32[]{:S(2)}) async-start(s8[8388608]{0:T(1024)(128)(4,1)} %bitcast.157), calls=%async_computation.3 | async-start | bytes 8388608
  187.5 3.7 copy-start.29
  191.2 10.3 %copy-start.12 = (bf16[2048,2048]{1,0:T(8,128)(2,1)}, bf16[2048,2048]{1,0:T(8,128)(2,1)S(1)}, u32[]{:S(2)}) copy-start(bf16[2048,2048]{1,0:T(8,128)(2,1)S(1)} %fusion.3) | copy-start | bytes 25165828
  201.5 9.7 %copy-start.27 = (s32[2048]{0:T(1024)S(1)}, s32[2048]{0:T(1024)}, u32[]{:S(2)}) copy-start(s32[2048]{0:T(1024)} %param.13) | copy-start | bytes 24580
  211.3 1.8 slice-start.9
  211.3 2.3 slice-start.6
  213.6 0.7 copy-start.28
  213.8 1.3 copy-start.9
  215.2 1.9 copy-start.18
  215.2 1.9 copy-start.20
  217.1 3.3 copy-start.3
  220.4 5.6 %copy-start.13 = (bf16[4,512,2,64]{1,0,3,2:T(4,128)(2,1)S(1)}, bf16[4,512,2,64]{1,0,3,2:T(4,128)(2,1)}, u32[]{:S(2)}) copy-start(bf16[4,512,2,64]{1,0,3,2:T(4,128)(2,1)} %reshape_reshape.4) | copy-start | bytes 1572868
  226.0 3.8 copy-start.15
  226.0 3.8 copy-start.30
  229.6 12.0 %slice-start = ((s8[8388608]{0:T(1024)(128)(4,1)}), s8[4194304]{0:T(1024)(128)(4,1)S(1)}, s32[]{:S(2)}) async-start(s8[8388608]{0:T(1024)(128)(4,1)} %bitcast.155), calls=%async_computation | async-start | bytes 8388608
  229.7 9.4 %copy-start.22 = (bf16[16,8,4,512]{3,1,2,0:T(8,128)(2,1)}, bf16[16,8,4,512]{3,1,2,0:T(8,128)(2,1)S(1)}, u32[]{:S(2)}) copy-start(bf16[16,8,4,512]{3,1,2,0:T(8,128)(2,1)S(1)} %copy.136) | copy-start | bytes 1572868
  229.8 9.4 %copy-start.5 = (bf16[4,2,512,512]{2,3,1,0:T(8,128)(2,1)S(1)}, bf16[4,2,512,512]{2,3,1,0:T(8,128)(2,1)}, u32[]{:S(2)}) copy-start(bf16[4,2,512,512]{2,3,1,0:T(8,128)(2,1)} %get-tuple-element.34) | copy-start | bytes 12582916
  229.8 11.8 %slice-start.1 = ((s8[8388608]{0:T(1024)(128)(4,1)}), s8[4194304]{0:T(1024)(128)(4,1)S(1)}, s32[]{:S(2)}) async-start(s8[8388608]{0:T(1024)(128)(4,1)} %bitcast.155), calls=%async_computation.1 | async-start | bytes 8388608
  241.6 22.5 %copy-start.14 = (f32[16,8,4,512]{3,1,2,0:T(8,128)}, f32[16,8,4,512]{3,1,2,0:T(8,128)S(1)}, u32[]{:S(2)}) copy-start(f32[16,8,4,512]{3,1,2,0:T(8,128)S(1)} %copy.138) | copy-start | bytes 3145732
  241.6 3.4 copy-start.19
  245.1 1.5 copy-start.21
  247.6 2.9 copy-start.6
  248.7 15.4 %slice-start.7 = ((s8[8388608]{0:T(1024)(128)(4,1)}), s8[4194304]{0:T(1024)(128)(4,1)S(1)}, s32[]{:S(2)}) async-start(s8[8388608]{0:T(1024)(128)(4,1)} %bitcast.163), calls=%async_computation.7 | async-start | bytes 8388608
  250.5 13.6 %slice-start.8 = ((s8[8388608]{0:T(1024)(128)(4,1)}), s8[4194304]{0:T(1024)(128)(4,1)S(1)}, s32[]{:S(2)}) async-start(s8[8388608]{0:T(1024)(128)(4,1)} %bitcast.163), calls=%async_computation.8 | async-start | bytes 8388608
  264.2 12.2 %copy-start.16 = (bf16[2048,512]{0,1:T(8,128)(2,1)S(1)}, bf16[2048,512]{0,1:T(8,128)(2,1)}, u32[]{:S(2)}) copy-start(bf16[2048,512]{0,1:T(8,128)(2,1)} %get-tuple-element.37) | copy-start | bytes 6291460
  264.2 12.2 %copy-start.23 = (bf16[16,8,4,512]{3,1,2,0:T(8,128)(2,1)S(1)}, bf16[16,8,4,512]{3,1,2,0:T(8,128)(2,1)}, u32[]{:S(2)}) copy-start(bf16[16,8,4,512]{3,1,2,0:T(8,128)(2,1)} %copy-done.22) | copy-start | bytes 1572868
  286.8 136.3 %copy-start = (bf16[512,512]{1,0:T(8,128)(2,1)S(1)}, bf16[512,512]{1,0:T(8,128)(2,1)}, u32[]{:S(2)}) copy-start(bf16[512,512]{1,0:T(8,128)(2,1)} %x_ref.3) | copy-start | bytes 1572868
  425.5 4.2 copy-start.1
  426.0 17.7 %copy-start.4 = (bf16[12,512,256]{2,1,0:T(8,128)(2,1)S(1)}, bf16[12,512,256]{2,1,0:T(8,128)(2,1)}, u32[]{:S(2)}) copy-start(bf16[12,512,256]{2,1,0:T(8,128)(2,1)} %get-tuple-element.25) | copy-start | bytes 9437188
  429.7 1.2 copy-start.2
  443.7 7.6 %slice-start.4 = ((s8[6291456]{0:T(1024)(128)(4,1)}), s8[4194304]{0:T(1024)(128)(4,1)S(1)}, s32[]{:S(2)}) async-start(s8[6291456]{0:T(1024)(128)(4,1)} %bitcast.159), calls=%async_computation.4 | async-start | bytes 8388608
  447.2 4.1 slice-start.5
  468.2 2.7 copy-start.8
  473.0 15.9 %copy-start.10 = (bf16[512,2048]{1,0:T(8,128)(2,1)S(1)}, bf16[512,2048]{1,0:T(8,128)(2,1)}, u32[]{:S(2)}) copy-start(bf16[512,2048]{1,0:T(8,128)(2,1)} %wu_ref.1) | copy-start | bytes 6291460
  491.3 7.2 %copy-start.11 = (bf16[2048,512]{1,0:T(8,128)(2,1)S(1)}, bf16[2048,512]{1,0:T(8,128)(2,1)}, u32[]{:S(2)}) copy-start(bf16[2048,512]{1,0:T(8,128)(2,1)} %wd_ref.1) | copy-start | bytes 6291460
  503.9 7.1 %copy-start.25 = (f32[11,2048]{1,0:T(8,128)S(1)}, f32[11,2048]{1,0:T(8,128)}, u32[]{:S(2)}) copy-start(f32[11,2048]{1,0:T(8,128)} %param.19) | copy-start | bytes 270340
  503.9 7.1 %copy-start.26 = (f32[11,2048]{1,0:T(8,128)S(1)}, f32[11,2048]{1,0:T(8,128)}, u32[]{:S(2)}) copy-start(f32[11,2048]{1,0:T(8,128)} %param.21) | copy-start | bytes 270340
  510.8 1.9 copy-start.17

commit v3 on v2

--- a/solution.py
+++ b/solution.py
@@ -101,18 +101,6 @@
     grad_queries = jnp.einsum("hlm,mhe->lhe", grad_scores, key_vecs, preferred_element_type=F32)
     grad_keys = jnp.einsum("hlm,lhe->mhe", grad_scores, queries, preferred_element_type=F32)
     return (grad_queries, grad_keys, grad_values)
-
-
-def newton_schulz(moment):
-    iterate = to_low(moment * lax.rsqrt(jnp.sum(moment * moment) + STAT_EPS))
-    for newton_step in range(5):
-        gram = to_low(jnp.dot(iterate.T, iterate, preferred_element_type=F32))
-        square = jnp.dot(gram, gram, preferred_element_type=F32)
-        poly = to_low(NEWTON_B * gram.astype(F32) + NEWTON_C * square)
-        iterate = to_low(
-            NEWTON_A * iterate.astype(F32) + jnp.dot(iterate, poly, preferred_element_type=F32)
-        )
-    return iterate
 
 
 def tile_blocks(qkv_block, out_block, up_block, down_block):
@@ -874,6 +862,104 @@
     )(gn, x, g, mean, rstd, gain, part)
 
 
+def muon_kernel(owned, per_step, HF, UT, rate, grad_ref, mom_ref, wq_ref, wo_ref, wu_ref, wd_ref,
+                og_ref, new_ref, nm_ref, wbuf, sem):
+    first = lax.axis_index("dp") * owned
+    step = pl.program_id(0)
+    steps = owned // per_step
+    n_qkv, n_out, n_up = 6, 2, 8
+
+    def fetch(tile, slot, n, start):
+        dst = wbuf.at[slot, n]
+
+        def go(src, target, s):
+            item = pltpu.make_async_copy(src, target, s)
+            if start:
+                item.start()
+            else:
+                item.wait()
+
+        @pl.when(tile < n_qkv)
+        def _():
+            j, half = lax.div(tile, 2), lax.rem(tile, 2)
+            for m in range(UT // HF):
+                go(wq_ref.at[half * (UT // HF) + m, :, pl.ds(j * HF, HF)],
+                   wbuf.at[slot, n, :, pl.ds(m * HF, HF)], sem.at[slot, n, m])
+
+        @pl.when((tile >= n_qkv) & (tile < n_qkv + n_out))
+        def _():
+            go(wo_ref.at[:, pl.ds((tile - n_qkv) * UT, UT)], dst, sem.at[slot, n, 0])
+
+        @pl.when((tile >= n_qkv + n_out) & (tile < n_qkv + n_out + n_up))
+        def _():
+            go(wu_ref.at[:, pl.ds((tile - n_qkv - n_out) * UT, UT)], dst, sem.at[slot, n, 0])
+
+        @pl.when(tile >= n_qkv + n_out + n_up)
+        def _():
+            left = tile - (n_qkv + n_out + n_up)
+            rows = dst.shape[0]
+            go(wd_ref.at[pl.ds(lax.div(left, 2) * rows, rows), pl.ds(lax.rem(left, 2) * UT, UT)],
+               dst, sem.at[slot, n, 0])
+
+    def fetch_all(at, start):
+        for n in range(per_step):
+            fetch(first + at * per_step + n, lax.rem(at, 2), n, start)
+
+    @pl.when(step == 0)
+    def _():
+        fetch_all(step, True)
+
+    @pl.when(step + 1 < steps)
+    def _():
+        fetch_all(step + 1, True)
+
+    iters = []
+    for n in range(per_step):
+        grad = grad_ref[n].astype(F32)
+        og_ref[n] = grad
+        moment = MOMENTUM_RATE * mom_ref[n] + grad
+        nm_ref[n] = moment
+        scale = lax.rsqrt(jnp.sum(moment * moment, keepdims=True) + STAT_EPS)
+        iters.append((moment * scale).astype(BF16))
+    contract = (((0,), (0,)), ((), ()))
+    for _ in range(5):
+        grams = [
+            lax.dot_general(x, x, contract, preferred_element_type=F32).astype(BF16) for x in iters
+        ]
+        squares = [jnp.dot(g, g, preferred_element_type=F32) for g in grams]
+        polys = [
+            (NEWTON_B * g.astype(F32) + NEWTON_C * s).astype(BF16) for g, s in zip(grams, squares)
+        ]
+        iters = [
+            (NEWTON_A * x.astype(F32) + jnp.dot(x, p, preferred_element_type=F32)).astype(BF16)
+            for x, p in zip(iters, polys)
+        ]
+    fetch_all(step, False)
+    for n in range(per_step):
+        new_ref[n] = wbuf[lax.rem(step, 2), n].astype(F32) - rate * iters[n].astype(F32)
+
+
+def muon_all(grads, moment, w_q, w_out, w_up, w_down, HF, UT):
+    owned, rows, cols = moment.shape
+    per_step = 3
+    rate = MUON_RATE * math.sqrt(max(1.0, rows / cols))
+    block = pl.BlockSpec((per_step, rows, cols), lambda i: (i, 0, 0))
+    out = jax.ShapeDtypeStruct(moment.shape, F32)
+    return pl.pallas_call(
+        functools.partial(muon_kernel, owned, per_step, HF, UT, rate),
+        name="muon_all",
+        grid=(owned // per_step,),
+        out_shape=(out, out, out),
+        in_specs=[block, block, ANY, ANY, ANY, ANY],
+        out_specs=(block, block, block),
+        scratch_shapes=[
+            pltpu.VMEM((2, per_step, rows, cols), BF16),
+            pltpu.SemaphoreType.DMA((2, per_step, 2)),
+        ],
+        compiler_params=pltpu.CompilerParams(vmem_limit_bytes=56 * 1024 * 1024),
+    )(grads, moment, w_q, w_out, w_up, w_down)
+
+
 def reduce_plain(p, q, dwi, dwf, C, HF, UT, n_col, row_width):
     def block(part):
         part = lax.psum_scatter(part, "row", scatter_dimension=0, tiled=True)
@@ -1010,7 +1096,6 @@
             partial_out, partial_norm, grad_w_in, grad_w_fin, C, HF, UT, n_col, row_width
         )
     result = x_val + branch + out_bias
-    owned_grads = owned_low.astype(F32)
 
     sums = jnp.sum(grad_mixed, axis=0)
     part = jnp.pad(sums.reshape(-1, 128), ((0, 1), (0, 0)))
@@ -1038,14 +1123,9 @@
     vec_moment_new = MOMENTUM_RATE * vector_moment + scaled
     vectors_new = vectors - VECTOR_RATE * vec_moment_new
 
-    owned_count = owned_grads.shape[0]
-    weight_tiles = lax.dynamic_slice_in_dim(
-        tile_blocks(w_qkv, w_out, w_up, w_down), d_index * owned_count, owned_count, 0
-    ).astype(F32)
-    moment_new = MOMENTUM_RATE * tile_moment[0, 0] + owned_grads
-    ortho_tiles = jax.vmap(newton_schulz)(moment_new)
-    tile_ratio = math.sqrt(max(1.0, moment_new.shape[1] / moment_new.shape[2]))
-    tiles_new = weight_tiles - MUON_RATE * tile_ratio * ortho_tiles.astype(F32)
+    owned_grads, tiles_new, moment_new = muon_all(
+        owned_low, tile_moment[0, 0], w_q, w_out, w_up, w_down, HF, UT
+    )
     return (
         result,
         grad_input,

time: 517 us -> 477 us (0.923)
  local copies, waits for them, and re-layouts: 47.2 us -> 25.1 us
  Pallas kernels: 318 us -> 340 us
  matrix products: 94.9 us -> 74.3 us
  other arithmetic: 50.6 us -> 30 us
    pallas_call x0 -> x1, Pallas kernels: none -> 21.9 us  [muon_all(): pl.pallas_call(functools.partial(muon_kernel, owned, per_step, HF, UT, ra...]
    dot_general x15 -> x0, matrix products: 15.5 us -> none  [the longest x5 6.91 us: newton_schulz(): jnp.dot(iterate, poly, preferred_element_type=F32)]
    broadcast_in_dim x3 -> x0, other arithmetic: 14 us -> none  [the longest x1 6.53 us: body(): tiles_new[None, None]]
    unnamed x96 -> x41, local copies, waits for them, and re-layouts: 22.1 us -> 11.6 us
    reshape x4 -> x0, local copies, waits for them, and re-layouts: 9.98 us -> none  [the longest x2 6.11 us: split_cols(): block_in.reshape(block_in.shape[0], block_in.shape[1] // tile_cols, tile_...]
where the time goes in v3:
time: 477 us; the launch traced here: 471 us
  Pallas kernels  340 us (71%)
  matrix products  74.3 us (16%)
  other arithmetic  30 us (6%)
  local copies, waits for them, and re-layouts  25.1 us (5%)
    pallas_call x1, Pallas kernels, gather_all(): pl.pallas_call(functools.partial(gather_kernel, n_dp, n_row, n_col, (T, C...  169 us
    pallas_call x1, Pallas kernels, reduce_all(): pl.pallas_call(functools.partial(reduce_kernel, n_row, n_col, (T, C, HF,...  136 us
    pallas_call x1, Pallas kernels, muon_all(): pl.pallas_call(functools.partial(muon_kernel, owned, per_step, HF, UT, ra...  21.9 us
    dot_general x1, matrix products, body(): jnp.einsum('tj,ij->ti', grad_mixed_low, w_in, preferred_element_type=F32)  13.3 us
    pallas_call x1, Pallas kernels, finish_all(): pl.pallas_call(functools.partial(finish_kernel, n_dp, n_row, n_col, width...  12.8 us
    dot_general x1, matrix products, body(): mixed_out = jnp.dot(normed, w_in, preferred_element_type=F32)  12 us
    unnamed x41, local copies, waits for them, and re-layouts  11.6 us
    dot_general x1, matrix products, body(): jnp.einsum('ti,tj->ij', normed, grad_mixed_low, preferred_element_type=F32)  10.6 us

profile of v3, /device:TPU:0, one launch (start us, length us, event | category | flops | bytes accessed | tf_op | source)
XLA Modules:
  0.0 471.2 jit_solution(5903858170974262680)
XLA Ops:
  0.7 0.7 eq.12
  1.4 0.7 convert_element_type.73
  2.1 0.9 slice_bitcast_fusion
  3.1 0.8 slice.101
  3.9 1.0 fusion.26
  5.1 0.5 broadcast_multiply_fusion
  5.6 0.9 compare_and_fusion
  6.5 2.6 copy.54
  9.1 1.5 copy.55
  10.6 1.6 copy.56.wq_ref
  12.2 169.4 %gather_all.1 = (bf16[2048,2048]{1,0:T(8,128)(2,1)}, bf16[2048,2048]{1,0:T(8,128)(2,1)}, bf16[2048,896]{1,0:T(8,128)(2,1)}, bf16[640,2048]{1,0:T(8,128)(2,1)}) custom-call(bf16[512,512]{1,0:T(8,128)(2,1)} %x_ref.3, bf16[512,512]{1,0:T(8,128)(2,1)} %g_ref.3, bf16[4,512,384]{2,1,0:T(8,128)(2,1)} %copy.56.wq_ref, bf16[512,2048]{1,0:T(8,128)(2,1)} %wu_ref.3, ...), custom_call_target="tpu_custom_call" | custom-call | tf_op jit(solution)/shard_map/gather_all/pallas_call | solution.py:341
  181.7 5.9 %convert_reduce_fusion = (f32[2048]{0:T(1024)S(1)}, f32[2048]{0:T(1024)S(1)}) fusion(bf16[2048,2048]{1,0:T(8,128)(2,1)} %get-tuple-element.21), kind=kLoop, calls=%fused_computation.2 | loop fusion | flops 16773120 | bytes 8404992 | tf_op jit(solution)/shard_map/reduce_sum | solution.py:1028
  187.6 5.9 %fusion.3 = bf16[2048,2048]{1,0:T(8,128)(2,1)} fusion(bf16[2048,2048]{1,0:T(8,128)(2,1)S(1)} %copy-done.3, f32[2048]{0:T(1024)S(1)} %bitcast.140, f32[2048]{0:T(1024)S(1)} %bitcast.138, f32[2048]{0:T(1024)S(1)} %get-tuple-element.66, f32[2048]{0:T(1024)S(1)} %get-tuple-element.65), kind=kLoop, calls=%fused_computation.6 | loop fusion | flops 25165824 | bytes 16809984 | tf_op jit(solution)/shard_map/convert_element_type | solution.py:1031
  194.0 8.9 %fusion.29 = f32[2048,640]{0,1:T(8,128)S(1)} fusion(bf16[2048,2048]{1,0:T(8,128)(2,1)} %get-tuple-element.24, bf16[640,2048]{1,0:T(8,128)(2,1)} %get-tuple-element.23), kind=kOutput, calls=%fused_computation.90 | convolution fusion | flops 5368709120 | bytes 16252928 | tf_op jit(solution)/shard_map/tj,ij->ti/dot_general | solution.py:1061
  202.8 2.3 copy-done.5
  205.3 0.4 reshape_reshape.4
  205.7 12.0 %fusion.28 = f32[2048,896]{0,1:T(8,128)S(1)} fusion(bf16[2048,2048]{1,0:T(8,128)(2,1)} %fusion.3, bf16[2048,896]{1,0:T(8,128)(2,1)} %get-tuple-element.22), kind=kOutput, calls=%fused_computation.89 | convolution fusion | flops 7516192768 | bytes 19398656 | tf_op jit(solution)/shard_map/dot_general | solution.py:1033
  217.6 5.0 %fusion.15 = (f32[2048,512]{0,1:T(8,128)}, bf16[2048,512]{0,1:T(8,128)(2,1)}) fusion(f32[2048,640]{0,1:T(8,128)S(1)} %copy-done.6, f32[2048,896]{0,1:T(8,128)S(1)} %fusion.28, f32[512]{0:T(512)S(1)} %pad_maximum_fusion.6), kind=kLoop, calls=%fused_computation.28 | loop fusion | flops 22020096 | bytes 14682112 | tf_op jit(solution)/shard_map/mul | solution.py:1063
  223.4 1.5 fusion.25
  224.8 1.2 convert_element_type.72
  226.0 1.1 slice.188
  227.1 1.3 add_convert_fusion
  228.4 1.1 slice.187
  229.6 1.9 fusion.7
  231.5 2.0 fusion.5
  233.5 3.1 fusion.6
  236.6 1.4 convolution_bitcast_fusion
  238.0 0.7 copy.76
  239.0 0.8 multiply_reduce_fusion
  239.9 3.4 multiply_convert_fusion
  243.3 1.4 convolution_bitcast_fusion.1
  244.7 0.8 convolution_bitcast_fusion.2
  246.2 1.6 slice-done.1
  247.7 1.3 copy-done.4
  249.0 10.6 %convolution_convert_fusion.2.dwi_ref = bf16[2048,896]{1,0:T(8,128)(2,1)} fusion(bf16[2048,2048]{1,0:T(8,128)(2,1)S(1)} %bitcast.99, f32[2048,512]{0,1:T(8,128)S(1)} %copy-done.4, f32[2048,128]{0,1:T(8,128)S(1)} %bitcast.103, f32[2048,128]{0,1:T(8,128)S(1)} %bitcast.109, f32[2048,128]{0,1:T(8,128)S(1)} %bitcast.106), kind=kOutput, calls=%fused_computation.32 | convolution fusion | flops 7532707840 | bytes 19398656 | tf_op jit(solution)/shard_map/ti,tj->ij/dot_general | solution.py:1083
  259.6 0.5 fusion.8
  260.1 13.3 %convolution_convert_fusion.q_ref = bf16[2048,2048]{1,0:T(8,128)(2,1)} fusion(bf16[2048,896]{1,0:T(8,128)(2,1)} %get-tuple-element.22, f32[2048,512]{0,1:T(8,128)S(1)} %copy-done.4, f32[2048,128]{0,1:T(8,128)S(1)} %bitcast.105, f32[2048,128]{0,1:T(8,128)S(1)} %bitcast.111, f32[2048,128]{0,1:T(8,128)S(1)} %bitcast.108), kind=kOutput, calls=%fused_computation.13 | convolution fusion | flops 7535067136 | bytes 19398656 | tf_op jit(solution)/shard_map/tj,ij->ti/dot_general | solution.py:1086
  273.5 0.4 copy.65
  274.0 10.6 %convolution_convert_fusion.3.dwf_ref = bf16[640,2048]{1,0:T(8,128)(2,1)} fusion(bf16[2048,2048]{1,0:T(8,128)(2,1)} %get-tuple-element.24, bf16[2048,512]{0,1:T(8,128)(2,1)S(1)} %copy-done.7, bf16[2048,128]{0,1:T(8,128)(2,1)S(1)} %bitcast.128), kind=kOutput, calls=%fused_computation.33 | convolution fusion | flops 5375262720 | bytes 13631488 | tf_op jit(solution)/shard_map/ti,tj->ij/dot_general | solution.py:1060
  284.6 9.3 %convolution_convert_fusion.1.p_ref = bf16[2048,2048]{1,0:T(8,128)(2,1)} fusion(bf16[640,2048]{1,0:T(8,128)(2,1)S(1)} %copy-done.12, bf16[2048,512]{0,1:T(8,128)(2,1)S(1)} %copy-done.7, bf16[2048,128]{0,1:T(8,128)(2,1)S(1)} %bitcast.129), kind=kOutput, calls=%fused_computation.14 | convolution fusion | flops 5378146304 | bytes 13631488 | tf_op jit(solution)/shard_map/dot_general | solution.py:1057
  293.9 136.3 %reduce_all.1 = (f32[512,512]{1,0:T(8,128)}, f32[512,512]{1,0:T(8,128)}, bf16[12,512,256]{2,1,0:T(8,128)(2,1)}) custom-call(bf16[2048,2048]{1,0:T(8,128)(2,1)} %convolution_convert_fusion.1.p_ref, bf16[2048,2048]{1,0:T(8,128)(2,1)} %convolution_convert_fusion.q_ref, bf16[2048,896]{1,0:T(8,128)(2,1)} %convolution_convert_fusion.2.dwi_ref, ...), custom_call_target="tpu_custom_call" | custom-call | tf_op jit(solution)/shard_map/reduce_all/pallas_call | solution.py:672
  430.2 2.4 add_add_fusion
  432.7 1.2 copy-done.2
  433.9 12.8 %finish_all.1 = (f32[512,512]{1,0:T(8,128)S(1)}, f32[4,4,8,128]{3,2,1,0:T(8,128)S(1)}, f32[4,8,512]{2,1,0:T(8,128)S(1)}) custom-call(f32[512,512]{1,0:T(8,128)S(1)} %copy-done.2, bf16[512,512]{1,0:T(8,128)(2,1)S(1)} %copy-done, bf16[512,512]{1,0:T(8,128)(2,1)S(1)} %copy-done.1, f32[512,1]{1,0:T(8,128)S(1)} %copy.77.mean_ref, f32[512,1]{1,0:T(8,128)S(1)} %copy.78.rstd_ref, ...), custom_call_target="tpu_custom_call" | custom-call | tf_op jit(solution)/shard_map/finish_all/pallas_call | solution.py:834
  446.8 0.4 concatenate.53
  447.4 0.8 multiply_subtract_fusion.2
  448.2 21.9 %muon_all.1 = (f32[12,512,256]{2,1,0:T(8,128)}, f32[12,512,256]{2,1,0:T(8,128)}, f32[12,512,256]{2,1,0:T(8,128)}) custom-call(bf16[12,512,256]{2,1,0:T(8,128)(2,1)} %get-tuple-element.28.grad_ref, f32[12,512,256]{2,1,0:T(8,128)} %bitcast.102, bf16[4,512,384]{2,1,0:T(8,128)(2,1)} %copy.56.wq_ref, bf16[512,512]{1,0:T(8,128)(2,1)} %wo_ref.3, ...), custom_call_target="tpu_custom_call" | custom-call | tf_op jit(solution)/shard_map/muon_all/pallas_call | solution.py:948
  470.1 1.0 copy.120
  (69 shorter events, 2.8 us)
Async XLA Ops:
  181.6 5.9 %copy-start.3 = (bf16[2048,2048]{1,0:T(8,128)(2,1)S(1)}, bf16[2048,2048]{1,0:T(8,128)(2,1)}, u32[]{:S(2)}) copy-start(bf16[2048,2048]{1,0:T(8,128)(2,1)} %get-tuple-element.21) | copy-start | bytes 25165828
  202.8 2.4 copy-start.5
  205.6 12.0 %copy-start.6 = (f32[2048,640]{0,1:T(8,128)S(1)}, f32[2048,640]{0,1:T(8,128)}, u32[]{:S(2)}) copy-start(f32[2048,640]{0,1:T(8,128)} %copy-done.5) | copy-start | bytes 15728644
  238.0 1.1 copy-start.8
  243.3 2.9 slice-start
  245.5 2.2 slice-start.1
  245.7 3.3 copy-start.4
  260.1 13.9 %copy-start.7 = (bf16[2048,512]{0,1:T(8,128)(2,1)S(1)}, bf16[2048,512]{0,1:T(8,128)(2,1)}, u32[]{:S(2)}) copy-start(bf16[2048,512]{0,1:T(8,128)(2,1)} %get-tuple-element.41) | copy-start | bytes 6291460
  274.0 10.6 %copy-start.12 = (bf16[640,2048]{1,0:T(8,128)(2,1)S(1)}, bf16[640,2048]{1,0:T(8,128)(2,1)}, u32[]{:S(2)}) copy-start(bf16[640,2048]{1,0:T(8,128)(2,1)} %get-tuple-element.23) | copy-start | bytes 7864324
  293.9 136.4 %copy-start = (bf16[512,512]{1,0:T(8,128)(2,1)S(1)}, bf16[512,512]{1,0:T(8,128)(2,1)}, u32[]{:S(2)}) copy-start(bf16[512,512]{1,0:T(8,128)(2,1)} %x_ref.3) | copy-start | bytes 1572868
  293.9 138.8 %copy-start.1 = (bf16[512,512]{1,0:T(8,128)(2,1)S(1)}, bf16[512,512]{1,0:T(8,128)(2,1)}, u32[]{:S(2)}) copy-start(bf16[512,512]{1,0:T(8,128)(2,1)} %g_ref.3) | copy-start | bytes 1572868
  430.2 17.2 %copy-start.10 = (f32[11,2048]{1,0:T(8,128)S(1)}, f32[11,2048]{1,0:T(8,128)}, u32[]{:S(2)}) copy-start(f32[11,2048]{1,0:T(8,128)} %param.19) | copy-start | bytes 270340
  430.2 17.2 %copy-start.11 = (f32[11,2048]{1,0:T(8,128)S(1)}, f32[11,2048]{1,0:T(8,128)}, u32[]{:S(2)}) copy-start(f32[11,2048]{1,0:T(8,128)} %param.21) | copy-start | bytes 270340
  432.7 1.2 copy-start.2
  447.2 22.8 %copy-start.9 = (f32[11,2048]{1,0:T(8,128)}, f32[11,2048]{1,0:T(8,128)S(1)}, u32[]{:S(2)}) copy-start(f32[11,2048]{1,0:T(8,128)S(1)} %concatenate.53) | copy-start | bytes 270340

commit v4 on v3

--- a/solution.py
+++ b/solution.py
@@ -81,16 +81,6 @@
     return jnp.where(causal_allowed(segment)[None], scores, MASKED_SCORE)
 
 
-def attend_forward(queries, key_vecs, values, segment, score_scale):
-    scores = masked_scores(queries, key_vecs, segment, score_scale)
-    row_max = jnp.max(scores, axis=-1, keepdims=True)
-    exp_scores = jnp.exp(scores - row_max)
-    row_total = jnp.sum(exp_scores, axis=-1, keepdims=True)
-    probs_low = to_low(exp_scores / row_total)
-    attended = jnp.einsum("hlm,mhe->lhe", probs_low, values, preferred_element_type=F32)
-    return (attended, (row_max + jnp.log(row_total))[..., 0])
-
-
 def attend_backward(queries, key_vecs, values, output_low, grad_low, logsum, segment, score_scale):
     scores = masked_scores(queries, key_vecs, segment, score_scale)
     probs = jnp.exp(scores - logsum[..., None])
@@ -129,9 +119,12 @@
     )
 
 
-def gather_kernel(n_dp, n_row, n_col, dims, x_ref, g_ref, wq_ref, wu_ref, wo_ref, wd_ref,
-                  xf, gf, wi, wf, stage_x, stage_q, stage_u, stage_o, stage_d,
-                  zs, zr, ys, yr, cs, cr, ws, wr, ds, dr, ls, lo):
+def forward_kernel(n_dp, n_row, n_col, dims,
+                   x_ref, g_ref, wq_ref, wu_ref, wo_ref, wd_ref,
+                   cos_ref, sin_ref, segc_ref, segr_ref, gain_ref, shift_ref, bias_ref,
+                   gf, wi, wf, nrm, hid, qkv, up, lse, mean_ref, rstd_ref,
+                   xv, nv, wv, stage_g, stage_o, stage_d,
+                   zs, zr, ys, yr, cs, cr, ws, wr, ds, dr, ls, lo, no):
     T, C, HF, UT = dims
     d, r, c = lax.axis_index("dp"), lax.axis_index("row"), lax.axis_index("col")
     r1 = r + 1 - 2 * lax.rem(r, 2)
@@ -139,10 +132,9 @@
     chunks = 2
     tc = T // chunks
     qw = 3 * HF
-    acts = ((x_ref, xf), (g_ref, gf))
-
-    def blk(a, rr, cc, t):
-        return acts[a][1].at[pl.ds(rr * T + t * tc, tc), pl.ds(cc * C, C)]
+    rows_all, D = n_row * T, n_col * C
+    seqs = rows_all // SEQ_LEN
+    acts = ((x_ref, xv), (g_ref, gf))
 
     barrier = pltpu.get_barrier_semaphore()
     peers = [{"row": r1}, {"row": r2}]
@@ -152,14 +144,18 @@
         pl.semaphore_signal(barrier, inc=1, device_id=peer, device_id_type=MESH)
     pl.semaphore_wait(barrier, len(peers))
 
-    def own(a, t):
-        return acts[a][0].at[pl.ds(t * tc, tc), :]
-
     def copy(src, dst, s, rcv, peer):
         return pltpu.make_async_remote_copy(
             src_ref=src, dst_ref=dst, send_sem=s, recv_sem=rcv, device_id=peer, device_id_type=MESH
         )
 
+    def blk(a, rr, cc, t):
+        return acts[a][1].at[pl.ds(pl.multiple_of(rr * T + t * tc, tc), tc),
+                             pl.ds(pl.multiple_of(cc * C, C), C)]
+
+    def own(a, t):
+        return acts[a][0].at[pl.ds(t * tc, tc), :]
+
     def z_copy(a, t, cc, src, right):
         peer = {"col": c + 1} if right else {"col": c - 1}
         return copy(src, blk(a, r, cc, t), zs.at[a, t, int(right), cc], zr.at[a, t, cc], peer)
@@ -172,57 +168,55 @@
             src, blk(a, rr, cc, t), cs.at[a, t, which, cc], cr.at[a, t, which, cc], {"row": r1}
         )
 
-    order = [(a, t) for a in range(2) for t in range(chunks)]
-
-    for a, t in order:
+    def send_own_z(a, t):
         @pl.when(c < n_col - 1)
-        def _(a=a, t=t):
+        def _():
             z_copy(a, t, c, own(a, t), True).start()
 
         @pl.when(c > 0)
-        def _(a=a, t=t):
+        def _():
             z_copy(a, t, c, own(a, t), False).start()
 
+    def send_own_row(a, t):
         y_copy(a, t, c, own(a, t)).start()
         c_copy(a, t, c, own(a, t), r, 0).start()
 
-    loads = [
-        pltpu.make_async_copy(x_ref, stage_x.at[0], ls.at[0]),
-        pltpu.make_async_copy(g_ref, stage_x.at[1], ls.at[1]),
-        pltpu.make_async_copy(wq_ref.at[c], stage_q, ls.at[2]),
-        pltpu.make_async_copy(wu_ref.at[:, pl.ds(c * UT, UT)], stage_u.at[0], ls.at[3]),
-        pltpu.make_async_copy(
-            wu_ref.at[:, pl.ds((n_col + c) * UT, UT)], stage_u.at[1], ls.at[4]
-        ),
-        pltpu.make_async_copy(wo_ref.at[pl.ds(c * HF, HF), :], stage_o, ls.at[5]),
-        pltpu.make_async_copy(wd_ref.at[pl.ds(c * UT, UT), :], stage_d.at[0], ls.at[6]),
-        pltpu.make_async_copy(wd_ref.at[pl.ds((n_col + c) * UT, UT), :], stage_d.at[1], ls.at[7]),
-    ]
-    for item in loads:
-        item.start()
-    stores = [
-        pltpu.make_async_copy(stage_x.at[0], xf.at[pl.ds(r * T, T), pl.ds(c * C, C)], lo.at[0]),
-        pltpu.make_async_copy(stage_x.at[1], gf.at[pl.ds(r * T, T), pl.ds(c * C, C)], lo.at[1]),
-        pltpu.make_async_copy(stage_q, wi.at[pl.ds(c * C, C), pl.ds(0, qw)], lo.at[2]),
-        pltpu.make_async_copy(stage_u.at[0], wi.at[pl.ds(c * C, C), pl.ds(qw, UT)], lo.at[3]),
-        pltpu.make_async_copy(stage_u.at[1], wi.at[pl.ds(c * C, C), pl.ds(qw + UT, UT)], lo.at[4]),
-        pltpu.make_async_copy(stage_o, wf.at[pl.ds(0, HF), pl.ds(c * C, C)], lo.at[5]),
-        pltpu.make_async_copy(stage_d.at[0], wf.at[pl.ds(HF, UT), pl.ds(c * C, C)], lo.at[6]),
-        pltpu.make_async_copy(stage_d.at[1], wf.at[pl.ds(HF + UT, UT), pl.ds(c * C, C)], lo.at[7]),
-    ]
-    for load, store in zip(loads, stores):
-        load.wait()
-        store.start()
+    def relay(a, s, t):
+        for right in (True, False):
+            cc = c - s if right else c + s
+
+            @pl.when((cc >= 0) & (cc < n_col))
+            def _(cc=cc, right=right):
+                z_copy(a, t, cc, blk(a, r, cc, t), right).wait_recv()
+
+                @pl.when((c < n_col - 1) if right else (c > 0))
+                def _():
+                    z_copy(a, t, cc, blk(a, r, cc, t), right).start()
+
+                y_copy(a, t, cc, blk(a, r, cc, t)).start()
+                c_copy(a, t, cc, blk(a, r, cc, t), r, 0).start()
+
+    def pass_row(a, s, t):
+        for right in (True, False):
+            cc = c - s if right else c + s
+            ok = (cc >= 0) & (cc < n_col)
+            if not right:
+                ok = ok & (s > 0)
+
+            @pl.when(ok)
+            def _(cc=cc):
+                y_copy(a, t, cc, blk(a, r, cc, t)).wait_recv()
+                c_copy(a, t, cc, blk(a, r2, cc, t), r2, 1).start()
 
     ck, hk, uk = C // n_dp, HF // n_dp, UT // n_dp
 
     def w_dst(part, dd, cc):
         if part == 0:
-            return wi.at[pl.ds(cc * C + dd * ck, ck), pl.ds(0, qw)]
+            return wv.at[pl.ds(cc * C + dd * ck, ck), pl.ds(0, qw)]
         if part == 1:
-            return wi.at[pl.ds(cc * C + dd * ck, ck), pl.ds(qw, UT)]
+            return wv.at[pl.ds(cc * C + dd * ck, ck), pl.ds(qw, UT)]
         if part == 2:
-            return wi.at[pl.ds(cc * C + dd * ck, ck), pl.ds(qw + UT, UT)]
+            return wv.at[pl.ds(cc * C + dd * ck, ck), pl.ds(qw + UT, UT)]
         if part == 3:
             return wf.at[pl.ds(dd * hk, hk), pl.ds(cc * C, C)]
         if part == 4:
@@ -248,111 +242,249 @@
             w_src(part, dest), w_dst(part, d, c), ws.at[part, k], wr.at[part, k], {"col": dest}
         )
 
-    def w_got(part, k):
-        return w_dst(part, d, lax.rem(c + n_col - k, n_col))
-
     def x_copy(part, k, j):
-        return copy(
-            w_got(part, k), w_got(part, k), ds.at[part, k, j], dr.at[part, k, j],
-            {"dp": lax.rem(d + j, n_dp)},
-        )
-
-    parts = range(6)
-
-    for s in range(1, n_col):
-        for a, t in order:
-            @pl.when(c - s >= 0)
-            def _(a=a, t=t, s=s):
-                cc = c - s
-                z_copy(a, t, cc, blk(a, r, cc, t), True).wait_recv()
-
-                @pl.when(c < n_col - 1)
-                def _():
-                    z_copy(a, t, cc, blk(a, r, cc, t), True).start()
-
-                y_copy(a, t, cc, blk(a, r, cc, t)).start()
-                c_copy(a, t, cc, blk(a, r, cc, t), r, 0).start()
-
-            @pl.when(c + s < n_col)
-            def _(a=a, t=t, s=s):
-                cc = c + s
-                z_copy(a, t, cc, blk(a, r, cc, t), False).wait_recv()
-
-                @pl.when(c > 0)
-                def _():
-                    z_copy(a, t, cc, blk(a, r, cc, t), False).start()
-
-                y_copy(a, t, cc, blk(a, r, cc, t)).start()
-                c_copy(a, t, cc, blk(a, r, cc, t), r, 0).start()
-
+        got = w_dst(part, d, lax.rem(c + n_col - k, n_col))
+        return copy(got, got, ds.at[part, k, j], dr.at[part, k, j], {"dp": lax.rem(d + j, n_dp)})
+
+    def w_send(parts, k):
         for part in parts:
-            w_copy(part, s).start()
-
-    for s in range(n_col):
-        for a, t in order:
-            for cc in ((c,) if s == 0 else (c - s, c + s)):
-                @pl.when((cc >= 0) & (cc < n_col))
-                def _(a=a, t=t, cc=cc):
-                    y_copy(a, t, cc, blk(a, r, cc, t)).wait_recv()
-                    c_copy(a, t, cc, blk(a, r2, cc, t), r2, 1).start()
-
-    for k in range(1, n_col):
+            w_copy(part, k).start()
+
+    def w_pass(parts, k):
         for part in parts:
             w_copy(part, k).wait_recv()
             for j in range(1, n_dp):
                 x_copy(part, k, j).start()
 
-    for a, t in order:
-        for cc in range(n_col):
-            c_copy(a, t, cc, blk(a, r, cc, t), r, 0).wait_recv()
-            c_copy(a, t, cc, blk(a, r, cc, t), r, 1).wait_recv()
-    for k in range(1, n_col):
+    def w_done(parts, k):
         for part in parts:
             for j in range(1, n_dp):
                 x_copy(part, k, j).wait_recv()
-    for a, t in order:
+
+    win, wfin = (0, 1, 2), (3, 4, 5)
+
+    for t in range(chunks):
+        send_own_z(0, t)
+    for t in range(chunks):
+        send_own_row(0, t)
+
+    col_at = pl.ds(c * C, C)
+    direct = [
+        pltpu.make_async_copy(x_ref, xv.at[pl.ds(r * T, T), col_at], ls.at[0]),
+        pltpu.make_async_copy(wq_ref.at[c], wv.at[col_at, pl.ds(0, qw)], ls.at[1]),
+        pltpu.make_async_copy(wu_ref.at[:, pl.ds(c * UT, UT)], wv.at[col_at, pl.ds(qw, UT)],
+                              ls.at[2]),
+        pltpu.make_async_copy(wu_ref.at[:, pl.ds((n_col + c) * UT, UT)],
+                              wv.at[col_at, pl.ds(qw + UT, UT)], ls.at[3]),
+    ]
+    loads = [
+        pltpu.make_async_copy(g_ref, stage_g, ls.at[4]),
+        pltpu.make_async_copy(wo_ref.at[pl.ds(c * HF, HF), :], stage_o, ls.at[5]),
+        pltpu.make_async_copy(wd_ref.at[pl.ds(c * UT, UT), :], stage_d.at[0], ls.at[6]),
+        pltpu.make_async_copy(wd_ref.at[pl.ds((n_col + c) * UT, UT), :], stage_d.at[1], ls.at[7]),
+    ]
+    stores = [
+        pltpu.make_async_copy(stage_g, gf.at[pl.ds(r * T, T), col_at], lo.at[0]),
+        pltpu.make_async_copy(stage_o, wf.at[pl.ds(0, HF), col_at], lo.at[1]),
+        pltpu.make_async_copy(stage_d.at[0], wf.at[pl.ds(HF, UT), col_at], lo.at[2]),
+        pltpu.make_async_copy(stage_d.at[1], wf.at[pl.ds(HF + UT, UT), col_at], lo.at[3]),
+    ]
+    for item in direct + loads:
+        item.start()
+
+    for t in range(chunks):
+        relay(0, 1, t)
+    w_send(win, 2)
+    for t in range(chunks):
+        relay(0, 2, t)
+    w_send(win, 3)
+    w_send(win, 1)
+    for t in range(chunks):
+        relay(0, 3, t)
+    for t in range(chunks):
+        send_own_z(1, t)
+        send_own_row(1, t)
+    for load, store in zip(loads, stores):
+        load.wait()
+        store.start()
+    for s in range(n_col):
+        for t in range(chunks):
+            pass_row(0, s, t)
+    for k in (2, 1, 3):
+        w_pass(win, k)
+    for t in range(chunks):
+        relay(1, 1, t)
+    w_send(wfin, 2)
+    for item in direct:
+        item.wait()
+    for t in range(chunks):
         for cc in range(n_col):
-            @pl.when((cc <= c) & (c < n_col - 1))
-            def _(a=a, t=t, cc=cc):
-                z_copy(a, t, cc, blk(a, r, cc, t), True).wait_send()
-
-            @pl.when((cc >= c) & (c > 0))
-            def _(a=a, t=t, cc=cc):
-                z_copy(a, t, cc, blk(a, r, cc, t), False).wait_send()
-
-            y_copy(a, t, cc, blk(a, r, cc, t)).wait_send()
-            c_copy(a, t, cc, blk(a, r, cc, t), r, 0).wait_send()
-            c_copy(a, t, cc, blk(a, r, cc, t), r, 1).wait_send()
+            c_copy(0, t, cc, blk(0, r, cc, t), r, 0).wait_recv()
+            c_copy(0, t, cc, blk(0, r, cc, t), r, 1).wait_recv()
+    for k in (2, 1, 3):
+        w_done(win, k)
+    keep_w = pltpu.make_async_copy(wv, wi, no.at[0])
+    keep_w.start()
+
+    tile = 256
+    tiles = rows_all // tile
+    sub = 16
+
+    def one_tile(i, carry):
+        base = pl.multiple_of(i * tile, tile)
+
+        def norm_rows(k, inner):
+            at = pl.ds(pl.multiple_of(base + k * sub, sub), sub)
+            val = xv[at, :].astype(F32)
+            mean = jnp.sum(val, axis=1, keepdims=True) / D
+            var = jnp.sum(val * val, axis=1, keepdims=True) / D - mean * mean
+            rstd = lax.rsqrt(var + NORM_EPS)
+            mean_ref[at, :] = mean
+            rstd_ref[at, :] = rstd
+            nv[at, :] = ((val - mean) * rstd * gain_ref[...] + shift_ref[...]).astype(BF16)
+            return inner
+
+        lax.fori_loop(0, tile // sub, norm_rows, 0)
+        at = pl.ds(base, tile)
+        mixed = jnp.dot(nv[at, :], wv[...], preferred_element_type=F32) + bias_ref[...]
+        cos, sin = cos_ref[at, :], sin_ref[at, :]
+        lane = lax.rem(lax.broadcasted_iota(jnp.int32, (tile, HF), 1), HEAD_DIM)
+        low = lane < ROTARY // 2
+        for j in range(2):
+            part = mixed[:, j * HF : (j + 1) * HF]
+            ahead = pltpu.roll(part, HF - ROTARY // 2, 1)
+            behind = pltpu.roll(part, ROTARY // 2, 1)
+            turned = part * cos + jnp.where(low, -ahead, behind) * sin
+            qkv[at, j * HF : (j + 1) * HF] = turned.astype(BF16)
+        qkv[at, 2 * HF : 3 * HF] = mixed[:, 2 * HF : 3 * HF].astype(BF16)
+        pre = mixed[:, qw:]
+        up[at, :] = pre
+        hid[at, HF:] = gelu_value(pre).astype(BF16)
+
+        s, t = 2 + lax.div(i, 2), lax.rem(i, 2)
+
+        @pl.when(s < n_col)
+        def _():
+            relay(1, s, t)
+
+        return carry
+
+    lax.fori_loop(0, 2, one_tile, 0)
+    w_send(wfin, 3)
+    w_send(wfin, 1)
+    lax.fori_loop(2, tiles, one_tile, 0)
+    keep_norm = pltpu.make_async_copy(nv, nrm, no.at[1])
+    keep_norm.start()
+
+    heads = HF // HEAD_DIM
+    qt = SEQ_LEN // 2
+
+    def one_seq(s, carry):
+        base = pl.multiple_of(s * SEQ_LEN, SEQ_LEN)
+        lane = lax.broadcasted_iota(jnp.int32, (qt, HF), 1)
+        for qi in range(2):
+            width = (qi + 1) * qt
+            q_at = pl.ds(base + qi * qt, qt)
+            k_at = pl.ds(base, width)
+            allowed = (segc_ref[q_at, :] == segr_ref[pl.ds(s, 1), 0:width]) & (
+                lax.broadcasted_iota(jnp.int32, (qt, width), 0) + qi * qt
+                >= lax.broadcasted_iota(jnp.int32, (qt, width), 1)
+            )
+            keys, vals = qkv[k_at, HF : 2 * HF], qkv[k_at, 2 * HF : 3 * HF]
+            queries = qkv[q_at, 0:HF]
+            total, logs = None, None
+            for h in range(heads):
+                mine = lax.div(lane, HEAD_DIM) == h
+                scores = lax.dot_general(
+                    jnp.where(mine, queries, jnp.zeros_like(queries)), keys,
+                    (((1,), (1,)), ((), ())), preferred_element_type=F32,
+                ) * (HEAD_DIM ** (-0.5))
+                scores = jnp.where(allowed, scores, MASKED_SCORE)
+                peak = jnp.max(scores, axis=1, keepdims=True)
+                weight = jnp.exp(scores - peak)
+                weight_sum = jnp.sum(weight, axis=1, keepdims=True)
+                probs = (weight * (1.0 / weight_sum)).astype(BF16)
+                out = jnp.dot(probs, vals, preferred_element_type=F32)
+                log_h = peak + jnp.log(weight_sum)
+                total = out if h == 0 else jnp.where(mine, out, total)
+                logs = jnp.broadcast_to(log_h, (qt, HF)) if h == 0 else jnp.where(mine, log_h, logs)
+            hid[q_at, 0:HF] = total.astype(BF16)
+            lse[q_at, :] = logs
+
+        @pl.when(s < n_col)
+        def _():
+            for t in range(chunks):
+                pass_row(1, s, t)
+
+        return carry
+
+    lax.fori_loop(0, seqs, one_seq, 0)
+    for k in (2, 3, 1):
+        w_pass(wfin, k)
+
+    for t in range(chunks):
+        for cc in range(n_col):
+            c_copy(1, t, cc, blk(1, r, cc, t), r, 0).wait_recv()
+            c_copy(1, t, cc, blk(1, r, cc, t), r, 1).wait_recv()
     for k in range(1, n_col):
-        for part in parts:
+        w_done(wfin, k)
+    for a in range(2):
+        for t in range(chunks):
+            for cc in range(n_col):
+                @pl.when((cc <= c) & (c < n_col - 1))
+                def _(a=a, t=t, cc=cc):
+                    z_copy(a, t, cc, blk(a, r, cc, t), True).wait_send()
+
+                @pl.when((cc >= c) & (c > 0))
+                def _(a=a, t=t, cc=cc):
+                    z_copy(a, t, cc, blk(a, r, cc, t), False).wait_send()
+
+                y_copy(a, t, cc, blk(a, r, cc, t)).wait_send()
+                c_copy(a, t, cc, blk(a, r, cc, t), r, 0).wait_send()
+                c_copy(a, t, cc, blk(a, r, cc, t), r, 1).wait_send()
+    for k in range(1, n_col):
+        for part in win + wfin:
             w_copy(part, k).wait_send()
             for j in range(1, n_dp):
                 x_copy(part, k, j).wait_send()
     for store in stores:
         store.wait()
-
-
-def gather_all(x, g, w_q, w_up, w_out, w_down, n_dp, n_row, n_col):
+    keep_w.wait()
+    keep_norm.wait()
+
+
+def forward_all(x, g, w_q, w_up, w_out, w_down, cos, sin, seg_col, seg_row, gain, shift, bias,
+                n_dp, n_row, n_col):
     T, C = x.shape
     HF = w_q.shape[2] // 3
     UT = w_up.shape[1] // (2 * n_col)
     n_in, n_out = 3 * HF + 2 * UT, HF + 2 * UT
+    rows, D = n_row * T, n_col * C
     dma = pltpu.SemaphoreType.DMA
+    vm = pl.BlockSpec(memory_space=pltpu.VMEM)
+    sds = jax.ShapeDtypeStruct
     return pl.pallas_call(
-        functools.partial(gather_kernel, n_dp, n_row, n_col, (T, C, HF, UT)),
-        name="gather_all",
+        functools.partial(forward_kernel, n_dp, n_row, n_col, (T, C, HF, UT)),
+        name="forward_all",
         out_shape=(
-            jax.ShapeDtypeStruct((n_row * T, n_col * C), BF16),
-            jax.ShapeDtypeStruct((n_row * T, n_col * C), BF16),
-            jax.ShapeDtypeStruct((n_col * C, n_in), BF16),
-            jax.ShapeDtypeStruct((n_out, n_col * C), BF16),
+            sds((rows, D), BF16),
+            sds((D, n_in), BF16),
+            sds((n_out, D), BF16),
+            sds((rows, D), BF16),
+            sds((rows, n_out), BF16),
+            sds((rows, 3 * HF), BF16),
+            sds((rows, 2 * UT), F32),
+            sds((rows, HF), F32),
+            sds((rows, 1), F32),
+            sds((rows, 1), F32),
         ),
-        in_specs=[ANY] * 6,
-        out_specs=(ANY,) * 4,
+        in_specs=[ANY] * 6 + [vm] * 7,
+        out_specs=(ANY,) * 4 + (vm,) * 6,
         scratch_shapes=[
-            pltpu.VMEM((2, T, C), BF16),
-            pltpu.VMEM((C, 3 * HF), BF16),
-            pltpu.VMEM((2, C, UT), BF16),
+            pltpu.VMEM((rows, D), BF16),
+            pltpu.VMEM((rows, D), BF16),
+            pltpu.VMEM((D, n_in), BF16),
+            pltpu.VMEM((T, C), BF16),
             pltpu.VMEM((HF, C), BF16),
             pltpu.VMEM((2, UT, C), BF16),
             dma((2, 2, 2, n_col)),
@@ -366,10 +498,13 @@
             dma((6, n_col, n_dp)),
             dma((6, n_col, n_dp)),
             dma((8,)),
-            dma((8,)),
+            dma((4,)),
+            dma((2,)),
         ],
-        compiler_params=pltpu.CompilerParams(collective_id=0, has_side_effects=True),
-    )(x, g, w_q, w_up, w_out, w_down)
+        compiler_params=pltpu.CompilerParams(
+            collective_id=0, has_side_effects=True, vmem_limit_bytes=60 * 1024 * 1024
+        ),
+    )(x, g, w_q, w_up, w_out, w_down, cos, sin, seg_col, seg_row, gain, shift, bias)
 
 
 def pick(index, table):
@@ -1019,40 +1154,41 @@
     w_q = (
         w_qkv.reshape(C, 3, n_col, HF).transpose(2, 0, 1, 3).reshape(n_col, C, 3 * HF)
     )
-    x_full, cot_rows, w_in, w_fin = gather_all(
-        inputs, cotangent, w_q, w_up, w_out, w_down, n_dp, n_row, n_col
-    )
-    seq_rows = x_full.shape[0]
-
-    x_wide = x_full.astype(F32)
-    mean_all = jnp.mean(x_wide, axis=1, keepdims=True)
-    var_all = jnp.mean(x_wide * x_wide, axis=1, keepdims=True) - mean_all * mean_all
-    rstd_all = lax.rsqrt(var_all + NORM_EPS)
-    normed = ((x_wide - mean_all) * rstd_all * gain + shift).astype(BF16)
-
-    mixed_out = jnp.dot(normed, w_in, preferred_element_type=F32)
-    qkv_part = mixed_out[:, : 3 * HF].reshape(seq_rows, 3, HF) + qkv_bias[None]
-    up_pre = mixed_out[:, 3 * HF :] + up_bias
+    cosine, sine_tab = rotary_tables(positions)
+    rows_all = positions.shape[0]
+    flat = jnp.ones((rows_all, HEAD_DIM - ROTARY), F32)
     heads_here = HF // HEAD_DIM
-    seq_count = seq_rows // SEQ_LEN
+    cos_wide = jnp.tile(jnp.concatenate([cosine, cosine, flat], axis=1), (1, heads_here))
+    sin_wide = jnp.tile(jnp.concatenate([sine_tab, sine_tab, 0.0 * flat], axis=1), (1, heads_here))
+    seq_count = rows_all // SEQ_LEN
+    cot_rows, w_in, w_fin, normed, hidden, qkv_low, up_pre, logs, mean_all, rstd_all = forward_all(
+        inputs,
+        cotangent,
+        w_q,
+        w_up,
+        w_out,
+        w_down,
+        cos_wide,
+        sin_wide,
+        segments[:, None],
+        segments.reshape(seq_count, SEQ_LEN),
+        gain[None],
+        shift[None],
+        jnp.concatenate([qkv_bias.reshape(-1), up_bias])[None],
+        n_dp,
+        n_row,
+        n_col,
+    )
+    seq_rows = rows_all
 
     def by_seq(tensor_in):
         return tensor_in.reshape((seq_count, SEQ_LEN) + tensor_in.shape[1:])
 
-    cosine, sine_tab = rotary_tables(positions)
-    queries = rotate(
-        qkv_part[:, 0].reshape(seq_rows, heads_here, HEAD_DIM), cosine, sine_tab, 1.0
-    ).astype(BF16)
-    key_vecs = rotate(
-        qkv_part[:, 1].reshape(seq_rows, heads_here, HEAD_DIM), cosine, sine_tab, 1.0
-    ).astype(BF16)
-    values = qkv_part[:, 2].reshape(seq_rows, heads_here, HEAD_DIM).astype(BF16)
-    attended, logsum = jax.vmap(attend_forward, in_axes=(0, 0, 0, 0, None))(
-        by_seq(queries), by_seq(key_vecs), by_seq(values), by_seq(segments), score_scale
-    )
-    attn_low = attended.reshape(seq_rows, HF).astype(BF16)
-    act_low = gelu_value(up_pre).astype(BF16)
-    hidden = jnp.concatenate([attn_low, act_low], axis=1)
+    queries = qkv_low[:, :HF].reshape(seq_rows, heads_here, HEAD_DIM)
+    key_vecs = qkv_low[:, HF : 2 * HF].reshape(seq_rows, heads_here, HEAD_DIM)
+    values = qkv_low[:, 2 * HF :].reshape(seq_rows, heads_here, HEAD_DIM)
+    attn_low = hidden[:, :HF]
+    logsum = by_seq(logs[:, ::HEAD_DIM]).transpose(0, 2, 1)
 
     partial_out = jnp.dot(hidden, w_fin, preferred_element_type=F32).astype(BF16)
     x_val = inputs.astype(F32)

time: 477 us -> 490 us (1.027)
  local copies, waits for them, and re-layouts: 25.1 us -> 52.9 us
  matrix products: 74.3 us -> 64 us
  other arithmetic: 30 us -> 20.5 us
  Pallas kernels: 340 us -> 347 us
    dot_general x2 -> x0, matrix products: 12.8 us -> none  [the longest x1 12 us: body(): mixed_out = jnp.dot(normed, w_in, preferred_element_type=F32)]
    reshape x0 -> x6, local copies, waits for them, and re-layouts: none -> 9.68 us  [the longest x2 4.86 us: body(): g_values = g_values.reshape(seq_rows, HF)]
    slice x3, local copies, waits for them, and re-layouts: 1.86 us -> 9.24 us  [the longest x1 5.27 us: body(): logsum = by_seq(logs[:, ::HEAD_DIM]).transpose(0, 2, 1)]
    convert_element_type x2 -> x1, other arithmetic: 9.01 us -> 2.09 us  [attend_backward(): row_delta = jnp.sum(grad_low.astype(F32) * output_low.astype(F32), axis=-1)]
    reduce_sum x2 -> x1, other arithmetic: 7.86 us -> 1.52 us  [attend_backward(): row_delta = jnp.sum(grad_low.astype(F32) * output_low.astype(F32), axis=-1)]
    pallas_call x1, Pallas kernels: 169 us -> 175 us  [forward_all(): pl.pallas_call(functools.partial(forward_kernel, n_dp, n_row, n_col, (T,...]
where the time goes in v4:
time: 490 us; the launch traced here: 486 us
  Pallas kernels  347 us (71%)
  matrix products  64 us (13%)
  local copies, waits for them, and re-layouts  52.9 us (11%)
  other arithmetic  20.5 us (4%)
    pallas_call x1, Pallas kernels, forward_all(): pl.pallas_call(functools.partial(forward_kernel, n_dp, n_row, n_col, (T,...  175 us
    pallas_call x1, Pallas kernels, reduce_all(): pl.pallas_call(functools.partial(reduce_kernel, n_row, n_col, (T, C, HF,...  138 us
    pallas_call x1, Pallas kernels, muon_all(): pl.pallas_call(functools.partial(muon_kernel, owned, per_step, HF, UT, ra...  21.9 us
    dot_general x1, matrix products, body(): jnp.einsum('ti,tj->ij', normed, grad_mixed_low, preferred_element_type=F32)  14.3 us
    unnamed x41, local copies, waits for them, and re-layouts  12.5 us
    pallas_call x1, Pallas kernels, finish_all(): pl.pallas_call(functools.partial(finish_kernel, n_dp, n_row, n_col, width...  11.9 us
    dot_general x1, matrix products, body(): jnp.einsum('tj,ij->ti', grad_mixed_low, w_in, preferred_element_type=F32)  11 us
    dot_general x1, matrix products, body(): jnp.einsum('ti,tj->ij', hidden, cot_rows, preferred_element_type=F32)  10 us

profile of v4, /device:TPU:0, one launch (start us, length us, event | category | flops | bytes accessed | tf_op | source)
XLA Modules:
  0.0 485.6 jit_solution(828575377617188761)
XLA Ops:
  2.2 0.9 slice_bitcast_fusion
  3.3 0.8 slice.79
  4.7 1.6 fusion.15
  7.0 1.7 compare_and_fusion
  8.9 1.3 copy.89.cos_ref
  10.4 1.3 copy.90.sin_ref
  11.7 1.3 copy.91.segc_ref
  13.0 2.6 copy.86
  15.6 1.5 copy.87
  17.1 1.6 copy.88.wq_ref
  18.7 174.8 %forward_all.1 = (bf16[2048,2048]{1,0:T(8,128)(2,1)}, bf16[2048,896]{1,0:T(8,128)(2,1)}, bf16[640,2048]{1,0:T(8,128)(2,1)}, bf16[2048,2048]{1,0:T(8,128)(2,1)}, ...) custom-call(bf16[512,512]{1,0:T(8,128)(2,1)} %x_ref.3, ...), custom_call_target="tpu_custom_call" | custom-call | tf_op jit(solution)/shard_map/forward_all/pallas_call | solution.py:466
  193.5 1.5 fusion.14
  194.9 1.0 constant_dynamic-slice_fusion.2.mean_ref
  195.9 1.0 constant_dynamic-slice_fusion.1.rstd_ref
  196.9 1.4 reshape.172
  200.6 5.3 %slice.83 = f32[2048,2]{1,0:T(8,128)S(1)} slice(f32[2048,128]{1,0:T(8,128)} %get-tuple-element.30), slice={[0:2048:1], [0:128:64]} | slice | bytes 32768 | tf_op jit(solution)/shard_map/slice | solution.py:1191
  206.2 2.1 slice_convert_fusion.1
  208.3 1.6 copy.100
  209.9 1.7 reshape.171
  211.6 10.0 %convolution_convert_fusion.3.dwf_ref = bf16[640,2048]{1,0:T(8,128)(2,1)} fusion(bf16[2048,640]{1,0:T(8,128)(2,1)} %get-tuple-element.27, bf16[2048,2048]{1,0:T(8,128)(2,1)} %get-tuple-element.31), kind=kOutput, calls=%fused_computation.18 | convolution fusion | flops 5370019840 | bytes 13631488 | tf_op jit(solution)/shard_map/ti,tj->ij/dot_general | solution.py:1196
  221.6 8.2 %fusion.17 = f32[2048,640]{0,1:T(8,128)S(1)} fusion(bf16[2048,2048]{1,0:T(8,128)(2,1)} %get-tuple-element.31, bf16[640,2048]{1,0:T(8,128)(2,1)S(1)} %copy-done.16), kind=kOutput, calls=%fused_computation.56 | convolution fusion | flops 5368709120 | bytes 16252928 | tf_op jit(solution)/shard_map/tj,ij->ti/dot_general | solution.py:1197
  229.9 2.5 slice.109
  232.8 1.5 multiply_reduce_fusion
  234.3 5.3 %copy.123 = f32[2048,512]{1,0:T(8,128)} copy(f32[2048,512]{0,1:T(8,128)} %slice.109) | data formatting | bytes 8388608
  239.7 6.3 %fusion.8 = f32[2048,512]{1,0:T(8,128)} fusion(f32[2048,512]{1,0:T(8,128)} %copy.123, f32[2048,512]{1,0:T(8,128)} %get-tuple-element.32), kind=kLoop, calls=%fused_computation.15 | loop fusion | flops 18874368 | bytes 12582912 | tf_op jit(solution)/shard_map/mul | solution.py:1199
  246.0 9.1 %convolution_convert_fusion.1.p_ref = bf16[2048,2048]{1,0:T(8,128)(2,1)} fusion(bf16[2048,640]{1,0:T(8,128)(2,1)S(1)} %copy-done.12, bf16[640,2048]{1,0:T(8,128)(2,1)S(1)} %copy-done.17), kind=kOutput, calls=%fused_computation.3 | convolution fusion | flops 5372903424 | bytes 13631488 | tf_op jit(solution)/shard_map/dot_general | solution.py:1193
  255.1 3.2 fusion
  258.3 1.7 convolution_bitcast_fusion
  260.0 4.3 multiply_convert_fusion
  264.3 0.8 convolution_bitcast_fusion.1
  265.2 1.4 convolution_bitcast_fusion.2
  266.7 0.8 slice.108
  267.8 1.0 pad_maximum_fusion.1
  268.8 1.5 copy.109
  270.4 2.1 pad_maximum_fusion.2
  272.5 2.6 copy.110
  275.0 2.3 copy.117
  277.3 2.6 reshape.173
  279.9 14.3 %convolution_convert_fusion.2.dwi_ref = bf16[2048,896]{1,0:T(8,128)(2,1)} fusion(bf16[2048,2048]{1,0:T(8,128)(2,1)} %get-tuple-element.34, f32[2048,512]{1,0:T(8,128)} %fusion.8, f32[2048,128]{1,0:T(8,128)S(1)} %reshape.173, f32[2048,128]{1,0:T(8,128)} %copy.110, f32[2048,128]{1,0:T(8,128)S(1)} %copy.109), kind=kOutput, calls=%fused_computation.17 | convolution fusion | flops 7532707840 | bytes 19398656 | tf_op jit(solution)/shard_map/ti,tj->ij/dot_general | solution.py:1219
  294.9 1.3 copy-done.15
  296.3 11.0 %convolution_convert_fusion.q_ref = bf16[2048,2048]{1,0:T(8,128)(2,1)} fusion(bf16[2048,896]{1,0:T(8,128)(2,1)S(1)} %copy-done.15, f32[2048,512]{1,0:T(8,128)S(1)} %copy-done.3, f32[2048,128]{1,0:T(8,128)S(1)} %reshape.173, f32[2048,128]{1,0:T(8,128)S(1)} %copy-done.5, f32[2048,128]{1,0:T(8,128)S(1)} %copy.109), kind=kOutput, calls=%fused_computation.2 | convolution fusion | flops 7535067136 | bytes 19398656 | tf_op jit(solution)/shard_map/tj,ij->ti/dot_general | solution.py:1222
  307.2 138.3 %reduce_all.1 = (f32[512,512]{1,0:T(8,128)}, f32[512,512]{1,0:T(8,128)}, bf16[12,512,256]{2,1,0:T(8,128)(2,1)}) custom-call(bf16[2048,2048]{1,0:T(8,128)(2,1)} %convolution_convert_fusion.1.p_ref, bf16[2048,2048]{1,0:T(8,128)(2,1)} %convolution_convert_fusion.q_ref, bf16[2048,896]{1,0:T(8,128)(2,1)} %convolution_convert_fusion.2.dwi_ref, ...), custom_call_target="tpu_custom_call" | custom-call | tf_op jit(solution)/shard_map/reduce_all/pallas_call | solution.py:807
  445.6 2.4 add_add_fusion
  448.0 1.2 copy-done.2
  449.3 11.9 %finish_all.1 = (f32[512,512]{1,0:T(8,128)S(1)}, f32[4,4,8,128]{3,2,1,0:T(8,128)S(1)}, f32[4,8,512]{2,1,0:T(8,128)S(1)}) custom-call(f32[512,512]{1,0:T(8,128)S(1)} %copy-done.2, bf16[512,512]{1,0:T(8,128)(2,1)S(1)} %copy-done, bf16[512,512]{1,0:T(8,128)(2,1)S(1)} %copy-done.1, f32[512,1]{1,0:T(8,128)S(1)} %constant_dynamic-slice_fusion.2.mean_ref, ...), custom_call_target="tpu_custom_call" | custom-call | tf_op jit(solution)/shard_map/finish_all/pallas_call | solution.py:969
  461.8 0.8 multiply_subtract_fusion.2
  462.6 21.9 %muon_all.1 = (f32[12,512,256]{2,1,0:T(8,128)}, f32[12,512,256]{2,1,0:T(8,128)}, f32[12,512,256]{2,1,0:T(8,128)}) custom-call(bf16[12,512,256]{2,1,0:T(8,128)(2,1)} %get-tuple-element.40.grad_ref, f32[12,512,256]{2,1,0:T(8,128)} %bitcast.66, bf16[4,512,384]{2,1,0:T(8,128)(2,1)} %copy.88.wq_ref, bf16[512,512]{1,0:T(8,128)(2,1)} %wo_ref.3, ...), custom_call_target="tpu_custom_call" | custom-call | tf_op jit(solution)/shard_map/muon_all/pallas_call | solution.py:1083
  484.5 1.0 copy.134
  (77 shorter events, 7.9 us)
Async XLA Ops:
  1.5 8.8 %copy-start.11 = (s32[4,512]{1,0:T(4,128)}, s32[4,512]{1,0:T(4,128)S(1)}, u32[]{:S(2)}) copy-start(s32[4,512]{1,0:T(4,128)S(1)} %reshape.158.segr_ref) | copy-start | bytes 24580
  6.3 4.0 copy-start.13
  8.7 3.0 copy-start.14
  211.6 10.1 %copy-start.16 = (bf16[640,2048]{1,0:T(8,128)(2,1)S(1)}, bf16[640,2048]{1,0:T(8,128)(2,1)}, u32[]{:S(2)}) copy-start(bf16[640,2048]{1,0:T(8,128)(2,1)} %get-tuple-element.28) | copy-start | bytes 7864324
  239.7 6.3 %copy-start.12 = (bf16[2048,640]{1,0:T(8,128)(2,1)S(1)}, bf16[2048,640]{1,0:T(8,128)(2,1)}, u32[]{:S(2)}) copy-start(bf16[2048,640]{1,0:T(8,128)(2,1)} %get-tuple-element.27) | copy-start | bytes 7864324
  239.7 6.3 %copy-start.17 = (bf16[640,2048]{1,0:T(8,128)(2,1)S(1)}, bf16[640,2048]{1,0:T(8,128)(2,1)}, u32[]{:S(2)}) copy-start(bf16[640,2048]{1,0:T(8,128)(2,1)} %get-tuple-element.28) | copy-start | bytes 7864324
  246.0 9.1 %copy-start.4 = (pred[4,512,512]{2,1,0:T(8,128)(4,1)S(1)}, pred[4,512,512]{2,1,0:T(8,128)(4,1)}, u32[]{:S(2)}) copy-start(pred[4,512,512]{2,1,0:T(8,128)(4,1)} %compare_and_fusion) | copy-start | bytes 3145732
  258.3 1.7 copy-start.8
  267.7 7.3 %copy-start.6 = (f32[4,512,2,64]{1,3,2,0:T(8,128)S(1)}, f32[4,512,2,64]{1,3,2,0:T(8,128)}, u32[]{:S(2)}) copy-start(f32[4,512,2,64]{1,3,2,0:T(8,128)} %convolution_bitcast_fusion) | copy-start | bytes 3145732
  279.9 14.3 %copy-start.3 = (f32[2048,512]{1,0:T(8,128)S(1)}, f32[2048,512]{1,0:T(8,128)}, u32[]{:S(2)}) copy-start(f32[2048,512]{1,0:T(8,128)} %fusion.8) | copy-start | bytes 12582916
  279.9 14.3 %copy-start.5 = (f32[2048,128]{1,0:T(8,128)S(1)}, f32[2048,128]{1,0:T(8,128)}, u32[]{:S(2)}) copy-start(f32[2048,128]{1,0:T(8,128)} %copy.110) | copy-start | bytes 3145732
  294.2 2.0 copy-start.15
  307.2 138.3 %copy-start = (bf16[512,512]{1,0:T(8,128)(2,1)S(1)}, bf16[512,512]{1,0:T(8,128)(2,1)}, u32[]{:S(2)}) copy-start(bf16[512,512]{1,0:T(8,128)(2,1)} %x_ref.3) | copy-start | bytes 1572868
  307.2 140.8 %copy-start.1 = (bf16[512,512]{1,0:T(8,128)(2,1)S(1)}, bf16[512,512]{1,0:T(8,128)(2,1)}, u32[]{:S(2)}) copy-start(bf16[512,512]{1,0:T(8,128)(2,1)} %g_ref.3) | copy-start | bytes 1572868
  445.6 16.2 %copy-start.9 = (f32[11,2048]{1,0:T(8,128)S(1)}, f32[11,2048]{1,0:T(8,128)}, u32[]{:S(2)}) copy-start(f32[11,2048]{1,0:T(8,128)} %param.19) | copy-start | bytes 270340
  445.6 16.2 %copy-start.10 = (f32[11,2048]{1,0:T(8,128)S(1)}, f32[11,2048]{1,0:T(8,128)}, u32[]{:S(2)}) copy-start(f32[11,2048]{1,0:T(8,128)} %param.21) | copy-start | bytes 270340
  448.0 1.2 copy-start.2
  461.6 22.8 %copy-start.7 = (f32[11,2048]{1,0:T(8,128)}, f32[11,2048]{1,0:T(8,128)S(1)}, u32[]{:S(2)}) copy-start(f32[11,2048]{1,0:T(8,128)S(1)} %concatenate.27) | copy-start | bytes 270340

commit v5 on v4

--- a/solution.py
+++ b/solution.py
@@ -81,9 +81,10 @@
     return jnp.where(causal_allowed(segment)[None], scores, MASKED_SCORE)
 
 
-def attend_backward(queries, key_vecs, values, output_low, grad_low, logsum, segment, score_scale):
+def attend_backward(queries, key_vecs, values, output_low, grad_low, segment, score_scale):
     scores = masked_scores(queries, key_vecs, segment, score_scale)
-    probs = jnp.exp(scores - logsum[..., None])
+    weight = jnp.exp(scores - jnp.max(scores, axis=-1, keepdims=True))
+    probs = weight * (1.0 / jnp.sum(weight, axis=-1, keepdims=True))
     grad_values = jnp.einsum("hlm,lhe->mhe", to_low(probs), grad_low, preferred_element_type=F32)
     grad_probs = jnp.einsum("lhe,mhe->hlm", grad_low, values, preferred_element_type=F32)
     row_delta = jnp.sum(grad_low.astype(F32) * output_low.astype(F32), axis=-1)
@@ -121,9 +122,9 @@
 
 def forward_kernel(n_dp, n_row, n_col, dims,
                    x_ref, g_ref, wq_ref, wu_ref, wo_ref, wd_ref,
-                   cos_ref, sin_ref, segc_ref, segr_ref, gain_ref, shift_ref, bias_ref,
-                   gf, wi, wf, nrm, hid, qkv, up, lse, mean_ref, rstd_ref,
-                   xv, nv, wv, stage_g, stage_o, stage_d,
+                   cs_ref, seg_ref, gain_ref, shift_ref, bias_ref,
+                   gf, wi, wf, nt, hid, ht, qkv, up, mean_ref, rstd_ref,
+                   xv, nb, ntv, wv, stage_g, stage_o, stage_d,
                    zs, zr, ys, yr, cs, cr, ws, wr, ds, dr, ls, lo, no):
     T, C, HF, UT = dims
     d, r, c = lax.axis_index("dp"), lax.axis_index("row"), lax.axis_index("col")
@@ -341,25 +342,26 @@
             rstd = lax.rsqrt(var + NORM_EPS)
             mean_ref[at, :] = mean
             rstd_ref[at, :] = rstd
-            nv[at, :] = ((val - mean) * rstd * gain_ref[...] + shift_ref[...]).astype(BF16)
+            nb[pl.ds(pl.multiple_of(k * sub, sub), sub), :] = (
+                (val - mean) * rstd * gain_ref[...] + shift_ref[...]
+            ).astype(BF16)
             return inner
 
         lax.fori_loop(0, tile // sub, norm_rows, 0)
         at = pl.ds(base, tile)
-        mixed = jnp.dot(nv[at, :], wv[...], preferred_element_type=F32) + bias_ref[...]
-        cos, sin = cos_ref[at, :], sin_ref[at, :]
-        lane = lax.rem(lax.broadcasted_iota(jnp.int32, (tile, HF), 1), HEAD_DIM)
-        low = lane < ROTARY // 2
+        mixed = jnp.dot(nb[...], wv[...], preferred_element_type=F32) + bias_ref[...]
+        for k in range(D // tile):
+            ntv[k * tile : (k + 1) * tile, at] = jnp.transpose(nb[:, k * tile : (k + 1) * tile])
+        cos, sin = wide_tables(cs_ref[at, :])
         for j in range(2):
             part = mixed[:, j * HF : (j + 1) * HF]
-            ahead = pltpu.roll(part, HF - ROTARY // 2, 1)
-            behind = pltpu.roll(part, ROTARY // 2, 1)
-            turned = part * cos + jnp.where(low, -ahead, behind) * sin
-            qkv[at, j * HF : (j + 1) * HF] = turned.astype(BF16)
+            qkv[at, j * HF : (j + 1) * HF] = turn(part, cos, sin, 1.0).astype(BF16)
         qkv[at, 2 * HF : 3 * HF] = mixed[:, 2 * HF : 3 * HF].astype(BF16)
         pre = mixed[:, qw:]
         up[at, :] = pre
-        hid[at, HF:] = gelu_value(pre).astype(BF16)
+        act = gelu_value(pre).astype(BF16)
+        hid[at, HF:] = act
+        ht[HF:, at] = jnp.transpose(act)
 
         s, t = 2 + lax.div(i, 2), lax.rem(i, 2)
 
@@ -373,7 +375,7 @@
     w_send(wfin, 3)
     w_send(wfin, 1)
     lax.fori_loop(2, tiles, one_tile, 0)
-    keep_norm = pltpu.make_async_copy(nv, nrm, no.at[1])
+    keep_norm = pltpu.make_async_copy(ntv, nt, no.at[1])
     keep_norm.start()
 
     heads = HF // HEAD_DIM
@@ -382,17 +384,19 @@
     def one_seq(s, carry):
         base = pl.multiple_of(s * SEQ_LEN, SEQ_LEN)
         lane = lax.broadcasted_iota(jnp.int32, (qt, HF), 1)
+        seg = seg_ref[pl.ds(s, 1), :]
+        seg_col = jnp.transpose(jnp.broadcast_to(seg, (128, SEQ_LEN)))[:, 0:1]
         for qi in range(2):
             width = (qi + 1) * qt
-            q_at = pl.ds(base + qi * qt, qt)
+            q_at = pl.ds(pl.multiple_of(base + qi * qt, qt), qt)
             k_at = pl.ds(base, width)
-            allowed = (segc_ref[q_at, :] == segr_ref[pl.ds(s, 1), 0:width]) & (
+            allowed = (seg_col[qi * qt : (qi + 1) * qt, :] == seg[:, 0:width]) & (
                 lax.broadcasted_iota(jnp.int32, (qt, width), 0) + qi * qt
                 >= lax.broadcasted_iota(jnp.int32, (qt, width), 1)
             )
             keys, vals = qkv[k_at, HF : 2 * HF], qkv[k_at, 2 * HF : 3 * HF]
             queries = qkv[q_at, 0:HF]
-            total, logs = None, None
+            total = None
             for h in range(heads):
                 mine = lax.div(lane, HEAD_DIM) == h
                 scores = lax.dot_general(
@@ -405,11 +409,10 @@
                 weight_sum = jnp.sum(weight, axis=1, keepdims=True)
                 probs = (weight * (1.0 / weight_sum)).astype(BF16)
                 out = jnp.dot(probs, vals, preferred_element_type=F32)
-                log_h = peak + jnp.log(weight_sum)
                 total = out if h == 0 else jnp.where(mine, out, total)
-                logs = jnp.broadcast_to(log_h, (qt, HF)) if h == 0 else jnp.where(mine, log_h, logs)
-            hid[q_at, 0:HF] = total.astype(BF16)
-            lse[q_at, :] = logs
+            low = total.astype(BF16)
+            hid[q_at, 0:HF] = low
+            ht[0:HF, q_at] = jnp.transpose(low)
 
         @pl.when(s < n_col)
         def _():
@@ -453,7 +456,7 @@
     keep_norm.wait()
 
 
-def forward_all(x, g, w_q, w_up, w_out, w_down, cos, sin, seg_col, seg_row, gain, shift, bias,
+def forward_all(x, g, w_q, w_up, w_out, w_down, packed, seg_row, gain, shift, bias,
                 n_dp, n_row, n_col):
     T, C = x.shape
     HF = w_q.shape[2] // 3
@@ -470,19 +473,20 @@
             sds((rows, D), BF16),
             sds((D, n_in), BF16),
             sds((n_out, D), BF16),
-            sds((rows, D), BF16),
+            sds((D, rows), BF16),
             sds((rows, n_out), BF16),
+            sds((n_out, rows), BF16),
             sds((rows, 3 * HF), BF16),
             sds((rows, 2 * UT), F32),
-            sds((rows, HF), F32),
             sds((rows, 1), F32),
             sds((rows, 1), F32),
         ),
-        in_specs=[ANY] * 6 + [vm] * 7,
+        in_specs=[ANY] * 6 + [vm] * 5,
         out_specs=(ANY,) * 4 + (vm,) * 6,
         scratch_shapes=[
             pltpu.VMEM((rows, D), BF16),
-            pltpu.VMEM((rows, D), BF16),
+            pltpu.VMEM((256, D), BF16),
+            pltpu.VMEM((D, rows), BF16),
             pltpu.VMEM((D, n_in), BF16),
             pltpu.VMEM((T, C), BF16),
             pltpu.VMEM((HF, C), BF16),
@@ -504,40 +508,83 @@
         compiler_params=pltpu.CompilerParams(
             collective_id=0, has_side_effects=True, vmem_limit_bytes=60 * 1024 * 1024
         ),
-    )(x, g, w_q, w_up, w_out, w_down, cos, sin, seg_col, seg_row, gain, shift, bias)
+    )(x, g, w_q, w_up, w_out, w_down, packed, seg_row, gain, shift, bias)
 
 
 def pick(index, table):
-    out = jnp.int32(table[0])
+    out = jnp.int32(table[0]) if isinstance(table[0], int) else table[0]
     for k in range(1, len(table)):
-        out = jnp.where(index == k, jnp.int32(table[k]), out)
+        out = jnp.where(index == k, table[k], out)
     return out
 
 
-def reduce_kernel(n_row, n_col, dims, p_ref, q_ref, dwi_ref, dwf_ref,
-                  res_ref, gn_ref, tiles_ref,
-                  abuf, obuf, sbuf, bbuf, zsb, zin, gi, gf, oi, of,
-                  a_s, a_r, o_l, y_s, y_r, z_s, z_r, x_s, x_r, g_l, t_s, t_r):
-    T, C, HF, UT, chunks = dims
-    tc = T // chunks
+def wide_tables(packed):
+    lane = lax.broadcasted_iota(jnp.int32, packed.shape, 1)
+    turned = pltpu.roll(packed, HEAD_DIM, 1)
+    first = lane < HEAD_DIM
+    return jnp.where(first, packed, turned), jnp.where(first, turned, packed)
+
+
+def turn(part, cos, sin, sign):
+    lane = lax.rem(lax.broadcasted_iota(jnp.int32, part.shape, 1), HEAD_DIM)
+    ahead = pltpu.roll(part, part.shape[1] - ROTARY // 2, 1)
+    behind = pltpu.roll(part, ROTARY // 2, 1)
+    return part * cos + jnp.where(lane < ROTARY // 2, -ahead, behind) * (sign * sin)
+
+
+def backward_kernel(n_row, n_col, dims,
+                    hid_ref, ht_ref, c_ref, wf_ref, wi_ref, nt_ref, qkv_ref, up_ref,
+                    cs_ref, seg_ref,
+                    res_ref, gn_ref, tiles_ref, part_ref,
+                    hd, hts, big, wf, wi, qv, ups, ga,
+                    abuf, obuf, asb, sbuf, bbuf, zsb, zin,
+                    dwf, dwi, gf, gu, gk,
+                    l_s, h_s, u_s, a_s, a_r, y_s, y_r, z_s, z_r, xf_s, xf_r, xu_s, xu_r, xk_s, xk_r,
+                    t_s, t_r, free_row, free_col):
+    T, C, HF, UT = dims
+    rows_all, D = n_row * T, n_col * C
+    qw, n_in, n_out = 3 * HF, 3 * HF + 2 * UT, HF + 2 * UT
     step_rows = 64
     d, r, c = lax.axis_index("dp"), lax.axis_index("row"), lax.axis_index("col")
     r1 = r + 1 - 2 * lax.rem(r, 2)
     r2 = lax.rem(r + 2, n_row)
     r12 = lax.rem(r1 + 2, n_row)
-    srcs = (p_ref, q_ref)
-    outs = (res_ref, gn_ref)
     far = [
         sorted(range(n_col), key=lambda f: (-abs(f - cc), f < cc if cc < n_col // 2 else f > cc))
         for cc in range(n_col)
     ]
     forder = [pick(c, [far[cc][i] for cc in range(n_col)]) for i in range(n_col)]
+    outs = (res_ref, gn_ref)
 
     barrier = pltpu.get_barrier_semaphore()
     peers = [{"row": r1}, {"row": r2}, {"dp": 1 - d}]
     peers += [{"col": lax.rem(c + k, n_col)} for k in range(1, n_col)]
     for peer in peers:
         pl.semaphore_signal(barrier, inc=1, device_id=peer, device_id_type=MESH)
+
+    loads = [
+        pltpu.make_async_copy(hid_ref, hd.at[:, pl.ds(2 * HF, n_out)], l_s.at[0]),
+        pltpu.make_async_copy(wf_ref, wf, l_s.at[1]),
+        pltpu.make_async_copy(c_ref, big, l_s.at[2]),
+        pltpu.make_async_copy(qkv_ref, qv, l_s.at[3]),
+        pltpu.make_async_copy(wi_ref, wi, l_s.at[4]),
+    ]
+    for item in loads:
+        item.start()
+    load_nt = pltpu.make_async_copy(nt_ref, big, l_s.at[5])
+
+    def load_ht(m, slot):
+        return pltpu.make_async_copy(ht_ref.at[pl.ds(pl.multiple_of(m * HF, HF), HF), :],
+                                     hts.at[slot], h_s.at[slot])
+
+    tile = 256
+
+    def load_up(i, slot):
+        return pltpu.make_async_copy(up_ref.at[pl.ds(pl.multiple_of(i * tile, tile), tile), :],
+                                     ups.at[slot], u_s.at[slot])
+
+    load_ht(0, 0).start()
+    load_up(0, 0).start()
     pl.semaphore_wait(barrier, len(peers))
 
     def copy(src, dst, s, rcv, peer):
@@ -545,113 +592,14 @@
             src_ref=src, dst_ref=dst, send_sem=s, recv_sem=rcv, device_id=peer, device_id_type=MESH
         )
 
-    def unit(v, rr, f, t):
-        return srcs[v].at[pl.ds(rr * T + t * tc, tc), pl.ds(f * C, C)]
-
-    def a_copy(v, h, f, t):
-        return copy(
-            unit(v, r12 if h else r1, f, t), abuf.at[v, h, f, t],
-            a_s.at[v, h, f, t], a_r.at[v, h, f, t], {"row": r1},
-        )
-
-    def o_copy(v, h, f, t):
-        return pltpu.make_async_copy(
-            unit(v, r2 if h else r, f, t), obuf.at[v, h, f, t], o_l.at[v, h, f, t]
-        )
-
-    def y_copy(v, f, t):
-        return copy(sbuf.at[v, f, t], bbuf.at[v, f, t], y_s.at[v, f, t], y_r.at[v, f, t],
-                    {"row": r2})
-
-    def z_copy(v, f, t, slot, step):
-        return copy(zsb.at[v, f, t], zin.at[v, slot, t], z_s.at[v, f, t], z_r.at[v, slot, t],
-                    {"col": c + step})
-
-    for v in range(2):
-        for i in range(n_col):
-            for t in range(chunks):
-                for h in (1, 0):
-                    a_copy(v, h, forder[i], t).start()
-                    o_copy(v, h, forder[i], t).start()
-
-    qw, n_in, n_out = 3 * HF, 3 * HF + 2 * UT, HF + 2 * UT
-    wide = (qw + UT, UT)
-    lane0 = (0, qw + UT)
-    tall = (HF, 2 * UT)
-    row0 = (0, HF)
-
-    def gi_src(own, cc):
-        return dwi_ref.at[pl.ds(cc * C, C), pl.ds(lane0[own], wide[own])]
-
-    def gf_src(own, cc):
-        return dwf_ref.at[pl.ds(row0[own], tall[own]), pl.ds(cc * C, C)]
-
-    def xi_copy(own, cc):
-        return copy(gi_src(own, cc), gi.at[cc, :, pl.ds(0, wide[own])], x_s.at[0, cc],
-                    x_r.at[0, cc], {"dp": 1 - d})
-
-    def xf_copy(own, cc):
-        return copy(gf_src(own, cc), gf.at[cc, pl.ds(0, tall[own]), :], x_s.at[1, cc],
-                    x_r.at[1, cc], {"dp": 1 - d})
-
-    def li_copy(own, cc):
-        return pltpu.make_async_copy(gi_src(own, cc), oi.at[cc, :, pl.ds(0, wide[own])],
-                                     g_l.at[0, cc])
-
-    def lf_copy(own, cc):
-        return pltpu.make_async_copy(gf_src(own, cc), of.at[cc, pl.ds(0, tall[own]), :],
-                                     g_l.at[1, cc])
-
-    def tile_parts(own, cc, source):
-        half, odd = source // 2, lax.rem(source, 2)
-        lw = 2 * HF
-        if own == 0:
-            parts = [
-                (oi.at[cc, :, pl.ds(j * HF, HF)], tiles_ref.at[2 * j + half, :, pl.ds(odd * HF, HF)])
-                for j in range(3)
-            ]
-            parts += [(oi.at[cc, :, pl.ds(qw, UT)], tiles_ref.at[8 + source])]
-            parts += [
-                (of.at[cc, pl.ds(0, HF), pl.ds(j * lw, lw)],
-                 tiles_ref.at[6 + j, pl.ds(source * HF, HF), :])
-                for j in range(2)
-            ]
-            return parts
-        parts = [(oi.at[cc, :, pl.ds(0, UT)], tiles_ref.at[source])]
-        for m in range(2):
-            for j in range(2):
-                parts.append(
-                    (of.at[cc, pl.ds(m * UT, UT), pl.ds(j * lw, lw)],
-                     tiles_ref.at[4 + 2 * (2 * m + half) + j, pl.ds(odd * UT, UT), :])
-                )
-        return parts
-
-    def t_copies(own, cc):
-        return [
-            copy(src, dst, t_s.at[n, cc], t_r.at[n, c], {"col": cc})
-            for n, (src, dst) in enumerate(tile_parts(own, cc, c))
-        ]
-
-    def t_waits(own, source):
-        return [
-            copy(src, dst, t_s.at[n, source], t_r.at[n, source], {"col": source})
-            for n, (src, dst) in enumerate(tile_parts(own, source, source))
-        ]
-
-    def t_local(own):
-        return [
-            pltpu.make_async_copy(src, dst, t_s.at[n, c])
-            for n, (src, dst) in enumerate(tile_parts(own, c, c))
-        ]
-
-    for i in range(n_col):
-        for own in range(2):
-            @pl.when(d == own)
-            def _(own=own, i=i):
-                xi_copy(1 - own, forder[i]).start()
-                xf_copy(1 - own, forder[i]).start()
-                li_copy(own, forder[i]).start()
-                lf_copy(own, forder[i]).start()
+    def a_copy(v, h, f):
+        return copy(asb.at[h, f], abuf.at[v, h, f], a_s.at[h, f], a_r.at[v, h, f], {"row": r1})
+
+    def y_copy(f):
+        return copy(sbuf.at[f], bbuf.at[f], y_s.at[f], y_r.at[f], {"row": r2})
+
+    def z_copy(f, slot, step):
+        return copy(zsb.at[f], zin.at[slot], z_s.at[f], z_r.at[slot], {"col": c + step})
 
     def looped(rows, fn):
         def one(k, carry):
@@ -659,189 +607,541 @@
             return carry
         lax.fori_loop(0, rows // step_rows, one, 0)
 
-    def first_sum(v, i):
-        f = forder[i]
-        for t in range(chunks):
-            a_copy(v, 1, f, t).wait_recv()
-            o_copy(v, 1, f, t).wait()
-
-            def add(rows, t=t):
-                sbuf[v, f, t, rows, :] = (
-                    obuf[v, 1, f, t, rows, :].astype(F32) + abuf[v, 1, f, t, rows, :].astype(F32)
-                ).astype(BF16)
-
-            looped(tc, add)
-            y_copy(v, f, t).start()
+    def first_sum(v, f):
+        a_copy(v, 1, f).wait_recv()
+
+        def add(rows):
+            sbuf[f, rows, :] = (
+                obuf[1, f, rows, :].astype(F32) + abuf[v, 1, f, rows, :].astype(F32)
+            ).astype(BF16)
+
+        looped(T, add)
+        y_copy(f).start()
 
     def second_sum(v, i):
         f = forder[i]
-        for t in range(chunks):
-            a_copy(v, 0, f, t).wait_recv()
-            o_copy(v, 0, f, t).wait()
-            y_copy(v, f, t).wait_recv()
-
-            def base(rows, t=t):
-                return (
-                    obuf[v, 0, f, t, rows, :].astype(F32)
-                    + abuf[v, 0, f, t, rows, :].astype(F32)
-                    + bbuf[v, f, t, rows, :].astype(F32)
-                )
-
-            if i < n_col - 1:
-                right = f > c
-                step = jnp.where(right, jnp.int32(1), jnp.int32(-1))
-                landed = jnp.where(f == c + step, jnp.where(right, f, jnp.int32(n_col)), f)
-                inner = jnp.where(right, c, n_col - 1 - c) > 0
-
-                @pl.when(inner)
-                def _(t=t):
-                    z_copy(v, f, t, f, 0).wait_recv()
-
-                    def add(rows):
-                        zsb[v, f, t, rows, :] = (
-                            base(rows) + zin[v, f, t, rows, :].astype(F32)
-                        ).astype(BF16)
-
-                    looped(tc, add)
-
-                @pl.when(jnp.logical_not(inner))
-                def _(t=t):
-                    def add(rows):
-                        zsb[v, f, t, rows, :] = base(rows).astype(BF16)
-
-                    looped(tc, add)
-
-                z_copy(v, f, t, landed, step).start()
-            else:
-                out = outs[v]
-
-                def put(rows, value, t=t):
-                    out[pl.ds(pl.multiple_of(rows.start + t * tc, step_rows), step_rows), :] = value
-
-                @pl.when(c > 0)
-                def _(t=t):
-                    z_copy(v, f, t, f, 0).wait_recv()
-
-                @pl.when(c < n_col - 1)
-                def _(t=t):
-                    z_copy(v, f, t, n_col, 0).wait_recv()
-
-                @pl.when(c == 0)
-                def _(t=t):
-                    looped(tc, lambda rows: put(
-                        rows, base(rows) + zin[v, n_col, t, rows, :].astype(F32)))
-
-                @pl.when(c == n_col - 1)
-                def _(t=t):
-                    looped(tc, lambda rows: put(
-                        rows, base(rows) + zin[v, f, t, rows, :].astype(F32)))
-
-                @pl.when((c > 0) & (c < n_col - 1))
-                def _(t=t):
-                    looped(tc, lambda rows: put(
-                        rows, base(rows) + zin[v, f, t, rows, :].astype(F32)
-                        + zin[v, n_col, t, rows, :].astype(F32)))
-
-    def grad_piece(i):
-        cc = forder[i]
+        a_copy(v, 0, f).wait_recv()
+        y_copy(f).wait_recv()
+
+        def base(rows):
+            return (
+                obuf[0, f, rows, :].astype(F32)
+                + abuf[v, 0, f, rows, :].astype(F32)
+                + bbuf[f, rows, :].astype(F32)
+            )
+
+        if i < n_col - 1:
+            right = f > c
+            step = jnp.where(right, jnp.int32(1), jnp.int32(-1))
+            landed = jnp.where(f == c + step, jnp.where(right, f, jnp.int32(n_col)), f)
+            inner = jnp.where(right, c, n_col - 1 - c) > 0
+
+            @pl.when(inner)
+            def _():
+                z_copy(f, f, 0).wait_recv()
+
+                def add(rows):
+                    zsb[f, rows, :] = (base(rows) + zin[f, rows, :].astype(F32)).astype(BF16)
+
+                looped(T, add)
+
+            @pl.when(jnp.logical_not(inner))
+            def _():
+                def add(rows):
+                    zsb[f, rows, :] = base(rows).astype(BF16)
+
+                looped(T, add)
+
+            z_copy(f, landed, step).start()
+        else:
+            out = outs[v]
+
+            @pl.when(c > 0)
+            def _():
+                z_copy(f, f, 0).wait_recv()
+
+            @pl.when(c < n_col - 1)
+            def _():
+                z_copy(f, n_col, 0).wait_recv()
+
+            def put(rows, value):
+                out[rows, :] = value
+
+            @pl.when(c == 0)
+            def _():
+                looped(T, lambda rows: put(rows, base(rows) + zin[n_col, rows, :].astype(F32)))
+
+            @pl.when(c == n_col - 1)
+            def _():
+                looped(T, lambda rows: put(rows, base(rows) + zin[f, rows, :].astype(F32)))
+
+            @pl.when((c > 0) & (c < n_col - 1))
+            def _():
+                looped(T, lambda rows: put(
+                    rows,
+                    base(rows) + zin[f, rows, :].astype(F32) + zin[n_col, rows, :].astype(F32)))
+
+    tall = (HF, 2 * UT)
+    row0 = (0, HF)
+    lane_u = (qw, qw + UT)
+    lw = 2 * HF
+
+    def xf_copy(own, b):
+        return copy(dwf.at[pl.ds(row0[own] + b * HF, HF), :], gf.at[pl.ds(b * HF, HF), :],
+                    xf_s.at[own, b], xf_r.at[b], {"dp": 1 - d})
+
+    def xu_copy(own, cc):
+        return copy(dwi.at[pl.ds(cc * C, C), pl.ds(lane_u[own], UT)], gu.at[cc],
+                    xu_s.at[own, cc], xu_r.at[cc], {"dp": 1 - d})
+
+    def xk_copy(cc):
+        return copy(dwi.at[pl.ds(cc * C, C), pl.ds(0, qw)], gk.at[cc], xk_s.at[cc], xk_r.at[cc],
+                    {"dp": 1 - d})
+
+    def parts_f(own, cc, source):
+        half, odd = lax.div(source, 2), lax.rem(source, 2)
+        at = cc * C
+        if own == 0:
+            return [
+                (dwf.at[pl.ds(0, HF), pl.ds(at + j * lw, lw)],
+                 tiles_ref.at[6 + j, pl.ds(source * HF, HF), :])
+                for j in range(2)
+            ]
+        return [
+            (dwf.at[pl.ds(HF + m * UT, UT), pl.ds(at + j * lw, lw)],
+             tiles_ref.at[4 + 2 * (2 * m + half) + j, pl.ds(odd * UT, UT), :])
+            for m in range(2) for j in range(2)
+        ]
+
+    def parts_u(own, cc, source):
+        dst = tiles_ref.at[8 + source] if own == 0 else tiles_ref.at[source]
+        return [(dwi.at[pl.ds(cc * C, C), pl.ds(lane_u[own], UT)], dst)]
+
+    def parts_k(own, cc, source):
+        half, odd = lax.div(source, 2), lax.rem(source, 2)
+        return [
+            (dwi.at[pl.ds(cc * C, C), pl.ds(j * HF, HF)],
+             tiles_ref.at[2 * j + half, :, pl.ds(odd * HF, HF)])
+            for j in range(3)
+        ]
+
+    kinds = {"f": (parts_f, 0), "u": (parts_u, 4), "k": (parts_k, 5)}
+
+    def t_send(kind, own, cc):
+        parts, first = kinds[kind]
+        return [
+            copy(src, dst, t_s.at[first + n, cc], t_r.at[first + n, c], {"col": cc})
+            for n, (src, dst) in enumerate(parts(own, cc, c))
+        ]
+
+    def t_wait(kind, own, source):
+        parts, first = kinds[kind]
+        return [
+            copy(src, dst, t_s.at[first + n, source], t_r.at[first + n, source], {"col": source})
+            for n, (src, dst) in enumerate(parts(own, source, source))
+        ]
+
+    def t_local(kind, own):
+        parts, first = kinds[kind]
+        return [
+            pltpu.make_async_copy(src, dst, t_s.at[first + n, c])
+            for n, (src, dst) in enumerate(parts(own, c, c))
+        ]
+
+    def owned_kinds(own):
+        return ("f", "u", "k") if own == 0 else ("f", "u")
+
+    def spread(kind, own):
+        for k in range(1, n_col):
+            for item in t_send(kind, own, lax.rem(c + k, n_col)):
+                item.start()
+        for item in t_local(kind, own):
+            item.start()
+
+    def add_f():
         for own in range(2):
             @pl.when(d == own)
             def _(own=own):
-                xi_copy(own, cc).wait_recv()
-                xf_copy(own, cc).wait_recv()
-                li_copy(own, cc).wait()
-                lf_copy(own, cc).wait()
-
-                def add_i(rows):
-                    at = (cc, rows, pl.ds(0, wide[own]))
-                    oi[at] = (oi[at].astype(F32) + gi[at].astype(F32)).astype(BF16)
-
-                def add_f(rows):
-                    at = (cc, rows, slice(None))
-                    of[at] = (of[at].astype(F32) + gf[at].astype(F32)).astype(BF16)
-
-                looped(C, add_i)
-                looped(tall[own], add_f)
-                for item in t_local(own) if i == n_col - 1 else t_copies(own, cc):
+                for b in range(tall[own] // HF):
+                    xf_copy(own, b).wait_recv()
+
+                def add(rows):
+                    at = (pl.ds(pl.multiple_of(rows.start + row0[own], step_rows), step_rows),
+                          slice(None))
+                    dwf[at] = (dwf[at].astype(F32) + gf[rows, :].astype(F32)).astype(BF16)
+
+                looped(tall[own], add)
+                spread("f", own)
+
+    def add_piece(kind, own, cc):
+        lane, width, buf, waiter = (
+            (lane_u[own], UT, gu, xu_copy(own, cc)) if kind == "u" else (0, qw, gk, xk_copy(cc))
+        )
+        waiter.wait_recv()
+
+        def add(rows):
+            at = (pl.ds(pl.multiple_of(rows.start + cc * C, step_rows), step_rows),
+                  pl.ds(lane, width))
+            dwi[at] = (dwi[at].astype(F32) + buf[cc, rows, :].astype(F32)).astype(BF16)
+
+        looped(C, add)
+
+    def add_u(i):
+        for own in range(2):
+            @pl.when(d == own)
+            def _(own=own):
+                cc = forder[i]
+                add_piece("u", own, cc)
+                for item in t_local("u", own) if i == n_col - 1 else t_send("u", own, cc):
                     item.start()
 
+    def add_k(i):
+        @pl.when(d == 0)
+        def _():
+            cc = forder[i]
+            add_piece("k", 0, cc)
+            for item in t_local("k", 0) if i == n_col - 1 else t_send("k", 0, cc):
+                item.start()
+
+    loads[0].wait()
+    loads[1].wait()
+
+    def p_unit(rr, f):
+        at = pl.ds(pl.multiple_of(rr * T, T), T)
+        lanes = pl.ds(pl.multiple_of(f * C, C), C)
+        return jnp.dot(hd[at, 2 * HF :], wf[:, lanes], preferred_element_type=F32).astype(BF16)
+
+    def p_step(i, carry):
+        f = pick(i, forder)
+        for h, rr in ((1, r12), (0, r1)):
+            asb[h, f] = p_unit(rr, f)
+            a_copy(0, h, f).start()
+        for h, rr in ((1, r2), (0, r)):
+            obuf[h, f] = p_unit(rr, f)
+
+        @pl.when(i > 0)
+        def _():
+            first_sum(0, pick(i - 1, forder))
+
+        return carry
+
+    lax.fori_loop(0, n_col, p_step, 0)
+
+    loads[2].wait()
+    blocks = n_out // HF
+
+    def f_step(m, carry):
+        slot = lax.rem(m, 2)
+        load_ht(m, slot).wait()
+
+        @pl.when(m + 1 < blocks)
+        def _():
+            load_ht(m + 1, 1 - slot).start()
+
+        at = pl.ds(pl.multiple_of(m * HF, HF), HF)
+        dwf[at, :] = jnp.dot(hts[slot], big[...], preferred_element_type=F32).astype(BF16)
+
+        @pl.when((m == 0) & (d == 1))
+        def _():
+            xf_copy(0, 0).start()
+
+        @pl.when((m > 0) & (d == 0))
+        def _():
+            xf_copy(1, m - 1).start()
+
+        return carry
+
+    lax.fori_loop(0, blocks, f_step, 0)
+    first_sum(0, forder[n_col - 1])
+    second_sum(0, 0)
+
+    part_ref[...] = jnp.zeros_like(part_ref)
+    tiles = rows_all // tile
+
+    def b_step(i, carry):
+        slot = lax.rem(i, 2)
+        load_up(i, slot).wait()
+
+        @pl.when(i + 1 < tiles)
+        def _():
+            load_up(i + 1, 1 - slot).start()
+
+        at = pl.ds(pl.multiple_of(i * tile, tile), tile)
+        back = lax.dot_general(
+            big[at, :], wf[...], (((1,), (1,)), ((), ())), preferred_element_type=F32
+        )
+        ga[at, :] = back[:, :HF].astype(BF16)
+        grad = back[:, HF:] * gelu_slope(ups[slot])
+        hd[at, qw:] = grad.astype(BF16)
+        sums = jnp.sum(grad, axis=0, keepdims=True)
+        for k in range(2 * UT // 128):
+            part_ref[3 + k : 4 + k, :] += sums[:, k * 128 : (k + 1) * 128]
+        return carry
+
+    lax.fori_loop(0, tiles, b_step, 0)
+    load_nt.start()
+    second_sum(0, 1)
+    load_nt.wait()
+
+    def u_step(i, carry):
+        cc = pick(i, forder)
+        at = pl.ds(pl.multiple_of(cc * C, C), C)
+        dwi[at, qw:] = jnp.dot(big[at, :], hd[:, qw:], preferred_element_type=F32).astype(BF16)
+        for own in range(2):
+            @pl.when(d == own)
+            def _(own=own):
+                xu_copy(1 - own, cc).start()
+
+        return carry
+
+    lax.fori_loop(0, n_col, u_step, 0)
+    second_sum(0, 2)
+
+    loads[3].wait()
+    loads[4].wait()
+    heads = HF // HEAD_DIM
+    qt = SEQ_LEN // 2
+    scale = HEAD_DIM ** (-0.5)
+    per_row = T // SEQ_LEN
+    first_dim = (((0,), (0,)), ((), ()))
+    last_dim = (((1,), (1,)), ((), ()))
+
+    def attend_seq(s):
+        base = pl.multiple_of(s * SEQ_LEN, SEQ_LEN)
+        lane = lax.broadcasted_iota(jnp.int32, (qt, HF), 1)
+        seg = seg_ref[pl.ds(s, 1), :]
+        seg_col = jnp.transpose(jnp.broadcast_to(seg, (128, SEQ_LEN)))[:, 0:1]
+        grad_q, grad_k, grad_v = [], None, None
+        for qi in range(2):
+            width = (qi + 1) * qt
+            q_at = pl.ds(base + qi * qt, qt)
+            k_at = pl.ds(base, width)
+            allowed = (seg_col[qi * qt : (qi + 1) * qt, :] == seg[:, 0:width]) & (
+                lax.broadcasted_iota(jnp.int32, (qt, width), 0) + qi * qt
+                >= lax.broadcasted_iota(jnp.int32, (qt, width), 1)
+            )
+            queries, g_att = qv[q_at, 0:HF], ga[q_at, :]
+            keys, vals = qv[k_at, HF : 2 * HF], qv[k_at, 2 * HF : 3 * HF]
+            both = g_att.astype(F32) * hd[q_at, 2 * HF : 3 * HF].astype(F32)
+            gq, gks, gvs = None, None, None
+            for h in range(heads):
+                mine = lax.div(lane, HEAD_DIM) == h
+                q_h = jnp.where(mine, queries, jnp.zeros_like(queries))
+                g_h = jnp.where(mine, g_att, jnp.zeros_like(g_att))
+                scores = lax.dot_general(q_h, keys, last_dim, preferred_element_type=F32) * scale
+                scores = jnp.where(allowed, scores, MASKED_SCORE)
+                peak = jnp.max(scores, axis=1, keepdims=True)
+                weight = jnp.exp(scores - peak)
+                probs = weight * (1.0 / jnp.sum(weight, axis=1, keepdims=True))
+                delta = jnp.sum(jnp.where(mine, both, 0.0), axis=1, keepdims=True)
+                g_prob = lax.dot_general(g_h, vals, last_dim, preferred_element_type=F32)
+                g_score = (probs * (g_prob - delta) * scale).astype(BF16)
+                gq_h = jnp.dot(g_score, keys, preferred_element_type=F32)
+                gk_h = lax.dot_general(g_score, q_h, first_dim, preferred_element_type=F32)
+                gv_h = lax.dot_general(probs.astype(BF16), g_h, first_dim,
+                                       preferred_element_type=F32)
+                gq = gq_h if h == 0 else jnp.where(mine, gq_h, gq)
+                gks = gk_h if h == 0 else gks + gk_h
+                gvs = gv_h if h == 0 else gvs + gv_h
+            grad_q.append(gq)
+            if qi == 0:
+                grad_k, grad_v = gks, gvs
+            else:
+                grad_k = jnp.concatenate([grad_k + gks[:qt], gks[qt:]], axis=0)
+                grad_v = jnp.concatenate([grad_v + gvs[:qt], gvs[qt:]], axis=0)
+        s_at = pl.ds(base, SEQ_LEN)
+        cos, sin = wide_tables(cs_ref[s_at, :])
+        grads = (
+            turn(jnp.concatenate(grad_q, axis=0), cos, sin, -1.0),
+            turn(grad_k, cos, sin, -1.0),
+            grad_v,
+        )
+        for j, grad in enumerate(grads):
+            part_ref[j : j + 1, :] += jnp.sum(grad, axis=0, keepdims=True)
+            hd[s_at, j * HF : (j + 1) * HF] = grad.astype(BF16)
+
+    def q_unit(rr, f):
+        at = pl.ds(pl.multiple_of(rr * T, T), T)
+        feats = pl.ds(pl.multiple_of(f * C, C), C)
+        return lax.dot_general(
+            hd[at, :], wi[feats, :], last_dim, preferred_element_type=F32
+        ).astype(BF16)
+
+    def credit(first):
+        if first:
+            pl.semaphore_signal(free_row, inc=1, device_id={"row": r2}, device_id_type=MESH)
+        for n, step in enumerate((1, -1)):
+            @pl.when((c + step >= 0) & (c + step < n_col))
+            def _(n=n, step=step):
+                if first:
+                    pl.semaphore_signal(free_col.at[n], inc=1, device_id={"col": c + step},
+                                        device_id_type=MESH)
+                else:
+                    pl.semaphore_wait(free_col.at[1 - n], 1)
+        if not first:
+            pl.semaphore_wait(free_row, 1)
+
+    def s_step(m, carry):
+        rr = pick(m, [r12, r2, r1, r])
+
+        def seq(s, inner):
+            attend_seq(rr * per_row + s)
+            return inner
+
+        lax.fori_loop(0, per_row, seq, 0)
+
+        @pl.when(m == 1)
+        def _():
+            second_sum(0, n_col - 1)
+            for f in range(n_col):
+                y_copy(f).wait_send()
+            for i in range(n_col - 1):
+                z_copy(forder[i], forder[i], 0).wait_send()
+            credit(True)
+            credit(False)
+
+        def units(i, inner):
+            f = pick(i, forder)
+            value = q_unit(rr, f)
+
+            def to_peer(h):
+                a_copy(0, h, f).wait_send()
+                asb[h, f] = value
+                a_copy(1, h, f).start()
+
+            @pl.when(m == 0)
+            def _():
+                to_peer(1)
+
+            @pl.when(m == 2)
+            def _():
+                to_peer(0)
+
+            @pl.when(m == 1)
+            def _():
+                obuf[1, f] = value
+                first_sum(1, f)
+
+            @pl.when(m == 3)
+            def _():
+                obuf[0, f] = value
+
+            return inner
+
+        lax.fori_loop(0, n_col, units, 0)
+        return carry
+
+    lax.fori_loop(0, n_row, s_step, 0)
+    add_f()
+
+    def k_step(i, carry):
+        cc = pick(i, forder)
+        at = pl.ds(pl.multiple_of(cc * C, C), C)
+        dwi[at, 0:qw] = jnp.dot(big[at, :], hd[:, 0:qw], preferred_element_type=F32).astype(BF16)
+
+        @pl.when(d == 1)
+        def _():
+            xk_copy(cc).start()
+
+        return carry
+
+    lax.fori_loop(0, n_col, k_step, 0)
     for i in range(n_col):
-        first_sum(0, i)
+        second_sum(1, i) if i < n_col - 1 else None
+        add_u(i)
     for i in range(n_col):
-        second_sum(0, i)
-        first_sum(1, i)
-        grad_piece(i)
-    for i in range(n_col):
-        second_sum(1, i)
+        add_k(i)
+    second_sum(1, n_col - 1)
 
     for own in range(2):
         @pl.when(d == own)
         def _(own=own):
-            for k in range(1, n_col):
-                for item in t_waits(own, lax.rem(c + k, n_col)):
-                    item.wait_recv()
-            for i in range(n_col - 1):
-                for item in t_copies(own, forder[i]):
-                    item.wait_send()
-            for item in t_local(own):
-                item.wait()
+            for kind in owned_kinds(own):
+                for k in range(1, n_col):
+                    for item in t_wait(kind, own, lax.rem(c + k, n_col)):
+                        item.wait_recv()
+                for k in range(1, n_col):
+                    for item in t_send(kind, own, lax.rem(c + k, n_col)):
+                        item.wait_send()
+                for item in t_local(kind, own):
+                    item.wait()
+            for b in range(tall[1 - own] // HF):
+                xf_copy(1 - own, b).wait_send()
             for cc in range(n_col):
-                xi_copy(1 - own, cc).wait_send()
-                xf_copy(1 - own, cc).wait_send()
-    for v in range(2):
-        for t in range(chunks):
-            for f in range(n_col):
-                a_copy(v, 0, f, t).wait_send()
-                a_copy(v, 1, f, t).wait_send()
-                y_copy(v, f, t).wait_send()
-            for i in range(n_col - 1):
-                z_copy(v, forder[i], t, forder[i], 0).wait_send()
-
-
-def reduce_all(p, q, dwi, dwf, T, C, HF, UT, n_row, n_col):
+                xu_copy(1 - own, cc).wait_send()
+                if own == 1:
+                    xk_copy(cc).wait_send()
+    for f in range(n_col):
+        a_copy(1, 0, f).wait_send()
+        a_copy(1, 1, f).wait_send()
+        y_copy(f).wait_send()
+    for i in range(n_col - 1):
+        z_copy(forder[i], forder[i], 0).wait_send()
+
+
+def backward_all(hid, ht, cot, w_fin, w_in, nt, qkv, up, packed, seg_row, T, C, HF, UT, n_row, n_col):
     dma = pltpu.SemaphoreType.DMA
-    chunks = 2
-    tc = T // chunks
-    unit = (chunks, tc, C)
     vm = pl.BlockSpec(memory_space=pltpu.VMEM)
+    rows, D = n_row * T, n_col * C
+    n_in, n_out = 3 * HF + 2 * UT, HF + 2 * UT
+    unit = (T, C)
+    V = pltpu.VMEM
     return pl.pallas_call(
-        functools.partial(reduce_kernel, n_row, n_col, (T, C, HF, UT, chunks)),
-        name="reduce_all",
+        functools.partial(backward_kernel, n_row, n_col, (T, C, HF, UT)),
+        name="backward_all",
         out_shape=(
-            jax.ShapeDtypeStruct((T, C), F32),
-            jax.ShapeDtypeStruct((T, C), F32),
+            jax.ShapeDtypeStruct(unit, F32),
+            jax.ShapeDtypeStruct(unit, F32),
             jax.ShapeDtypeStruct((12, C, UT), BF16),
+            jax.ShapeDtypeStruct((8, 128), F32),
         ),
-        in_specs=[ANY] * 4,
-        out_specs=(vm, vm, ANY),
+        in_specs=[ANY] * 8 + [vm] * 2,
+        out_specs=(vm, vm, ANY, vm),
         scratch_shapes=[
-            pltpu.VMEM((2, 2, n_col) + unit, BF16),
-            pltpu.VMEM((2, 2, n_col) + unit, BF16),
-            pltpu.VMEM((2, n_col) + unit, BF16),
-            pltpu.VMEM((2, n_col) + unit, BF16),
-            pltpu.VMEM((2, n_col) + unit, BF16),
-            pltpu.VMEM((2, n_col + 1) + unit, BF16),
-            pltpu.VMEM((n_col, C, 3 * HF + UT), BF16),
-            pltpu.VMEM((n_col, 2 * UT, C), BF16),
-            pltpu.VMEM((n_col, C, 3 * HF + UT), BF16),
-            pltpu.VMEM((n_col, 2 * UT, C), BF16),
-            dma((2, 2, n_col, chunks)),
-            dma((2, 2, n_col, chunks)),
-            dma((2, 2, n_col, chunks)),
-            dma((2, n_col, chunks)),
-            dma((2, n_col, chunks)),
-            dma((2, n_col, chunks)),
-            dma((2, n_col + 1, chunks)),
+            V((rows, n_in), BF16),
+            V((2, HF, rows), BF16),
+            V((rows, D), BF16),
+            V((n_out, D), BF16),
+            V((D, n_in), BF16),
+            V((rows, 3 * HF), BF16),
+            V((2, 256, 2 * UT), F32),
+            V((rows, HF), BF16),
+            V((2, 2, n_col) + unit, BF16),
+            V((2, n_col) + unit, BF16),
+            V((2, n_col) + unit, BF16),
+            V((n_col,) + unit, BF16),
+            V((n_col,) + unit, BF16),
+            V((n_col,) + unit, BF16),
+            V((n_col + 1,) + unit, BF16),
+            V((n_out, D), BF16),
+            V((D, n_in), BF16),
+            V((2 * UT, D), BF16),
+            V((n_col, C, UT), BF16),
+            V((n_col, C, 3 * HF), BF16),
+            dma((6,)),
+            dma((2,)),
+            dma((2,)),
             dma((2, n_col)),
+            dma((2, 2, n_col)),
+            dma((n_col,)),
+            dma((n_col,)),
+            dma((n_col,)),
+            dma((n_col + 1,)),
+            dma((2, 2 * UT // HF)),
+            dma((2 * UT // HF,)),
             dma((2, n_col)),
-            dma((2, n_col)),
-            dma((6, n_col)),
-            dma((6, n_col)),
+            dma((n_col,)),
+            dma((n_col,)),
+            dma((n_col,)),
+            dma((8, n_col)),
+            dma((8, n_col)),
+            pltpu.SemaphoreType.REGULAR,
+            pltpu.SemaphoreType.REGULAR((2,)),
         ],
         compiler_params=pltpu.CompilerParams(
-            collective_id=1, has_side_effects=True, vmem_limit_bytes=62 * 1024 * 1024
+            collective_id=1, has_side_effects=True, vmem_limit_bytes=67043328
         ),
-    )(p, q, dwi, dwf)
+    )(hid, ht, cot, w_fin, w_in, nt, qkv, up, packed, seg_row)
 
 
 def finish_kernel(n_dp, n_row, n_col, width, gn_ref, x_ref, g_ref, mean_ref, rstd_ref, gain_ref, part_ref,
@@ -1113,6 +1413,39 @@
     return block(p), block(q), owned
 
 
+def backward_plain(hidden, hidden_t, cot, w_fin, w_in, norm_t, qkv, up_pre, cosine, sine_tab, segments, HF):
+    rows = cot.shape[0]
+    seqs, heads = rows // SEQ_LEN, HF // HEAD_DIM
+
+    def by_head(tensor_in):
+        return tensor_in.reshape(seqs, SEQ_LEN, heads, HEAD_DIM)
+
+    partial_out = jnp.dot(hidden, w_fin, preferred_element_type=F32).astype(BF16)
+    grad_w_fin = jnp.dot(hidden_t, cot, preferred_element_type=F32).astype(BF16)
+    back = jnp.einsum("tj,ij->ti", cot, w_fin, preferred_element_type=F32)
+    grad_up = back[:, HF:] * gelu_slope(up_pre)
+    grads = jax.vmap(attend_backward, in_axes=(0, 0, 0, 0, 0, 0, None))(
+        by_head(qkv[:, :HF]),
+        by_head(qkv[:, HF : 2 * HF]),
+        by_head(qkv[:, 2 * HF :]),
+        by_head(hidden[:, :HF]),
+        by_head(back[:, :HF].astype(BF16)),
+        segments.reshape(seqs, SEQ_LEN),
+        HEAD_DIM ** (-0.5),
+    )
+    g_q, g_k, g_v = [item.reshape(rows, heads, HEAD_DIM) for item in grads]
+    g_q = rotate(g_q, cosine, sine_tab, -1.0)
+    g_k = rotate(g_k, cosine, sine_tab, -1.0)
+    grad_mixed = jnp.concatenate(
+        [item.reshape(rows, HF) for item in (g_q, g_k, g_v)] + [grad_up], axis=1
+    )
+    low = grad_mixed.astype(BF16)
+    grad_w_in = jnp.dot(norm_t, low, preferred_element_type=F32).astype(BF16)
+    partial_norm = jnp.einsum("tj,ij->ti", low, w_in, preferred_element_type=F32).astype(BF16)
+    part = jnp.pad(jnp.sum(grad_mixed, axis=0).reshape(-1, 128), ((0, 1), (0, 0)))
+    return (partial_out, partial_norm, grad_w_in, grad_w_fin), part
+
+
 def body(
     inputs,
     cotangent,
@@ -1126,7 +1459,6 @@
     tile_moment,
     vector_moment,
 ):
-    d_index = lax.axis_index("dp")
     row_index = lax.axis_index("row")
     col_index = lax.axis_index("col")
     n_dp, n_row, n_col = lax.axis_size("dp"), lax.axis_size("row"), lax.axis_size("col")
@@ -1135,7 +1467,6 @@
     row_width = w_qkv.shape[2]
     HF = row_width // n_col
     UT = w_up.shape[1] // (2 * n_col)
-    score_scale = HEAD_DIM ** (-0.5)
     feat_start = (row_index * n_col + col_index) * HF
     unit_a = (row_index * 2 * n_col + col_index) * UT
     unit_b = unit_a + n_col * UT
@@ -1157,21 +1488,20 @@
     cosine, sine_tab = rotary_tables(positions)
     rows_all = positions.shape[0]
     flat = jnp.ones((rows_all, HEAD_DIM - ROTARY), F32)
-    heads_here = HF // HEAD_DIM
-    cos_wide = jnp.tile(jnp.concatenate([cosine, cosine, flat], axis=1), (1, heads_here))
-    sin_wide = jnp.tile(jnp.concatenate([sine_tab, sine_tab, 0.0 * flat], axis=1), (1, heads_here))
+    packed = jnp.concatenate(
+        [cosine, cosine, flat, sine_tab, sine_tab, 0.0 * flat], axis=1
+    )
     seq_count = rows_all // SEQ_LEN
-    cot_rows, w_in, w_fin, normed, hidden, qkv_low, up_pre, logs, mean_all, rstd_all = forward_all(
+    seg_row = segments.reshape(seq_count, SEQ_LEN)
+    cot_rows, w_in, w_fin, norm_t, hidden, hidden_t, qkv_low, up_pre, mean_all, rstd_all = forward_all(
         inputs,
         cotangent,
         w_q,
         w_up,
         w_out,
         w_down,
-        cos_wide,
-        sin_wide,
-        segments[:, None],
-        segments.reshape(seq_count, SEQ_LEN),
+        packed,
+        seg_row,
         gain[None],
         shift[None],
         jnp.concatenate([qkv_bias.reshape(-1), up_bias])[None],
@@ -1179,62 +1509,19 @@
         n_row,
         n_col,
     )
-    seq_rows = rows_all
-
-    def by_seq(tensor_in):
-        return tensor_in.reshape((seq_count, SEQ_LEN) + tensor_in.shape[1:])
-
-    queries = qkv_low[:, :HF].reshape(seq_rows, heads_here, HEAD_DIM)
-    key_vecs = qkv_low[:, HF : 2 * HF].reshape(seq_rows, heads_here, HEAD_DIM)
-    values = qkv_low[:, 2 * HF :].reshape(seq_rows, heads_here, HEAD_DIM)
-    attn_low = hidden[:, :HF]
-    logsum = by_seq(logs[:, ::HEAD_DIM]).transpose(0, 2, 1)
-
-    partial_out = jnp.dot(hidden, w_fin, preferred_element_type=F32).astype(BF16)
-    x_val = inputs.astype(F32)
-
-    grad_w_fin = jnp.einsum("ti,tj->ij", hidden, cot_rows, preferred_element_type=F32).astype(BF16)
-    back = jnp.einsum("tj,ij->ti", cot_rows, w_fin, preferred_element_type=F32)
-    grad_attn_low = back[:, :HF].astype(BF16)
-    grad_up = back[:, HF:] * gelu_slope(up_pre)
-    g_queries, g_keys, g_values = jax.vmap(attend_backward, in_axes=(0, 0, 0, 0, 0, 0, 0, None))(
-        by_seq(queries),
-        by_seq(key_vecs),
-        by_seq(values),
-        by_seq(attn_low.reshape(seq_rows, heads_here, HEAD_DIM)),
-        by_seq(grad_attn_low.reshape(seq_rows, heads_here, HEAD_DIM)),
-        logsum,
-        by_seq(segments),
-        score_scale,
-    )
-    g_queries = rotate(
-        g_queries.reshape(seq_rows, heads_here, HEAD_DIM), cosine, sine_tab, -1.0
-    ).reshape(seq_rows, HF)
-    g_keys = rotate(g_keys.reshape(seq_rows, heads_here, HEAD_DIM), cosine, sine_tab, -1.0).reshape(
-        seq_rows, HF
-    )
-    g_values = g_values.reshape(seq_rows, HF)
-    grad_mixed = jnp.concatenate([g_queries, g_keys, g_values, grad_up], axis=1)
-    grad_mixed_low = grad_mixed.astype(BF16)
-    grad_w_in = jnp.einsum(
-        "ti,tj->ij", normed, grad_mixed_low, preferred_element_type=F32
-    ).astype(BF16)
-    partial_norm = jnp.einsum(
-        "tj,ij->ti", grad_mixed_low, w_in, preferred_element_type=F32
-    ).astype(BF16)
-
     if n_dp == 2:
-        branch, grad_norm, owned_low = reduce_all(
-            partial_out, partial_norm, grad_w_in, grad_w_fin, T, C, HF, UT, n_row, n_col
+        branch, grad_norm, owned_low, part = backward_all(
+            hidden, hidden_t, cot_rows, w_fin, w_in, norm_t, qkv_low, up_pre, packed, seg_row,
+            T, C, HF, UT, n_row, n_col,
         )
     else:
-        branch, grad_norm, owned_low = reduce_plain(
-            partial_out, partial_norm, grad_w_in, grad_w_fin, C, HF, UT, n_col, row_width
+        partials, part = backward_plain(
+            hidden, hidden_t, cot_rows, w_fin, w_in, norm_t, qkv_low, up_pre, cosine, sine_tab, segments, HF
         )
+        branch, grad_norm, owned_low = reduce_plain(*partials, C, HF, UT, n_col, row_width)
+    x_val = inputs.astype(F32)
     result = x_val + branch + out_bias
 
-    sums = jnp.sum(grad_mixed, axis=0)
-    part = jnp.pad(sums.reshape(-1, 128), ((0, 1), (0, 0)))
     grad_input, vec_a, vec_b = finish_all(
         grad_norm,
         inputs,

time: 490 us -> 411 us (0.84)
  matrix products: 64 us -> 0 us
  Pallas kernels: 347 us -> 380 us
  local copies, waits for them, and re-layouts: 52.9 us -> 22.5 us
  other arithmetic: 20.5 us -> 7.21 us
    dot_general x10 -> x0, matrix products: 64 us -> none  [the longest x1 14.3 us: body(): jnp.einsum('ti,tj->ij', normed, grad_mixed_low, preferred_element_type=F32)]
    pallas_call x1, Pallas kernels: 138 us -> 167 us  [backward_all(): pl.pallas_call(functools.partial(backward_kernel, n_row, n_col, (T, C, HF...]
    slice x6 -> x0, local copies, waits for them, and re-layouts: 10.2 us -> none  [the longest x1 5.27 us: body(): logsum = by_seq(logs[:, ::HEAD_DIM]).transpose(0, 2, 1)]
    reshape x7 -> x1, local copies, waits for them, and re-layouts: 9.86 us -> 0.61 us  [body(): seg_row = segments.reshape(seq_count, SEQ_LEN)]
    another operation x10 -> x0, local copies, waits for them, and re-layouts: 6.88 us -> none  [the longest x6 4.07 us: by_seq(): return tensor_in.reshape((seq_count, SEQ_LEN) + tensor_in.shape[1:])]
    mul x2 -> x0, other arithmetic: 6.83 us -> none  [the longest x1 6.29 us: body(): grad_up = back[:, HF:] * gelu_slope(up_pre)]
    unnamed x41 -> x28, local copies, waits for them, and re-layouts: 12.5 us -> 9.51 us
where the time goes in v5:
time: 411 us; the launch traced here: 410 us
  Pallas kernels  380 us (92%)
  local copies, waits for them, and re-layouts  22.5 us (5%)
  other arithmetic  7.21 us (2%)
    pallas_call x1, Pallas kernels, forward_all(): pl.pallas_call(functools.partial(forward_kernel, n_dp, n_row, n_col, (T,...  175 us
    pallas_call x1, Pallas kernels, backward_all(): pl.pallas_call(functools.partial(backward_kernel, n_row, n_col, (T, C, HF...  167 us
    pallas_call x1, Pallas kernels, muon_all(): pl.pallas_call(functools.partial(muon_kernel, owned, per_step, HF, UT, ra...  22 us
    pallas_call x1, Pallas kernels, finish_all(): pl.pallas_call(functools.partial(finish_kernel, n_dp, n_row, n_col, width...  15.5 us
    unnamed x28, local copies, waits for them, and re-layouts  9.51 us

profile of v5, /device:TPU:0, one launch (start us, length us, event | category | flops | bytes accessed | tf_op | source)
XLA Modules:
  0.0 410.1 jit_solution(4295054273959753215)
XLA Ops:
  0.6 0.9 slice_bitcast_fusion
  1.6 0.1 fusion.1
  1.7 0.8 slice.39
  2.5 0.6 broadcast_in_dim.21.bias_ref
  3.1 1.6 fusion
  4.7 0.7 convert_element_type.7
  5.4 3.7 multiply_sine_fusion
  9.1 0.1 broadcast_in_dim.20
  9.2 1.0 mul.70
  10.2 4.3 %concatenate.9.cs_ref = f32[2048,128]{1,0:T(8,128)} concatenate(f32[2048,16]{1,0:T(8,128)S(1)} %get-tuple-element.57, f32[2048,16]{1,0:T(8,128)S(1)} %get-tuple-element.57, f32[2048,32]{1,0:T(8,128)S(1)} %broadcast_in_dim.20, f32[2048,16]{1,0:T(8,128)S(1)} %get-tuple-element.56, f32[2048,16]{1,0:T(8,128)S(1)} %get-tuple-element.56, f32[2048,32]{1,0:T(8,128)} %mul.70), dimensions={1} | concatenate | bytes 2097152 | tf_op jit(solution)/shard_map/concatenate | solution.py:1491
  14.5 1.7 copy.31
  16.3 0.0 copy-start.11
  16.3 0.1 copy.32
  16.4 1.6 copy.34.wq_ref
  18.0 0.0 copy-done.11
  18.0 0.6 reshape.64.seg_ref
  18.6 175.4 %forward_all.1 = (bf16[2048,2048]{1,0:T(8,128)(2,1)}, bf16[2048,896]{1,0:T(8,128)(2,1)}, bf16[640,2048]{1,0:T(8,128)(2,1)}, bf16[2048,2048]{1,0:T(8,128)(2,1)}, ...) custom-call(bf16[512,512]{1,0:T(8,128)(2,1)} %x_ref.3, ...), custom_call_target="tpu_custom_call" | custom-call | tf_op jit(solution)/shard_map/forward_all/pallas_call | solution.py:469
  194.0 1.9 constant_dynamic-slice_fusion.1
  195.8 166.7 %backward_all.1 = (f32[512,512]{1,0:T(8,128)}, f32[512,512]{1,0:T(8,128)}, bf16[12,512,256]{2,1,0:T(8,128)(2,1)}, f32[8,128]{1,0:T(8,128)}) custom-call(bf16[2048,640]{1,0:T(8,128)(2,1)} %get-tuple-element.28.hid_ref, bf16[640,2048]{1,0:T(8,128)(2,1)} %get-tuple-element.29.ht_ref, bf16[2048,2048]{1,0:T(8,128)(2,1)} %get-tuple-element.30.c_ref, ...), custom_call_target="tpu_custom_call" | custom-call | tf_op jit(solution)/shard_map/backward_all/pallas_call | solution.py:1089
  362.5 0.7 dynamic-slice_add_fusion
  363.3 0.0 copy-start
  363.3 1.0 copy-done
  364.3 0.0 copy-start.2
  364.3 1.0 copy-done.2
  365.3 0.0 copy-start.3
  365.3 1.2 copy-done.3
  366.6 0.0 copy-start.4
  366.6 0.9 copy-done.4
  367.5 0.9 copy-done.5
  368.5 0.0 copy-start.6
  368.5 0.7 copy-done.6
  369.1 0.0 copy-start.9
  369.1 0.0 copy-start.10
  369.1 15.5 %finish_all.1 = (f32[512,512]{1,0:T(8,128)S(1)}, f32[4,4,8,128]{3,2,1,0:T(8,128)S(1)}, f32[4,8,512]{2,1,0:T(8,128)S(1)}) custom-call(f32[512,512]{1,0:T(8,128)S(1)} %copy-done.3, bf16[512,512]{1,0:T(8,128)(2,1)S(1)} %copy-done, bf16[512,512]{1,0:T(8,128)(2,1)S(1)} %copy-done.2, f32[512,1]{1,0:T(8,128)S(1)} %copy-done.5, f32[512,1]{1,0:T(8,128)S(1)} %copy-done.4, ...), custom_call_target="tpu_custom_call" | custom-call | tf_op jit(solution)/shard_map/finish_all/pallas_call | solution.py:1269
  384.8 0.2 concatenate.11
  385.0 0.0 copy-start.7
  385.1 0.1 multiply_reduce_fusion
  385.2 0.0 copy-done.9
  385.2 0.0 copy-done.10
  385.2 0.8 multiply_subtract_fusion
  386.0 0.0 copy-start.1
  386.0 0.0 copy-start.8
  386.0 22.0 %muon_all.1 = (f32[12,512,256]{2,1,0:T(8,128)}, f32[12,512,256]{2,1,0:T(8,128)}, f32[12,512,256]{2,1,0:T(8,128)}) custom-call(bf16[12,512,256]{2,1,0:T(8,128)(2,1)} %get-tuple-element.42.grad_ref, f32[12,512,256]{2,1,0:T(8,128)} %bitcast.27, bf16[4,512,384]{2,1,0:T(8,128)(2,1)} %copy.34.wq_ref, bf16[512,512]{1,0:T(8,128)(2,1)} %wo_ref.3, ...), custom_call_target="tpu_custom_call" | custom-call | tf_op jit(solution)/shard_map/muon_all/pallas_call | solution.py:1383
  408.0 0.0 copy-done.7
  408.0 0.0 copy-done.1
  408.0 0.0 copy-done.8
  408.0 1.1 add_add_fusion
  409.2 1.0 copy.40
  (14 shorter events, 0.2 us)
Async XLA Ops:
  16.3 1.7 copy-start.11
  363.3 1.0 copy-start
  364.3 1.0 copy-start.2
  365.3 1.2 copy-start.3
  366.6 0.9 copy-start.4
  367.5 0.9 copy-start.5
  368.5 0.7 copy-start.6
  369.1 16.1 %copy-start.9 = (f32[11,2048]{1,0:T(8,128)S(1)}, f32[11,2048]{1,0:T(8,128)}, u32[]{:S(2)}) copy-start(f32[11,2048]{1,0:T(8,128)} %param.19) | copy-start | bytes 270340
  369.1 16.1 %copy-start.10 = (f32[11,2048]{1,0:T(8,128)S(1)}, f32[11,2048]{1,0:T(8,128)}, u32[]{:S(2)}) copy-start(f32[11,2048]{1,0:T(8,128)} %param.21) | copy-start | bytes 270340
  385.0 22.9 %copy-start.7 = (f32[11,2048]{1,0:T(8,128)}, f32[11,2048]{1,0:T(8,128)S(1)}, u32[]{:S(2)}) copy-start(f32[11,2048]{1,0:T(8,128)S(1)} %concatenate.11) | copy-start | bytes 270340
  386.0 22.0 %copy-start.1 = (bf16[512,512]{1,0:T(8,128)(2,1)S(1)}, bf16[512,512]{1,0:T(8,128)(2,1)}, u32[]{:S(2)}) copy-start(bf16[512,512]{1,0:T(8,128)(2,1)} %x_ref.3) | copy-start | bytes 1572868
  386.0 22.0 %copy-start.8 = (f32[512,512]{1,0:T(8,128)S(1)}, f32[512,512]{1,0:T(8,128)}, u32[]{:S(2)}) copy-start(f32[512,512]{1,0:T(8,128)} %get-tuple-element.36) | copy-start | bytes 3145732

commit v6 on v5

--- a/solution.py
+++ b/solution.py
@@ -120,11 +120,26 @@
     )
 
 
+def pick(index, table):
+    out = jnp.int32(table[0]) if isinstance(table[0], int) else table[0]
+    for k in range(1, len(table)):
+        out = jnp.where(index == k, table[k], out)
+    return out
+
+
+def far_order(c, n_col):
+    far = [
+        sorted(range(n_col), key=lambda f: (-abs(f - cc), f < cc if cc < n_col // 2 else f > cc))
+        for cc in range(n_col)
+    ]
+    return [pick(c, [far[cc][i] for cc in range(n_col)]) for i in range(n_col)]
+
+
 def forward_kernel(n_dp, n_row, n_col, dims,
                    x_ref, g_ref, wq_ref, wu_ref, wo_ref, wd_ref,
-                   cs_ref, seg_ref, gain_ref, shift_ref, bias_ref,
-                   gf, wi, wf, nt, hid, ht, qkv, up, mean_ref, rstd_ref,
-                   xv, nb, ntv, wv, stage_g, stage_o, stage_d,
+                   pos_ref, seg_ref, freq_ref, vec_ref,
+                   gf, wi, wf, nt, hid_out, ht_out, qkv_out, up_out, cs_out, mean_ref, rstd_ref,
+                   xv, ntv, wv, hid, ht, qkv, up, tab, mean_v, rstd_v, stage_g, stage_o, stage_d,
                    zs, zr, ys, yr, cs, cr, ws, wr, ds, dr, ls, lo, no):
     T, C, HF, UT = dims
     d, r, c = lax.axis_index("dp"), lax.axis_index("row"), lax.axis_index("col")
@@ -136,6 +151,7 @@
     rows_all, D = n_row * T, n_col * C
     seqs = rows_all // SEQ_LEN
     acts = ((x_ref, xv), (g_ref, gf))
+    forder = far_order(c, n_col)
 
     barrier = pltpu.get_barrier_semaphore()
     peers = [{"row": r1}, {"row": r2}]
@@ -237,30 +253,38 @@
             return wd_ref.at[pl.ds(cc * UT + d * uk, uk), :]
         return wd_ref.at[pl.ds((n_col + cc) * UT + d * uk, uk), :]
 
-    def w_copy(part, k):
-        dest = lax.rem(c + k, n_col)
+    def w_copy(part, dest):
         return copy(
-            w_src(part, dest), w_dst(part, d, c), ws.at[part, k], wr.at[part, k], {"col": dest}
+            w_src(part, dest), w_dst(part, d, c), ws.at[part, dest], wr.at[part, c], {"col": dest}
         )
 
-    def x_copy(part, k, j):
-        got = w_dst(part, d, lax.rem(c + n_col - k, n_col))
-        return copy(got, got, ds.at[part, k, j], dr.at[part, k, j], {"dp": lax.rem(d + j, n_dp)})
-
-    def w_send(parts, k):
-        for part in parts:
-            w_copy(part, k).start()
-
-    def w_pass(parts, k):
-        for part in parts:
-            w_copy(part, k).wait_recv()
+    def w_from(part, source):
+        return copy(
+            w_src(part, source), w_dst(part, d, source), ws.at[part, source], wr.at[part, source],
+            {"col": source},
+        )
+
+    def x_copy(part, source, j):
+        got = w_dst(part, d, source)
+        return copy(got, got, ds.at[part, source, j], dr.at[part, source, j],
+                    {"dp": lax.rem(d + j, n_dp)})
+
+    others = forder[: n_col - 1]
+
+    def w_send(part):
+        for dest in others:
+            w_copy(part, dest).start()
+
+    def w_pass(part):
+        for source in others[::-1]:
+            w_from(part, source).wait_recv()
             for j in range(1, n_dp):
-                x_copy(part, k, j).start()
-
-    def w_done(parts, k):
-        for part in parts:
+                x_copy(part, source, j).start()
+
+    def w_done(part):
+        for source in others:
             for j in range(1, n_dp):
-                x_copy(part, k, j).wait_recv()
+                x_copy(part, source, j).wait_recv()
 
     win, wfin = (0, 1, 2), (3, 4, 5)
 
@@ -293,45 +317,77 @@
     for item in direct + loads:
         item.start()
 
-    for t in range(chunks):
-        relay(0, 1, t)
-    w_send(win, 2)
-    for t in range(chunks):
-        relay(0, 2, t)
-    w_send(win, 3)
-    w_send(win, 1)
-    for t in range(chunks):
-        relay(0, 3, t)
+    for n in range(1, n_col):
+        for t in range(chunks):
+            relay(0, n, t)
+        w_send(win[n - 1])
     for t in range(chunks):
         send_own_z(1, t)
         send_own_row(1, t)
     for load, store in zip(loads, stores):
         load.wait()
         store.start()
-    for s in range(n_col):
+    w_pass(win[0])
+
+    def one_table(n, carry):
+        rows = jnp.broadcast_to(pos_ref[pl.ds(n, 1), :], (2 * HEAD_DIM, SEQ_LEN))
+        angle = jnp.transpose(rows) * freq_ref[...]
+        lane = lax.broadcasted_iota(jnp.int32, angle.shape, 1)
+        turns = jnp.floor(angle * (2.0 / math.pi) + 0.5)
+        rest = angle - turns * 1.5703125
+        rest = rest - turns * 4.837512969970703125e-4
+        rest = rest - turns * 7.54978994889188e-8
+        sq = rest * rest
+        sine = rest + rest * sq * (
+            -1.6666654611e-1 + sq * (8.3321608736e-3 - sq * 1.9515295891e-4)
+        )
+        cosine = 1.0 - 0.5 * sq + sq * sq * (
+            4.166664568298827e-2 + sq * (-1.388731625493765e-3 + sq * 2.443315711809948e-5)
+        )
+        quarter = jnp.where(lane < HEAD_DIM, turns, turns - 1.0)
+        quarter = quarter - 4.0 * jnp.floor(quarter * 0.25)
+        odd = (quarter == 1.0) | (quarter == 3.0)
+        value = jnp.where(odd, sine, cosine)
+        value = jnp.where((quarter == 1.0) | (quarter == 2.0), -value, value)
+        tab[pl.ds(pl.multiple_of(n * SEQ_LEN, SEQ_LEN), SEQ_LEN), :] = value
+        return carry
+
+    lax.fori_loop(0, seqs, one_table, 0)
+    keep_cs = pltpu.make_async_copy(tab, cs_out, no.at[2])
+    keep_cs.start()
+    for n in range(n_col):
         for t in range(chunks):
-            pass_row(0, s, t)
-    for k in (2, 1, 3):
-        w_pass(win, k)
-    for t in range(chunks):
-        relay(1, 1, t)
-    w_send(wfin, 2)
+            pass_row(0, n, t)
+    w_pass(win[1])
     for item in direct:
         item.wait()
     for t in range(chunks):
         for cc in range(n_col):
             c_copy(0, t, cc, blk(0, r, cc, t), r, 0).wait_recv()
             c_copy(0, t, cc, blk(0, r, cc, t), r, 1).wait_recv()
-    for k in (2, 1, 3):
-        w_done(win, k)
-    keep_w = pltpu.make_async_copy(wv, wi, no.at[0])
-    keep_w.start()
+
+    def act_sent(a):
+        for t in range(chunks):
+            for cc in range(n_col):
+                @pl.when((cc <= c) & (c < n_col - 1))
+                def _(t=t, cc=cc):
+                    z_copy(a, t, cc, blk(a, r, cc, t), True).wait_send()
+
+                @pl.when((cc >= c) & (c > 0))
+                def _(t=t, cc=cc):
+                    z_copy(a, t, cc, blk(a, r, cc, t), False).wait_send()
+
+                y_copy(a, t, cc, blk(a, r, cc, t)).wait_send()
+                c_copy(a, t, cc, blk(a, r, cc, t), r, 0).wait_send()
+                c_copy(a, t, cc, blk(a, r, cc, t), r, 1).wait_send()
+
+    act_sent(0)
 
     tile = 256
     tiles = rows_all // tile
     sub = 16
 
-    def one_tile(i, carry):
+    def norm_tile(i, carry):
         base = pl.multiple_of(i * tile, tile)
 
         def norm_rows(k, inner):
@@ -340,19 +396,45 @@
             mean = jnp.sum(val, axis=1, keepdims=True) / D
             var = jnp.sum(val * val, axis=1, keepdims=True) / D - mean * mean
             rstd = lax.rsqrt(var + NORM_EPS)
-            mean_ref[at, :] = mean
-            rstd_ref[at, :] = rstd
-            nb[pl.ds(pl.multiple_of(k * sub, sub), sub), :] = (
-                (val - mean) * rstd * gain_ref[...] + shift_ref[...]
-            ).astype(BF16)
+            mean_v[at, :] = mean
+            rstd_v[at, :] = rstd
+            xv[at, :] = ((val - mean) * rstd * vec_ref[5:6, :] + vec_ref[6:7, :]).astype(BF16)
             return inner
 
         lax.fori_loop(0, tile // sub, norm_rows, 0)
         at = pl.ds(base, tile)
-        mixed = jnp.dot(nb[...], wv[...], preferred_element_type=F32) + bias_ref[...]
         for k in range(D // tile):
-            ntv[k * tile : (k + 1) * tile, at] = jnp.transpose(nb[:, k * tile : (k + 1) * tile])
-        cos, sin = wide_tables(cs_ref[at, :])
+            ntv[k * tile : (k + 1) * tile, at] = jnp.transpose(xv[at, k * tile : (k + 1) * tile])
+        return carry
+
+    lax.fori_loop(0, tiles // 2, norm_tile, 0)
+    w_pass(win[2])
+    for t in range(chunks):
+        relay(1, 1, t)
+    w_send(wfin[0])
+    lax.fori_loop(tiles // 2, tiles, norm_tile, 0)
+    keep_norm = pltpu.make_async_copy(ntv, nt, no.at[1])
+    keep_norm.start()
+    own_rows = pl.ds(pl.multiple_of(r * T, T), T)
+    mean_ref[...] = mean_v[own_rows, :]
+    rstd_ref[...] = rstd_v[own_rows, :]
+    for part in win:
+        w_done(part)
+    keep_w = pltpu.make_async_copy(wv, wi, no.at[0])
+    keep_w.start()
+
+    q_lanes = pl.ds(pl.multiple_of((r * n_col + c) * HF, HF), HF)
+    biases = [vec_ref[j : j + 1, q_lanes] for j in range(3)]
+    biases += [
+        vec_ref[pl.ds(7 + r, 1), pl.ds(pl.multiple_of((m * n_col + c) * UT, UT), UT)]
+        for m in range(2)
+    ]
+    bias = jnp.concatenate(biases, axis=1)
+
+    def one_tile(i, carry):
+        at = pl.ds(pl.multiple_of(i * tile, tile), tile)
+        mixed = jnp.dot(xv[at, :], wv[...], preferred_element_type=F32) + bias
+        cos, sin = wide_tables(tab[at, :])
         for j in range(2):
             part = mixed[:, j * HF : (j + 1) * HF]
             qkv[at, j * HF : (j + 1) * HF] = turn(part, cos, sin, 1.0).astype(BF16)
@@ -372,11 +454,14 @@
         return carry
 
     lax.fori_loop(0, 2, one_tile, 0)
-    w_send(wfin, 3)
-    w_send(wfin, 1)
-    lax.fori_loop(2, tiles, one_tile, 0)
-    keep_norm = pltpu.make_async_copy(ntv, nt, no.at[1])
-    keep_norm.start()
+    w_send(wfin[1])
+    lax.fori_loop(2, 4, one_tile, 0)
+    w_send(wfin[2])
+    lax.fori_loop(4, tiles, one_tile, 0)
+    keep_up = pltpu.make_async_copy(up, up_out, no.at[3])
+    keep_qkv = pltpu.make_async_copy(qkv, qkv_out, no.at[4])
+    keep_up.start()
+    keep_qkv.start()
 
     heads = HF // HEAD_DIM
     qt = SEQ_LEN // 2
@@ -422,41 +507,32 @@
         return carry
 
     lax.fori_loop(0, seqs, one_seq, 0)
-    for k in (2, 3, 1):
-        w_pass(wfin, k)
+    keep_hid = pltpu.make_async_copy(hid, hid_out, no.at[5])
+    keep_ht = pltpu.make_async_copy(ht, ht_out, no.at[6])
+    keep_hid.start()
+    keep_ht.start()
+    for part in wfin:
+        w_pass(part)
 
     for t in range(chunks):
         for cc in range(n_col):
             c_copy(1, t, cc, blk(1, r, cc, t), r, 0).wait_recv()
             c_copy(1, t, cc, blk(1, r, cc, t), r, 1).wait_recv()
-    for k in range(1, n_col):
-        w_done(wfin, k)
-    for a in range(2):
-        for t in range(chunks):
-            for cc in range(n_col):
-                @pl.when((cc <= c) & (c < n_col - 1))
-                def _(a=a, t=t, cc=cc):
-                    z_copy(a, t, cc, blk(a, r, cc, t), True).wait_send()
-
-                @pl.when((cc >= c) & (c > 0))
-                def _(a=a, t=t, cc=cc):
-                    z_copy(a, t, cc, blk(a, r, cc, t), False).wait_send()
-
-                y_copy(a, t, cc, blk(a, r, cc, t)).wait_send()
-                c_copy(a, t, cc, blk(a, r, cc, t), r, 0).wait_send()
-                c_copy(a, t, cc, blk(a, r, cc, t), r, 1).wait_send()
-    for k in range(1, n_col):
-        for part in win + wfin:
-            w_copy(part, k).wait_send()
+    for part in wfin:
+        w_done(part)
+    act_sent(1)
+    for part in win + wfin:
+        for peer in others:
+            w_copy(part, peer).wait_send()
             for j in range(1, n_dp):
-                x_copy(part, k, j).wait_send()
+                x_copy(part, peer, j).wait_send()
     for store in stores:
         store.wait()
-    keep_w.wait()
-    keep_norm.wait()
-
-
-def forward_all(x, g, w_q, w_up, w_out, w_down, packed, seg_row, gain, shift, bias,
+    for item in (keep_w, keep_norm, keep_cs, keep_up, keep_qkv, keep_hid, keep_ht):
+        item.wait()
+
+
+def forward_all(x, g, w_q, w_up, w_out, w_down, pos_row, seg_row, freq, vectors,
                 n_dp, n_row, n_col):
     T, C = x.shape
     HF = w_q.shape[2] // 3
@@ -478,16 +554,23 @@
             sds((n_out, rows), BF16),
             sds((rows, 3 * HF), BF16),
             sds((rows, 2 * UT), F32),
-            sds((rows, 1), F32),
-            sds((rows, 1), F32),
+            sds((rows, 2 * HEAD_DIM), F32),
+            sds((T, 1), F32),
+            sds((T, 1), F32),
         ),
-        in_specs=[ANY] * 6 + [vm] * 5,
-        out_specs=(ANY,) * 4 + (vm,) * 6,
+        in_specs=[ANY] * 6 + [vm] * 4,
+        out_specs=(ANY,) * 9 + (vm,) * 2,
         scratch_shapes=[
             pltpu.VMEM((rows, D), BF16),
-            pltpu.VMEM((256, D), BF16),
             pltpu.VMEM((D, rows), BF16),
             pltpu.VMEM((D, n_in), BF16),
+            pltpu.VMEM((rows, n_out), BF16),
+            pltpu.VMEM((n_out, rows), BF16),
+            pltpu.VMEM((rows, 3 * HF), BF16),
+            pltpu.VMEM((rows, 2 * UT), F32),
+            pltpu.VMEM((rows, 2 * HEAD_DIM), F32),
+            pltpu.VMEM((rows, 1), F32),
+            pltpu.VMEM((rows, 1), F32),
             pltpu.VMEM((T, C), BF16),
             pltpu.VMEM((HF, C), BF16),
             pltpu.VMEM((2, UT, C), BF16),
@@ -503,19 +586,12 @@
             dma((6, n_col, n_dp)),
             dma((8,)),
             dma((4,)),
-            dma((2,)),
+            dma((7,)),
         ],
         compiler_params=pltpu.CompilerParams(
             collective_id=0, has_side_effects=True, vmem_limit_bytes=60 * 1024 * 1024
         ),
-    )(x, g, w_q, w_up, w_out, w_down, packed, seg_row, gain, shift, bias)
-
-
-def pick(index, table):
-    out = jnp.int32(table[0]) if isinstance(table[0], int) else table[0]
-    for k in range(1, len(table)):
-        out = jnp.where(index == k, table[k], out)
-    return out
+    )(x, g, w_q, w_up, w_out, w_down, pos_row, seg_row, freq, vectors)
 
 
 def wide_tables(packed):
@@ -549,11 +625,7 @@
     r1 = r + 1 - 2 * lax.rem(r, 2)
     r2 = lax.rem(r + 2, n_row)
     r12 = lax.rem(r1 + 2, n_row)
-    far = [
-        sorted(range(n_col), key=lambda f: (-abs(f - cc), f < cc if cc < n_col // 2 else f > cc))
-        for cc in range(n_col)
-    ]
-    forder = [pick(c, [far[cc][i] for cc in range(n_col)]) for i in range(n_col)]
+    forder = far_order(c, n_col)
     outs = (res_ref, gn_ref)
 
     barrier = pltpu.get_barrier_semaphore()
@@ -1413,7 +1485,8 @@
     return block(p), block(q), owned
 
 
-def backward_plain(hidden, hidden_t, cot, w_fin, w_in, norm_t, qkv, up_pre, cosine, sine_tab, segments, HF):
+def backward_plain(hidden, hidden_t, cot, w_fin, w_in, norm_t, qkv, up_pre, positions, segments, HF):
+    cosine, sine_tab = rotary_tables(positions)
     rows = cot.shape[0]
     seqs, heads = rows // SEQ_LEN, HF // HEAD_DIM
 
@@ -1459,7 +1532,6 @@
     tile_moment,
     vector_moment,
 ):
-    row_index = lax.axis_index("row")
     col_index = lax.axis_index("col")
     n_dp, n_row, n_col = lax.axis_size("dp"), lax.axis_size("row"), lax.axis_size("col")
     T, C = inputs.shape
@@ -1467,47 +1539,25 @@
     row_width = w_qkv.shape[2]
     HF = row_width // n_col
     UT = w_up.shape[1] // (2 * n_col)
-    feat_start = (row_index * n_col + col_index) * HF
-    unit_a = (row_index * 2 * n_col + col_index) * UT
-    unit_b = unit_a + n_col * UT
     col_start = col_index * C
-    gain, shift = vectors[5], vectors[6]
-    norm_gain = lax.dynamic_slice_in_dim(gain, col_start, C)
+    norm_gain = lax.dynamic_slice_in_dim(vectors[5], col_start, C)
     out_bias = lax.dynamic_slice_in_dim(vectors[3] + vectors[4], col_start, C)
-    qkv_bias = lax.dynamic_slice_in_dim(vectors[0:3], feat_start, HF, axis=1)
-    up_flat = vectors[7:].reshape(-1)
-    up_bias = jnp.concatenate(
-        [
-            lax.dynamic_slice_in_dim(up_flat, unit_a, UT),
-            lax.dynamic_slice_in_dim(up_flat, unit_b, UT),
-        ]
-    )
     w_q = (
         w_qkv.reshape(C, 3, n_col, HF).transpose(2, 0, 1, 3).reshape(n_col, C, 3 * HF)
     )
-    cosine, sine_tab = rotary_tables(positions)
     rows_all = positions.shape[0]
-    flat = jnp.ones((rows_all, HEAD_DIM - ROTARY), F32)
-    packed = jnp.concatenate(
-        [cosine, cosine, flat, sine_tab, sine_tab, 0.0 * flat], axis=1
+    seq_count = rows_all // SEQ_LEN
+    half = jnp.exp(
+        jnp.arange(ROTARY // 2, dtype=F32) * (-2.0 * math.log(10000.0) / ROTARY)
     )
-    seq_count = rows_all // SEQ_LEN
+    freq = jnp.tile(jnp.concatenate([half, half, jnp.zeros((HEAD_DIM - ROTARY,), F32)]), 2)
     seg_row = segments.reshape(seq_count, SEQ_LEN)
-    cot_rows, w_in, w_fin, norm_t, hidden, hidden_t, qkv_low, up_pre, mean_all, rstd_all = forward_all(
-        inputs,
-        cotangent,
-        w_q,
-        w_up,
-        w_out,
-        w_down,
-        packed,
-        seg_row,
-        gain[None],
-        shift[None],
-        jnp.concatenate([qkv_bias.reshape(-1), up_bias])[None],
-        n_dp,
-        n_row,
-        n_col,
+    pos_row = positions.reshape(seq_count, SEQ_LEN).astype(F32)
+    cot_rows, w_in, w_fin, norm_t, hidden, hidden_t, qkv_low, up_pre, packed, mean_own, rstd_own = (
+        forward_all(
+            inputs, cotangent, w_q, w_up, w_out, w_down, pos_row, seg_row, freq[None], vectors,
+            n_dp, n_row, n_col,
+        )
     )
     if n_dp == 2:
         branch, grad_norm, owned_low, part = backward_all(
@@ -1516,7 +1566,7 @@
         )
     else:
         partials, part = backward_plain(
-            hidden, hidden_t, cot_rows, w_fin, w_in, norm_t, qkv_low, up_pre, cosine, sine_tab, segments, HF
+            hidden, hidden_t, cot_rows, w_fin, w_in, norm_t, qkv_low, up_pre, positions, segments, HF
         )
         branch, grad_norm, owned_low = reduce_plain(*partials, C, HF, UT, n_col, row_width)
     x_val = inputs.astype(F32)
@@ -1526,8 +1576,8 @@
         grad_norm,
         inputs,
         cotangent,
-        lax.dynamic_slice_in_dim(mean_all, row_index * T, T),
-        lax.dynamic_slice_in_dim(rstd_all, row_index * T, T),
+        mean_own,
+        rstd_own,
         norm_gain[None],
         part,
         D,

time: 411 us -> 378 us (0.920)
  Pallas kernels: 380 us -> 361 us
  local copies, waits for them, and re-layouts: 22.5 us -> 13.4 us
  other arithmetic: 7.21 us -> 2.18 us
    pallas_call x1, Pallas kernels: 175 us -> 157 us  [forward_all(): pl.pallas_call(functools.partial(forward_kernel, n_dp, n_row, n_col, (T,...]
    concatenate x1 -> x0, local copies, waits for them, and re-layouts: 4.3 us -> none  [body(): jnp.concatenate([cosine, cosine, flat, sine_tab, sine_tab, 0.0 * flat], a...]
where the time goes in v6:
time: 378 us; the launch traced here: 377 us
  Pallas kernels  361 us (96%)
  local copies, waits for them, and re-layouts  13.4 us (4%)
    pallas_call x1, Pallas kernels, backward_all(): pl.pallas_call(functools.partial(backward_kernel, n_row, n_col, (T, C, HF...  166 us
    pallas_call x1, Pallas kernels, forward_all(): pl.pallas_call(functools.partial(forward_kernel, n_dp, n_row, n_col, (T,...  157 us
    pallas_call x1, Pallas kernels, muon_all(): pl.pallas_call(functools.partial(muon_kernel, owned, per_step, HF, UT, ra...  22 us
    pallas_call x1, Pallas kernels, finish_all(): pl.pallas_call(functools.partial(finish_kernel, n_dp, n_row, n_col, width...  16.2 us
    unnamed x28, local copies, waits for them, and re-layouts  8.6 us

profile of v6, /device:TPU:0, one launch (start us, length us, event | category | flops | bytes accessed | tf_op | source)
XLA Modules:
  0.0 377.3 jit_solution(4970603702537891836)
XLA Ops:
  0.6 1.7 copy.25
  2.4 0.0 copy-start.11
  2.4 0.0 copy-start.12
  2.4 0.1 copy.26
  2.5 1.6 copy.27.wq_ref
  4.1 0.0 copy-done.11
  4.1 0.6 reshape.55.seg_ref
  4.7 0.0 copy-done.12
  4.7 0.6 convert_element_type.10.pos_ref
  5.3 0.1 pad_maximum_fusion
  5.4 0.6 broadcast_in_dim_tile.3.freq_ref
  6.0 156.6 %forward_all.1 = (bf16[2048,2048]{1,0:T(8,128)(2,1)}, bf16[2048,896]{1,0:T(8,128)(2,1)}, bf16[640,2048]{1,0:T(8,128)(2,1)}, bf16[2048,2048]{1,0:T(8,128)(2,1)}, ...) custom-call(bf16[512,512]{1,0:T(8,128)(2,1)} %x_ref.3, ...), custom_call_target="tpu_custom_call" | custom-call | tf_op jit(solution)/shard_map/forward_all/pallas_call | solution.py:545
  162.6 166.0 %backward_all.1 = (f32[512,512]{1,0:T(8,128)}, f32[512,512]{1,0:T(8,128)}, bf16[12,512,256]{2,1,0:T(8,128)(2,1)}, f32[8,128]{1,0:T(8,128)}) custom-call(bf16[2048,640]{1,0:T(8,128)(2,1)} %get-tuple-element.29.hid_ref, bf16[640,2048]{1,0:T(8,128)(2,1)} %get-tuple-element.30.ht_ref, bf16[2048,2048]{1,0:T(8,128)(2,1)} %get-tuple-element.31.c_ref, ...), custom_call_target="tpu_custom_call" | custom-call | tf_op jit(solution)/shard_map/backward_all/pallas_call | solution.py:1161
  328.6 1.0 fusion
  329.6 0.0 copy-start
  329.7 1.0 copy-done
  330.7 0.0 copy-start.2
  330.7 1.0 copy-done.2
  331.7 0.0 copy-start.3
  331.7 1.2 copy-done.3
  333.0 0.0 copy-start.4
  333.0 0.9 copy-done.4
  333.9 0.0 copy-start.5
  333.9 0.9 copy-done.5
  334.9 0.0 copy-start.6
  334.9 0.7 copy-done.6
  335.5 0.0 copy-start.9
  335.5 0.0 copy-start.10
  335.5 16.2 %finish_all.1 = (f32[512,512]{1,0:T(8,128)S(1)}, f32[4,4,8,128]{3,2,1,0:T(8,128)S(1)}, f32[4,8,512]{2,1,0:T(8,128)S(1)}) custom-call(f32[512,512]{1,0:T(8,128)S(1)} %copy-done.3, bf16[512,512]{1,0:T(8,128)(2,1)S(1)} %copy-done, bf16[512,512]{1,0:T(8,128)(2,1)S(1)} %copy-done.2, f32[512,1]{1,0:T(8,128)S(1)} %copy-done.4, f32[512,1]{1,0:T(8,128)S(1)} %copy-done.5, ...), custom_call_target="tpu_custom_call" | custom-call | tf_op jit(solution)/shard_map/finish_all/pallas_call | solution.py:1341
  352.0 0.2 concatenate.7
  352.2 0.0 copy-start.7
  352.2 0.1 multiply_reduce_fusion
  352.3 0.0 copy-done.9
  352.3 0.0 copy-done.10
  352.3 0.8 multiply_subtract_fusion
  353.1 0.0 copy-start.1
  353.1 0.0 copy-start.8
  353.1 22.0 %muon_all.1 = (f32[12,512,256]{2,1,0:T(8,128)}, f32[12,512,256]{2,1,0:T(8,128)}, f32[12,512,256]{2,1,0:T(8,128)}) custom-call(bf16[12,512,256]{2,1,0:T(8,128)(2,1)} %get-tuple-element.44.grad_ref, f32[12,512,256]{2,1,0:T(8,128)} %bitcast.22, bf16[4,512,384]{2,1,0:T(8,128)(2,1)} %copy.27.wq_ref, bf16[512,512]{1,0:T(8,128)(2,1)} %wo_ref.3, ...), custom_call_target="tpu_custom_call" | custom-call | tf_op jit(solution)/shard_map/muon_all/pallas_call | solution.py:1455
  375.1 0.0 copy-done.7
  375.1 0.0 copy-done.1
  375.1 0.0 copy-done.8
  375.1 1.1 add_add_fusion
  376.3 1.0 copy.32
  (14 shorter events, 0.2 us)
Async XLA Ops:
  2.4 1.7 copy-start.11
  2.4 2.3 copy-start.12
  329.6 1.0 copy-start
  330.7 1.0 copy-start.2
  331.7 1.2 copy-start.3
  333.0 0.9 copy-start.4
  333.9 0.9 copy-start.5
  334.9 0.7 copy-start.6
  335.5 16.8 %copy-start.9 = (f32[11,2048]{1,0:T(8,128)S(1)}, f32[11,2048]{1,0:T(8,128)}, u32[]{:S(2)}) copy-start(f32[11,2048]{1,0:T(8,128)} %vec_ref.1) | copy-start | bytes 270340
  335.5 16.8 %copy-start.10 = (f32[11,2048]{1,0:T(8,128)S(1)}, f32[11,2048]{1,0:T(8,128)}, u32[]{:S(2)}) copy-start(f32[11,2048]{1,0:T(8,128)} %param.21) | copy-start | bytes 270340
  352.2 22.9 %copy-start.7 = (f32[11,2048]{1,0:T(8,128)}, f32[11,2048]{1,0:T(8,128)S(1)}, u32[]{:S(2)}) copy-start(f32[11,2048]{1,0:T(8,128)S(1)} %concatenate.7) | copy-start | bytes 270340
  353.1 22.0 %copy-start.1 = (bf16[512,512]{1,0:T(8,128)(2,1)S(1)}, bf16[512,512]{1,0:T(8,128)(2,1)}, u32[]{:S(2)}) copy-start(bf16[512,512]{1,0:T(8,128)(2,1)} %x_ref.3) | copy-start | bytes 1572868
  353.1 22.0 %copy-start.8 = (f32[512,512]{1,0:T(8,128)S(1)}, f32[512,512]{1,0:T(8,128)}, u32[]{:S(2)}) copy-start(f32[512,512]{1,0:T(8,128)} %get-tuple-element.38) | copy-start | bytes 3145732

commit v7 on v6

--- a/solution.py
+++ b/solution.py
@@ -681,6 +681,8 @@
 
     def first_sum(v, f):
         a_copy(v, 1, f).wait_recv()
+        if v == 1:
+            y_copy(f).wait_send()
 
         def add(rows):
             sbuf[f, rows, :] = (
@@ -688,7 +690,12 @@
             ).astype(BF16)
 
         looped(T, add)
+        if v == 1:
+            pl.semaphore_wait(free_row.at[f], 1)
         y_copy(f).start()
+
+    def release(f, peer):
+        pl.semaphore_signal(free_col.at[f], inc=1, device_id={"col": peer}, device_id_type=MESH)
 
     def second_sum(v, i):
         f = forder[i]
@@ -707,6 +714,8 @@
             step = jnp.where(right, jnp.int32(1), jnp.int32(-1))
             landed = jnp.where(f == c + step, jnp.where(right, f, jnp.int32(n_col)), f)
             inner = jnp.where(right, c, n_col - 1 - c) > 0
+            if v == 1:
+                z_copy(f, f, 0).wait_send()
 
             @pl.when(inner)
             def _():
@@ -716,6 +725,8 @@
                     zsb[f, rows, :] = (base(rows) + zin[f, rows, :].astype(F32)).astype(BF16)
 
                 looped(T, add)
+                if v == 0:
+                    release(f, c - step)
 
             @pl.when(jnp.logical_not(inner))
             def _():
@@ -724,6 +735,8 @@
 
                 looped(T, add)
 
+            if v == 1:
+                pl.semaphore_wait(free_col.at[f], 1)
             z_copy(f, landed, step).start()
         else:
             out = outs[v]
@@ -752,6 +765,18 @@
                 looped(T, lambda rows: put(
                     rows,
                     base(rows) + zin[f, rows, :].astype(F32) + zin[n_col, rows, :].astype(F32)))
+
+            if v == 0:
+                @pl.when(c > 0)
+                def _():
+                    release(f, c - 1)
+
+                @pl.when(c < n_col - 1)
+                def _():
+                    release(f, c + 1)
+
+        if v == 0:
+            pl.semaphore_signal(free_row.at[f], inc=1, device_id={"row": r2}, device_id_type=MESH)
 
     tall = (HF, 2 * UT)
     row0 = (0, HF)
@@ -780,9 +805,18 @@
                 for j in range(2)
             ]
         return [
-            (dwf.at[pl.ds(HF + m * UT, UT), pl.ds(at + j * lw, lw)],
-             tiles_ref.at[4 + 2 * (2 * m + half) + j, pl.ds(odd * UT, UT), :])
-            for m in range(2) for j in range(2)
+            (dwf.at[pl.ds(HF, UT), pl.ds(at + j * lw, lw)],
+             tiles_ref.at[4 + 2 * half + j, pl.ds(odd * UT, UT), :])
+            for j in range(2)
+        ]
+
+    def parts_e(own, cc, source):
+        half, odd = lax.div(source, 2), lax.rem(source, 2)
+        at = cc * C
+        return [
+            (dwf.at[pl.ds(HF + UT, UT), pl.ds(at + j * lw, lw)],
+             tiles_ref.at[8 + 2 * half + j, pl.ds(odd * UT, UT), :])
+            for j in range(2)
         ]
 
     def parts_u(own, cc, source):
@@ -797,7 +831,7 @@
             for j in range(3)
         ]
 
-    kinds = {"f": (parts_f, 0), "u": (parts_u, 4), "k": (parts_k, 5)}
+    kinds = {"f": (parts_f, 0), "e": (parts_e, 2), "u": (parts_u, 4), "k": (parts_k, 5)}
 
     def t_send(kind, own, cc):
         parts, first = kinds[kind]
@@ -821,7 +855,7 @@
         ]
 
     def owned_kinds(own):
-        return ("f", "u", "k") if own == 0 else ("f", "u")
+        return ("f", "u", "k") if own == 0 else ("f", "e", "u")
 
     def spread(kind, own):
         for k in range(1, n_col):
@@ -830,20 +864,30 @@
         for item in t_local(kind, own):
             item.start()
 
+    def add_rows(own, first, count):
+        for b in range(first, first + count):
+            xf_copy(own, b).wait_recv()
+
+        def add(rows):
+            here = pl.ds(pl.multiple_of(rows.start + first * HF, step_rows), step_rows)
+            at = (pl.ds(pl.multiple_of(rows.start + row0[own] + first * HF, step_rows), step_rows),
+                  slice(None))
+            dwf[at] = (dwf[at].astype(F32) + gf[here, :].astype(F32)).astype(BF16)
+
+        looped(count * HF, add)
+
     def add_f():
         for own in range(2):
             @pl.when(d == own)
             def _(own=own):
-                for b in range(tall[own] // HF):
-                    xf_copy(own, b).wait_recv()
-
-                def add(rows):
-                    at = (pl.ds(pl.multiple_of(rows.start + row0[own], step_rows), step_rows),
-                          slice(None))
-                    dwf[at] = (dwf[at].astype(F32) + gf[rows, :].astype(F32)).astype(BF16)
-
-                looped(tall[own], add)
+                add_rows(own, 0, 1 if own == 0 else UT // HF)
                 spread("f", own)
+
+    def add_e():
+        @pl.when(d == 1)
+        def _():
+            add_rows(1, UT // HF, UT // HF)
+            spread("e", 1)
 
     def add_piece(kind, own, cc):
         lane, width, buf, waiter = (
@@ -858,22 +902,15 @@
 
         looped(C, add)
 
-    def add_u(i):
+    def add_w(i):
         for own in range(2):
             @pl.when(d == own)
             def _(own=own):
                 cc = forder[i]
-                add_piece("u", own, cc)
-                for item in t_local("u", own) if i == n_col - 1 else t_send("u", own, cc):
-                    item.start()
-
-    def add_k(i):
-        @pl.when(d == 0)
-        def _():
-            cc = forder[i]
-            add_piece("k", 0, cc)
-            for item in t_local("k", 0) if i == n_col - 1 else t_send("k", 0, cc):
-                item.start()
+                for kind in ("k", "u") if own == 0 else ("u",):
+                    add_piece(kind, own, cc)
+                    for item in t_local(kind, own) if i == n_col - 1 else t_send(kind, own, cc):
+                        item.start()
 
     loads[0].wait()
     loads[1].wait()
@@ -923,9 +960,9 @@
 
         return carry
 
-    lax.fori_loop(0, blocks, f_step, 0)
+    early = 1 + UT // HF
     first_sum(0, forder[n_col - 1])
-    second_sum(0, 0)
+    lax.fori_loop(0, early, f_step, 0)
 
     part_ref[...] = jnp.zeros_like(part_ref)
     tiles = rows_all // tile
@@ -952,22 +989,7 @@
 
     lax.fori_loop(0, tiles, b_step, 0)
     load_nt.start()
-    second_sum(0, 1)
-    load_nt.wait()
-
-    def u_step(i, carry):
-        cc = pick(i, forder)
-        at = pl.ds(pl.multiple_of(cc * C, C), C)
-        dwi[at, qw:] = jnp.dot(big[at, :], hd[:, qw:], preferred_element_type=F32).astype(BF16)
-        for own in range(2):
-            @pl.when(d == own)
-            def _(own=own):
-                xu_copy(1 - own, cc).start()
-
-        return carry
-
-    lax.fori_loop(0, n_col, u_step, 0)
-    second_sum(0, 2)
+    second_sum(0, 0)
 
     loads[3].wait()
     loads[4].wait()
@@ -1039,90 +1061,66 @@
             hd[at, :], wi[feats, :], last_dim, preferred_element_type=F32
         ).astype(BF16)
 
-    def credit(first):
-        if first:
-            pl.semaphore_signal(free_row, inc=1, device_id={"row": r2}, device_id_type=MESH)
-        for n, step in enumerate((1, -1)):
-            @pl.when((c + step >= 0) & (c + step < n_col))
-            def _(n=n, step=step):
-                if first:
-                    pl.semaphore_signal(free_col.at[n], inc=1, device_id={"col": c + step},
-                                        device_id_type=MESH)
-                else:
-                    pl.semaphore_wait(free_col.at[1 - n], 1)
-        if not first:
-            pl.semaphore_wait(free_row, 1)
-
-    def s_step(m, carry):
-        rr = pick(m, [r12, r2, r1, r])
-
-        def seq(s, inner):
-            attend_seq(rr * per_row + s)
-            return inner
-
-        lax.fori_loop(0, per_row, seq, 0)
-
-        @pl.when(m == 1)
+    def seq_step(s, carry):
+        attend_seq(s)
+        return carry
+
+    lax.fori_loop(0, rows_all // SEQ_LEN, seq_step, 0)
+    second_sum(0, 1)
+    load_nt.wait()
+
+    half_rows = C // 2
+
+    def w_step(i, carry):
+        cc = pick(lax.div(i, 2), forder)
+        at = pl.ds(pl.multiple_of(cc * C + lax.rem(i, 2) * half_rows, half_rows), half_rows)
+        dwi[at, :] = jnp.dot(big[at, :], hd[...], preferred_element_type=F32).astype(BF16)
+
+        @pl.when(lax.rem(i, 2) == 1)
         def _():
-            second_sum(0, n_col - 1)
-            for f in range(n_col):
-                y_copy(f).wait_send()
-            for i in range(n_col - 1):
-                z_copy(forder[i], forder[i], 0).wait_send()
-            credit(True)
-            credit(False)
-
-        def units(i, inner):
+            for own in range(2):
+                @pl.when(d == own)
+                def _(own=own):
+                    if own == 1:
+                        xk_copy(cc).start()
+                    xu_copy(1 - own, cc).start()
+
+        return carry
+
+    lax.fori_loop(0, n_col, w_step, 0)
+    second_sum(0, 2)
+    lax.fori_loop(n_col, 2 * n_col, w_step, 0)
+    load_c = pltpu.make_async_copy(c_ref, big, l_s.at[2])
+    load_c.start()
+
+    def q_step(h, rows_peer, rows_own):
+        def units(i, carry):
             f = pick(i, forder)
-            value = q_unit(rr, f)
-
-            def to_peer(h):
-                a_copy(0, h, f).wait_send()
-                asb[h, f] = value
-                a_copy(1, h, f).start()
-
-            @pl.when(m == 0)
-            def _():
-                to_peer(1)
-
-            @pl.when(m == 2)
-            def _():
-                to_peer(0)
-
-            @pl.when(m == 1)
-            def _():
-                obuf[1, f] = value
-                first_sum(1, f)
-
-            @pl.when(m == 3)
-            def _():
-                obuf[0, f] = value
-
-            return inner
+            a_copy(0, h, f).wait_send()
+            asb[h, f] = q_unit(rows_peer, f)
+            a_copy(1, h, f).start()
+            obuf[h, f] = q_unit(rows_own, f)
+            return carry
 
         lax.fori_loop(0, n_col, units, 0)
-        return carry
-
-    lax.fori_loop(0, n_row, s_step, 0)
+
+    q_step(1, r12, r2)
+    for i in range(n_col - 1):
+        first_sum(1, forder[i])
     add_f()
-
-    def k_step(i, carry):
-        cc = pick(i, forder)
-        at = pl.ds(pl.multiple_of(cc * C, C), C)
-        dwi[at, 0:qw] = jnp.dot(big[at, :], hd[:, 0:qw], preferred_element_type=F32).astype(BF16)
-
-        @pl.when(d == 1)
-        def _():
-            xk_copy(cc).start()
-
-        return carry
-
-    lax.fori_loop(0, n_col, k_step, 0)
-    for i in range(n_col):
-        second_sum(1, i) if i < n_col - 1 else None
-        add_u(i)
-    for i in range(n_col):
-        add_k(i)
+    load_c.wait()
+    lax.fori_loop(early, blocks, f_step, 0)
+    second_sum(0, n_col - 1)
+    first_sum(1, forder[n_col - 1])
+    add_w(0)
+    q_step(0, r1, r)
+    add_w(1)
+    second_sum(1, 0)
+    add_w(2)
+    second_sum(1, 1)
+    add_e()
+    second_sum(1, 2)
+    add_w(3)
     second_sum(1, n_col - 1)
 
     for own in range(2):
@@ -1207,8 +1205,8 @@
             dma((n_col,)),
             dma((8, n_col)),
             dma((8, n_col)),
-            pltpu.SemaphoreType.REGULAR,
-            pltpu.SemaphoreType.REGULAR((2,)),
+            pltpu.SemaphoreType.REGULAR((n_col,)),
+            pltpu.SemaphoreType.REGULAR((n_col,)),
         ],
         compiler_params=pltpu.CompilerParams(
             collective_id=1, has_side_effects=True, vmem_limit_bytes=67043328
@@ -1216,10 +1214,15 @@
     )(hid, ht, cot, w_fin, w_in, nt, qkv, up, packed, seg_row)
 
 
-def finish_kernel(n_dp, n_row, n_col, width, gn_ref, x_ref, g_ref, mean_ref, rstd_ref, gain_ref, part_ref,
-                  gx_ref, va_ref, vb_ref,
-                  st, da, db, ra, rb,
-                  st_s, st_r, d_s, d_r, r_s, r_r, c_s, c_r):
+def finish_kernel(n_dp, n_row, n_col, width, *refs):
+    hbm, (gx_ref, va_ref, vb_ref), local = refs[:7], refs[7:10], refs[10:17]
+    gn_ref, x_ref, g_ref, mean_ref, rstd_ref, gain_ref, part_ref = local
+    l_s, st, da, db, ra, rb, st_s, st_r, d_s, d_r, r_s, r_r, c_s, c_r = refs[17:]
+    loads = [
+        pltpu.make_async_copy(src, dst, l_s.at[n]) for n, (src, dst) in enumerate(zip(hbm, local))
+    ]
+    for item in loads:
+        item.start()
     d, r, c = lax.axis_index("dp"), lax.axis_index("row"), lax.axis_index("col")
     T, C = gn_ref.shape
 
@@ -1230,13 +1233,14 @@
     peers = [{"dp": k} for k in dps] + [{"row": k} for k in rows] + [{"col": k} for k in cols]
     for peer in peers:
         pl.semaphore_signal(barrier, inc=1, device_id=peer, device_id_type=MESH)
-    pl.semaphore_wait(barrier, len(peers))
 
     def copy(src, dst, s, rcv, peer):
         return pltpu.make_async_remote_copy(
             src_ref=src, dst_ref=dst, send_sem=s, recv_sem=rcv, device_id=peer, device_id_type=MESH
         )
 
+    for item in loads:
+        item.wait()
     gain = gain_ref[...]
 
     def fold(value):
@@ -1257,6 +1261,7 @@
     def st_wait(k):
         return copy(st.at[k], st.at[k], st_s.at[k], st_r.at[k], {"col": k})
 
+    pl.semaphore_wait(barrier, len(peers))
     for k in cols:
         st_copy(k).start()
 
@@ -1335,6 +1340,7 @@
 
 
 def finish_all(gn, x, g, mean, rstd, gain, part, width, n_dp, n_row, n_col):
+    args = (gn, x, g, mean, rstd, gain, part)
     T, C = gn.shape
     dma = pltpu.SemaphoreType.DMA
     vm = pl.BlockSpec(memory_space=pltpu.VMEM)
@@ -1346,9 +1352,11 @@
             jax.ShapeDtypeStruct((n_col, n_row, 8, 128), F32),
             jax.ShapeDtypeStruct((n_col, 8, C), F32),
         ),
-        in_specs=[vm] * 7,
+        in_specs=[ANY] * 7,
         out_specs=(vm,) * 3,
-        scratch_shapes=[
+        scratch_shapes=[pltpu.VMEM(item.shape, item.dtype) for item in args]
+        + [
+            dma((7,)),
             pltpu.VMEM((n_col, 8, T), F32),
             pltpu.VMEM((n_dp, 8, 128), F32),
             pltpu.VMEM((n_dp, 8, C), F32),
@@ -1366,7 +1374,7 @@
         compiler_params=pltpu.CompilerParams(
             collective_id=2, has_side_effects=True, vmem_limit_bytes=48 * 1024 * 1024
         ),
-    )(gn, x, g, mean, rstd, gain, part)
+    )(*args)
 
 
 def muon_kernel(owned, per_step, HF, UT, rate, grad_ref, mom_ref, wq_ref, wo_ref, wu_ref, wd_ref,
@@ -1448,7 +1456,7 @@
 
 def muon_all(grads, moment, w_q, w_out, w_up, w_down, HF, UT):
     owned, rows, cols = moment.shape
-    per_step = 3
+    per_step = 4 if owned % 4 == 0 else 3
     rate = MUON_RATE * math.sqrt(max(1.0, rows / cols))
     block = pl.BlockSpec((per_step, rows, cols), lambda i: (i, 0, 0))
     out = jax.ShapeDtypeStruct(moment.shape, F32)

time: 378 us -> 372 us (0.984)
  Pallas kernels: 361 us -> 355 us
    pallas_call x1, Pallas kernels: 16.2 us -> 11.2 us  [finish_all(): pl.pallas_call(functools.partial(finish_kernel, n_dp, n_row, n_col, width...]
where the time goes in v7:
time: 372 us; the launch traced here: 371 us
  Pallas kernels  355 us (95%)
  local copies, waits for them, and re-layouts  13.4 us (4%)
    pallas_call x1, Pallas kernels, backward_all(): pl.pallas_call(functools.partial(backward_kernel, n_row, n_col, (T, C, HF...  168 us
    pallas_call x1, Pallas kernels, forward_all(): pl.pallas_call(functools.partial(forward_kernel, n_dp, n_row, n_col, (T,...  157 us
    pallas_call x1, Pallas kernels, muon_all(): pl.pallas_call(functools.partial(muon_kernel, owned, per_step, HF, UT, ra...  19 us
    pallas_call x1, Pallas kernels, finish_all(): pl.pallas_call(functools.partial(finish_kernel, n_dp, n_row, n_col, width...  11.2 us
    unnamed x28, local copies, waits for them, and re-layouts  8.6 us

profile of v7, /device:TPU:0, one launch (start us, length us, event | category | flops | bytes accessed | tf_op | source)
XLA Modules:
  0.0 371.1 jit_solution(12566524662769531748)
XLA Ops:
  0.6 1.7 copy.25
  2.4 0.0 copy-start.11
  2.4 0.0 copy-start.12
  2.4 0.1 copy.26
  2.5 1.6 copy.27.wq_ref
  4.1 0.0 copy-done.11
  4.1 0.6 reshape.55.seg_ref
  4.7 0.0 copy-done.12
  4.7 0.6 convert_element_type.10.pos_ref
  5.3 0.1 pad_maximum_fusion
  5.4 0.6 broadcast_in_dim_tile.3.freq_ref
  6.0 156.6 %forward_all.1 = (bf16[2048,2048]{1,0:T(8,128)(2,1)}, bf16[2048,896]{1,0:T(8,128)(2,1)}, bf16[640,2048]{1,0:T(8,128)(2,1)}, bf16[2048,2048]{1,0:T(8,128)(2,1)}, ...) custom-call(bf16[512,512]{1,0:T(8,128)(2,1)} %refs_1_.1, ...), custom_call_target="tpu_custom_call" | custom-call | tf_op jit(solution)/shard_map/forward_all/pallas_call | solution.py:545
  162.6 167.8 %backward_all.1 = (f32[512,512]{1,0:T(8,128)}, f32[512,512]{1,0:T(8,128)}, bf16[12,512,256]{2,1,0:T(8,128)(2,1)}, f32[8,128]{1,0:T(8,128)}) custom-call(bf16[2048,640]{1,0:T(8,128)(2,1)} %get-tuple-element.29.hid_ref, bf16[640,2048]{1,0:T(8,128)(2,1)} %get-tuple-element.30.ht_ref, bf16[2048,2048]{1,0:T(8,128)(2,1)} %get-tuple-element.31.c_ref, ...), custom_call_target="tpu_custom_call" | custom-call | tf_op jit(solution)/shard_map/backward_all/pallas_call | solution.py:1159
  330.4 1.0 fusion
  331.4 0.0 copy-start
  331.5 1.0 copy-done
  332.5 0.0 copy-start.2
  332.5 1.0 copy-done.2
  333.5 0.0 copy-start.3
  333.5 1.2 copy-done.3
  334.8 0.0 copy-start.4
  334.8 0.9 copy-done.4
  335.7 0.0 copy-start.5
  335.7 0.9 copy-done.5
  336.7 0.0 copy-start.6
  336.7 0.7 copy-done.6
  337.3 0.0 copy-start.9
  337.3 0.0 copy-start.10
  337.3 11.2 %finish_all.1 = (f32[512,512]{1,0:T(8,128)S(1)}, f32[4,4,8,128]{3,2,1,0:T(8,128)S(1)}, f32[4,8,512]{2,1,0:T(8,128)S(1)}) custom-call(f32[512,512]{1,0:T(8,128)S(1)} %copy-done.3, bf16[512,512]{1,0:T(8,128)(2,1)S(1)} %copy-done, bf16[512,512]{1,0:T(8,128)(2,1)S(1)} %copy-done.2, f32[512,1]{1,0:T(8,128)S(1)} %copy-done.4, f32[512,1]{1,0:T(8,128)S(1)} %copy-done.5, ...), custom_call_target="tpu_custom_call" | custom-call | tf_op jit(solution)/shard_map/finish_all/pallas_call | solution.py:1347
  348.7 0.2 concatenate.7
  348.9 0.0 copy-start.7
  349.0 0.1 multiply_reduce_fusion
  349.1 0.0 copy-done.9
  349.1 0.0 copy-done.10
  349.1 0.8 multiply_subtract_fusion
  349.9 0.0 copy-start.1
  349.9 0.0 copy-start.8
  349.9 19.0 %muon_all.1 = (f32[12,512,256]{2,1,0:T(8,128)}, f32[12,512,256]{2,1,0:T(8,128)}, f32[12,512,256]{2,1,0:T(8,128)}) custom-call(bf16[12,512,256]{2,1,0:T(8,128)(2,1)} %get-tuple-element.44.grad_ref, f32[12,512,256]{2,1,0:T(8,128)} %bitcast.22, bf16[4,512,384]{2,1,0:T(8,128)(2,1)} %copy.27.wq_ref, bf16[512,512]{1,0:T(8,128)(2,1)} %wo_ref.3, ...), custom_call_target="tpu_custom_call" | custom-call | tf_op jit(solution)/shard_map/muon_all/pallas_call | solution.py:1463
  368.9 0.0 copy-done.7
  369.0 0.0 copy-done.1
  369.0 0.0 copy-done.8
  369.0 1.1 add_add_fusion
  370.1 1.0 copy.32
  (14 shorter events, 0.2 us)
Async XLA Ops:
  2.4 1.7 copy-start.11
  2.4 2.3 copy-start.12
  331.4 1.0 copy-start
  332.5 1.0 copy-start.2
  333.5 1.2 copy-start.3
  334.8 0.9 copy-start.4
  335.7 0.9 copy-start.5
  336.7 0.7 copy-start.6
  337.3 11.8 %copy-start.9 = (f32[11,2048]{1,0:T(8,128)S(1)}, f32[11,2048]{1,0:T(8,128)}, u32[]{:S(2)}) copy-start(f32[11,2048]{1,0:T(8,128)} %vec_ref.1) | copy-start | bytes 270340
  337.3 11.8 %copy-start.10 = (f32[11,2048]{1,0:T(8,128)S(1)}, f32[11,2048]{1,0:T(8,128)}, u32[]{:S(2)}) copy-start(f32[11,2048]{1,0:T(8,128)} %param.21) | copy-start | bytes 270340
  348.9 20.0 %copy-start.7 = (f32[11,2048]{1,0:T(8,128)}, f32[11,2048]{1,0:T(8,128)S(1)}, u32[]{:S(2)}) copy-start(f32[11,2048]{1,0:T(8,128)S(1)} %concatenate.7) | copy-start | bytes 270340
  349.9 19.1 %copy-start.1 = (bf16[512,512]{1,0:T(8,128)(2,1)S(1)}, bf16[512,512]{1,0:T(8,128)(2,1)}, u32[]{:S(2)}) copy-start(bf16[512,512]{1,0:T(8,128)(2,1)} %refs_1_.1) | copy-start | bytes 1572868
  349.9 19.1 %copy-start.8 = (f32[512,512]{1,0:T(8,128)S(1)}, f32[512,512]{1,0:T(8,128)}, u32[]{:S(2)}) copy-start(f32[512,512]{1,0:T(8,128)} %get-tuple-element.38) | copy-start | bytes 3145732

commit v8 on v7

--- a/solution.py
+++ b/solution.py
@@ -137,7 +137,7 @@
 
 def forward_kernel(n_dp, n_row, n_col, dims,
                    x_ref, g_ref, wq_ref, wu_ref, wo_ref, wd_ref,
-                   pos_ref, seg_ref, freq_ref, vec_ref,
+                   pos_ref, seg_ref, vec_ref,
                    gf, wi, wf, nt, hid_out, ht_out, qkv_out, up_out, cs_out, mean_ref, rstd_ref,
                    xv, ntv, wv, hid, ht, qkv, up, tab, mean_v, rstd_v, stage_g, stage_o, stage_d,
                    zs, zr, ys, yr, cs, cr, ws, wr, ds, dr, ls, lo, no):
@@ -329,9 +329,15 @@
         store.start()
     w_pass(win[0])
 
+    place = lax.rem(lax.broadcasted_iota(jnp.int32, (1, 2 * HEAD_DIM), 1), HEAD_DIM)
+    power = jnp.exp(
+        lax.rem(place, ROTARY // 2).astype(F32) * (-2.0 * math.log(10000.0) / ROTARY)
+    )
+    freq = jnp.where(place < ROTARY, power, 0.0)
+
     def one_table(n, carry):
-        rows = jnp.broadcast_to(pos_ref[pl.ds(n, 1), :], (2 * HEAD_DIM, SEQ_LEN))
-        angle = jnp.transpose(rows) * freq_ref[...]
+        rows = jnp.broadcast_to(pos_ref[pl.ds(n, 1), :].astype(F32), (2 * HEAD_DIM, SEQ_LEN))
+        angle = jnp.transpose(rows) * freq
         lane = lax.broadcasted_iota(jnp.int32, angle.shape, 1)
         turns = jnp.floor(angle * (2.0 / math.pi) + 0.5)
         rest = angle - turns * 1.5703125
@@ -532,7 +538,7 @@
         item.wait()
 
 
-def forward_all(x, g, w_q, w_up, w_out, w_down, pos_row, seg_row, freq, vectors,
+def forward_all(x, g, w_q, w_up, w_out, w_down, pos_row, seg_row, vectors,
                 n_dp, n_row, n_col):
     T, C = x.shape
     HF = w_q.shape[2] // 3
@@ -558,7 +564,7 @@
             sds((T, 1), F32),
             sds((T, 1), F32),
         ),
-        in_specs=[ANY] * 6 + [vm] * 4,
+        in_specs=[ANY] * 6 + [vm] * 3,
         out_specs=(ANY,) * 9 + (vm,) * 2,
         scratch_shapes=[
             pltpu.VMEM((rows, D), BF16),
@@ -591,7 +597,7 @@
         compiler_params=pltpu.CompilerParams(
             collective_id=0, has_side_effects=True, vmem_limit_bytes=60 * 1024 * 1024
         ),
-    )(x, g, w_q, w_up, w_out, w_down, pos_row, seg_row, freq, vectors)
+    )(x, g, w_q, w_up, w_out, w_down, pos_row, seg_row, vectors)
 
 
 def wide_tables(packed):
@@ -1372,7 +1378,7 @@
             dma((n_col, 2)),
         ],
         compiler_params=pltpu.CompilerParams(
-            collective_id=2, has_side_effects=True, vmem_limit_bytes=48 * 1024 * 1024
+            collective_id=2, has_side_effects=True, vmem_limit_bytes=67043328
         ),
     )(*args)
 
@@ -1555,15 +1561,11 @@
     )
     rows_all = positions.shape[0]
     seq_count = rows_all // SEQ_LEN
-    half = jnp.exp(
-        jnp.arange(ROTARY // 2, dtype=F32) * (-2.0 * math.log(10000.0) / ROTARY)
-    )
-    freq = jnp.tile(jnp.concatenate([half, half, jnp.zeros((HEAD_DIM - ROTARY,), F32)]), 2)
     seg_row = segments.reshape(seq_count, SEQ_LEN)
-    pos_row = positions.reshape(seq_count, SEQ_LEN).astype(F32)
+    pos_row = positions.reshape(seq_count, SEQ_LEN)
     cot_rows, w_in, w_fin, norm_t, hidden, hidden_t, qkv_low, up_pre, packed, mean_own, rstd_own = (
         forward_all(
-            inputs, cotangent, w_q, w_up, w_out, w_down, pos_row, seg_row, freq[None], vectors,
+            inputs, cotangent, w_q, w_up, w_out, w_down, pos_row, seg_row, vectors,
             n_dp, n_row, n_col,
         )
     )

time: 372 us -> 370 us (level)
    unnamed x28 -> x16, local copies, waits for them, and re-layouts: 8.6 us -> 2.97 us
where the time goes in v8:
time: 370 us
  Pallas kernels  355 us (96%)
  local copies, waits for them, and re-layouts  10.5 us (3%)
    pallas_call x1, Pallas kernels, backward_all(): pl.pallas_call(functools.partial(backward_kernel, n_row, n_col, (T, C, HF...  167 us
    pallas_call x1, Pallas kernels, forward_all(): pl.pallas_call(functools.partial(forward_kernel, n_dp, n_row, n_col, (T,...  157 us
    pallas_call x1, Pallas kernels, muon_all(): pl.pallas_call(functools.partial(muon_kernel, owned, per_step, HF, UT, ra...  19 us
    pallas_call x1, Pallas kernels, finish_all(): pl.pallas_call(functools.partial(finish_kernel, n_dp, n_row, n_col, width...  12.1 us

profile of v8, /device:TPU:0, one launch (start us, length us, event | category | flops | bytes accessed | tf_op | source)
XLA Modules:
  0.0 370.0 jit_solution(1907898386632152031)
XLA Ops:
  0.6 1.7 copy.25
  2.4 0.0 copy-start.4
  2.4 0.0 copy-start.5
  2.4 0.1 copy.26
  2.5 1.6 copy.27.wq_ref
  4.1 0.0 copy-done.4
  4.1 0.6 reshape.56.seg_ref
  4.7 0.0 copy-done.5
  4.7 0.6 reshape.55.pos_ref
  5.3 156.6 %forward_all.1 = (bf16[2048,2048]{1,0:T(8,128)(2,1)}, bf16[2048,896]{1,0:T(8,128)(2,1)}, bf16[640,2048]{1,0:T(8,128)(2,1)}, bf16[2048,2048]{1,0:T(8,128)(2,1)}, ...) custom-call(bf16[512,512]{1,0:T(8,128)(2,1)} %refs_1_.1, ...), custom_call_target="tpu_custom_call" | custom-call | tf_op jit(solution)/shard_map/forward_all/pallas_call | solution.py:551
  161.9 167.2 %backward_all.1 = (f32[512,512]{1,0:T(8,128)}, f32[512,512]{1,0:T(8,128)}, bf16[12,512,256]{2,1,0:T(8,128)(2,1)}, f32[8,128]{1,0:T(8,128)}) custom-call(bf16[2048,640]{1,0:T(8,128)(2,1)} %get-tuple-element.29.hid_ref, bf16[640,2048]{1,0:T(8,128)(2,1)} %get-tuple-element.30.ht_ref, bf16[2048,2048]{1,0:T(8,128)(2,1)} %get-tuple-element.31.c_ref, ...), custom_call_target="tpu_custom_call" | custom-call | tf_op jit(solution)/shard_map/backward_all/pallas_call | solution.py:1165
  329.2 1.0 fusion
  330.1 0.6 dynamic-slice_add_fusion
  330.7 12.1 %finish_all.1 = (f32[512,512]{1,0:T(8,128)}, f32[4,4,8,128]{3,2,1,0:T(8,128)}, f32[4,8,512]{2,1,0:T(8,128)}) custom-call(f32[512,512]{1,0:T(8,128)} %get-tuple-element.39.refs_0_, bf16[512,512]{1,0:T(8,128)(2,1)} %refs_1_.1, bf16[512,512]{1,0:T(8,128)(2,1)} %refs_2_.1, f32[512,1]{1,0:T(8,128)} %get-tuple-element.40.refs_3_, ...), custom_call_target="tpu_custom_call" | custom-call | tf_op jit(solution)/shard_map/finish_all/pallas_call | solution.py:1353
  342.9 0.8 slice.40
  343.8 0.8 slice.37
  344.7 0.8 slice.39
  345.5 0.8 slice.38
  346.4 0.2 concatenate.3
  346.6 0.0 copy-start.1
  346.6 0.1 multiply_reduce_fusion
  346.7 1.8 multiply_subtract_fusion
  348.5 0.0 copy-start
  348.5 0.0 copy-start.2
  348.5 0.0 copy-start.6
  348.5 19.0 %muon_all.1 = (f32[12,512,256]{2,1,0:T(8,128)}, f32[12,512,256]{2,1,0:T(8,128)}, f32[12,512,256]{2,1,0:T(8,128)}) custom-call(bf16[12,512,256]{2,1,0:T(8,128)(2,1)} %get-tuple-element.44.grad_ref, f32[12,512,256]{2,1,0:T(8,128)} %bitcast.18, bf16[4,512,384]{2,1,0:T(8,128)(2,1)} %copy.27.wq_ref, bf16[512,512]{1,0:T(8,128)(2,1)} %wo_ref.3, ...), custom_call_target="tpu_custom_call" | custom-call | tf_op jit(solution)/shard_map/muon_all/pallas_call | solution.py:1469
  367.5 0.0 copy-done.1
  367.5 0.0 copy-start.3
  367.6 0.0 copy-done
  367.6 0.0 copy-done.2
  367.6 0.0 copy-done.6
  367.6 1.1 add_add_fusion
  368.7 0.3 copy-done.3
  369.0 1.0 copy.32
  (5 shorter events, 0.1 us)
Async XLA Ops:
  2.4 1.7 copy-start.4
  2.4 2.3 copy-start.5
  346.6 21.0 %copy-start.1 = (f32[11,2048]{1,0:T(8,128)}, f32[11,2048]{1,0:T(8,128)S(1)}, u32[]{:S(2)}) copy-start(f32[11,2048]{1,0:T(8,128)S(1)} %concatenate.3) | copy-start | bytes 270340
  348.5 19.1 %copy-start = (bf16[512,512]{1,0:T(8,128)(2,1)S(1)}, bf16[512,512]{1,0:T(8,128)(2,1)}, u32[]{:S(2)}) copy-start(bf16[512,512]{1,0:T(8,128)(2,1)} %refs_1_.1) | copy-start | bytes 1572868
  348.5 19.1 %copy-start.2 = (f32[512,512]{1,0:T(8,128)S(1)}, f32[512,512]{1,0:T(8,128)}, u32[]{:S(2)}) copy-start(f32[512,512]{1,0:T(8,128)} %get-tuple-element.38) | copy-start | bytes 3145732
  348.5 19.1 %copy-start.6 = (f32[1,512]{1,0:T(1,128)S(1)}, f32[1,512]{1,0:T(1,128)}, u32[]{:S(2)}) copy-start(f32[1,512]{1,0:T(1,128)} %get-tuple-element.55) | copy-start | bytes 6148
  367.5 1.4 copy-start.3

commit v9 on v8

--- a/solution.py
+++ b/solution.py
@@ -1221,9 +1221,9 @@
 
 
 def finish_kernel(n_dp, n_row, n_col, width, *refs):
-    hbm, (gx_ref, va_ref, vb_ref), local = refs[:7], refs[7:10], refs[10:17]
+    hbm, (gx_ref, vec_ref), local = refs[:7], refs[7:9], refs[9:16]
     gn_ref, x_ref, g_ref, mean_ref, rstd_ref, gain_ref, part_ref = local
-    l_s, st, da, db, ra, rb, st_s, st_r, d_s, d_r, r_s, r_r, c_s, c_r = refs[17:]
+    l_s, st, da, db, ra, rb, va_ref, vb_ref, st_s, st_r, d_s, d_r, r_s, r_r, c_s, c_r = refs[16:]
     loads = [
         pltpu.make_async_copy(src, dst, l_s.at[n]) for n, (src, dst) in enumerate(zip(hbm, local))
     ]
@@ -1333,6 +1333,21 @@
     for k in cols:
         for item in c_pair(k, k):
             item.wait_recv()
+    unit = 128
+    units = (vec_ref.shape[1] // unit) // (2 * n_col)
+    for cc in range(n_col):
+        lanes = slice(cc * C, (cc + 1) * C)
+        vec_ref[5:7, lanes] = vb_ref[cc, 0:2, :]
+        for row in (3, 4):
+            vec_ref[row : row + 1, lanes] = vb_ref[cc, 2:3, :]
+        for rr in range(n_row):
+            at = (rr * n_col + cc) * unit
+            vec_ref[0:3, at : at + unit] = va_ref[cc, rr, 0:3, :]
+            for half in range(2):
+                for k in range(units):
+                    to = ((half * n_col + cc) * units + k) * unit
+                    src = 3 + half * units + k
+                    vec_ref[7 + rr : 8 + rr, to : to + unit] = va_ref[cc, rr, src : src + 1, :]
     for k in cols:
         st_copy(k).wait_send()
         for item in c_pair(c, k):
@@ -1355,11 +1370,10 @@
         name="finish_all",
         out_shape=(
             jax.ShapeDtypeStruct((T, C), F32),
-            jax.ShapeDtypeStruct((n_col, n_row, 8, 128), F32),
-            jax.ShapeDtypeStruct((n_col, 8, C), F32),
+            jax.ShapeDtypeStruct((7 + n_row, n_col * C), F32),
         ),
         in_specs=[ANY] * 7,
-        out_specs=(vm,) * 3,
+        out_specs=(vm,) * 2,
         scratch_shapes=[pltpu.VMEM(item.shape, item.dtype) for item in args]
         + [
             dma((7,)),
@@ -1368,6 +1382,8 @@
             pltpu.VMEM((n_dp, 8, C), F32),
             pltpu.VMEM((n_row, 8, 128), F32),
             pltpu.VMEM((n_row, 8, C), F32),
+            pltpu.VMEM((n_col, n_row, 8, 128), F32),
+            pltpu.VMEM((n_col, 8, C), F32),
             dma((n_col,)),
             dma((n_col,)),
             dma((n_dp, 2)),
@@ -1582,7 +1598,7 @@
     x_val = inputs.astype(F32)
     result = x_val + branch + out_bias
 
-    grad_input, vec_a, vec_b = finish_all(
+    grad_input, vec_grad = finish_all(
         grad_norm,
         inputs,
         cotangent,
@@ -1594,13 +1610,6 @@
         n_dp,
         n_row,
         n_col,
-    )
-    vec_a = vec_a.transpose(2, 1, 0, 3)
-    qkv_rows = vec_a[:3].reshape(3, D)
-    up_rows = vec_a[3:7].reshape(2, UT // 128, n_row, n_col, 128).transpose(2, 0, 3, 1, 4)
-    norm_rows = vec_b.transpose(1, 0, 2).reshape(8, D)
-    vec_grad = jnp.concatenate(
-        [qkv_rows, norm_rows[2:3], norm_rows[2:3], norm_rows[:2], up_rows.reshape(-1, D)], axis=0
     )
     scaled = vec_grad * lax.rsqrt(jnp.mean(vec_grad * vec_grad, axis=1, keepdims=True) + STAT_EPS)
     vec_moment_new = MOMENTUM_RATE * vector_moment + scaled

time: 370 us -> 368 us (level)
  no operation moved by 1% of the time
where the time goes in v9:
time: 368 us
  Pallas kernels  355 us (96%)
  local copies, waits for them, and re-layouts  7.48 us (2%)
  other arithmetic  4.61 us (1%)
    pallas_call x1, Pallas kernels, backward_all(): pl.pallas_call(functools.partial(backward_kernel, n_row, n_col, (T, C, HF...  167 us
    pallas_call x1, Pallas kernels, forward_all(): pl.pallas_call(functools.partial(forward_kernel, n_dp, n_row, n_col, (T,...  157 us
    pallas_call x1, Pallas kernels, muon_all(): pl.pallas_call(functools.partial(muon_kernel, owned, per_step, HF, UT, ra...  19 us
    pallas_call x1, Pallas kernels, finish_all(): pl.pallas_call(functools.partial(finish_kernel, n_dp, n_row, n_col, width...  12.2 us

profile of v9, /device:TPU:0, one launch (start us, length us, event | category | flops | bytes accessed | tf_op | source)
XLA Modules:
  0.0 367.9 jit_solution(1248296528504368644)
XLA Ops:
  0.6 1.7 copy.22
  2.4 0.0 copy-start.4
  2.4 0.0 copy-start.5
  2.4 0.1 copy.23
  2.5 1.6 copy.24.wq_ref
  4.1 0.0 copy-done.4
  4.1 0.6 reshape.44.seg_ref
  4.7 0.0 copy-done.5
  4.7 0.6 reshape.43.pos_ref
  5.3 156.6 %forward_all.1 = (bf16[2048,2048]{1,0:T(8,128)(2,1)}, bf16[2048,896]{1,0:T(8,128)(2,1)}, bf16[640,2048]{1,0:T(8,128)(2,1)}, bf16[2048,2048]{1,0:T(8,128)(2,1)}, ...) custom-call(bf16[512,512]{1,0:T(8,128)(2,1)} %refs_1_.1, ...), custom_call_target="tpu_custom_call" | custom-call | tf_op jit(solution)/shard_map/forward_all/pallas_call | solution.py:551
  161.9 167.2 %backward_all.1 = (f32[512,512]{1,0:T(8,128)}, f32[512,512]{1,0:T(8,128)}, bf16[12,512,256]{2,1,0:T(8,128)(2,1)}, f32[8,128]{1,0:T(8,128)}) custom-call(bf16[2048,640]{1,0:T(8,128)(2,1)} %get-tuple-element.28.hid_ref, bf16[640,2048]{1,0:T(8,128)(2,1)} %get-tuple-element.29.ht_ref, bf16[2048,2048]{1,0:T(8,128)(2,1)} %get-tuple-element.30.c_ref, ...), custom_call_target="tpu_custom_call" | custom-call | tf_op jit(solution)/shard_map/backward_all/pallas_call | solution.py:1165
  329.2 1.0 fusion
  330.1 0.6 dynamic-slice_add_fusion
  330.7 12.2 %finish_all.1 = (f32[512,512]{1,0:T(8,128)}, f32[11,2048]{1,0:T(8,128)}) custom-call(f32[512,512]{1,0:T(8,128)} %get-tuple-element.38.refs_0_, bf16[512,512]{1,0:T(8,128)(2,1)} %refs_1_.1, bf16[512,512]{1,0:T(8,128)(2,1)} %refs_2_.1, f32[512,1]{1,0:T(8,128)} %get-tuple-element.39.refs_3_, f32[512,1]{1,0:T(8,128)} %get-tuple-element.40.refs_4_, ...), custom_call_target="tpu_custom_call" | custom-call | tf_op jit(solution)/shard_map/finish_all/pallas_call | solution.py:1368
  342.9 1.0 multiply_reduce_fusion
  344.0 1.8 multiply_subtract_fusion
  345.8 0.0 copy-start
  345.8 0.0 copy-start.2
  345.8 0.0 copy-start.6
  345.8 19.0 %muon_all.1 = (f32[12,512,256]{2,1,0:T(8,128)}, f32[12,512,256]{2,1,0:T(8,128)}, f32[12,512,256]{2,1,0:T(8,128)}) custom-call(bf16[12,512,256]{2,1,0:T(8,128)(2,1)} %get-tuple-element.43.grad_ref, f32[12,512,256]{2,1,0:T(8,128)} %bitcast.11, bf16[4,512,384]{2,1,0:T(8,128)(2,1)} %copy.24.wq_ref, bf16[512,512]{1,0:T(8,128)(2,1)} %wo_ref.3, ...), custom_call_target="tpu_custom_call" | custom-call | tf_op jit(solution)/shard_map/muon_all/pallas_call | solution.py:1485
  364.8 0.0 copy-start.3
  364.8 0.0 copy-start.1
  364.9 0.0 copy-done
  364.9 0.0 copy-done.2
  364.9 0.0 copy-done.6
  364.9 1.1 add_add_fusion
  366.0 0.2 copy-done.3
  366.2 1.0 copy.28
  367.2 0.0 copy-done.1
  367.2 0.7 copy.29
  (1 shorter events, 0.0 us)
Async XLA Ops:
  2.4 1.7 copy-start.4
  2.4 2.3 copy-start.5
  345.8 19.1 %copy-start = (bf16[512,512]{1,0:T(8,128)(2,1)S(1)}, bf16[512,512]{1,0:T(8,128)(2,1)}, u32[]{:S(2)}) copy-start(bf16[512,512]{1,0:T(8,128)(2,1)} %refs_1_.1) | copy-start | bytes 1572868
  345.8 19.1 %copy-start.2 = (f32[512,512]{1,0:T(8,128)S(1)}, f32[512,512]{1,0:T(8,128)}, u32[]{:S(2)}) copy-start(f32[512,512]{1,0:T(8,128)} %get-tuple-element.37) | copy-start | bytes 3145732
  345.8 19.1 %copy-start.6 = (f32[1,512]{1,0:T(1,128)S(1)}, f32[1,512]{1,0:T(1,128)}, u32[]{:S(2)}) copy-start(f32[1,512]{1,0:T(1,128)} %get-tuple-element.53) | copy-start | bytes 6148
  364.8 1.4 copy-start.3
  364.8 2.4 copy-start.1
